TPU v7x, 8 devices: a whole 2x2x1 slice. The times are simulated.
8 devices in a mesh: dp: 2 (over z, y), col: 2 (over x), row: 2 (over core).
Axes of the slice: x: 2, y: 2, z: 1, core: 2. Of those that a mesh axis runs over, the one named last changes fastest.
Arguments:
- x_attn: bfloat16 [16384, 1024], P('dp', 'row')
- dy_attn: bfloat16 [16384, 1024], P('dp', 'col')
- x_mlp: bfloat16 [16384, 1024], P('dp', 'row')
- dy_gate: bfloat16 [16384, 4096], P('dp', 'col')
- dy_up: bfloat16 [16384, 4096], P('dp', 'col')
- h_mlp: bfloat16 [16384, 4096], P('dp', 'row')
- dy_out: bfloat16 [16384, 1024], P('dp', 'col')
- w_attn: float32 [1024, 1024], P('row', 'col')
- w_gate: float32 [1024, 4096], P('row', 'col')
- w_up: float32 [1024, 4096], P('row', 'col')
- w_down: float32 [4096, 1024], P('row', 'col')
- r_attn: float32 [1024], P('row')
- c_attn: float32 [1024], P('col')
- r_gate: float32 [1024], P('row')
- c_gate: float32 [4096], P('col')
- r_up: float32 [1024], P('row')
- c_up: float32 [4096], P('col')
- r_down: float32 [4096], P('row')
- c_down: float32 [1024], P('col')
- hyper_params: float32 [3], replicated
Outputs:
- output 1: float32 [1024, 1024], P('row', 'col')
- output 2: float32 [1024], P('row')
- output 3: float32 [1024], P('col')
- output 4: float32 [1024, 4096], P('row', 'col')
- output 5: float32 [1024], P('row')
- output 6: float32 [4096], P('col')
- output 7: float32 [1024, 4096], P('row', 'col')
- output 8: float32 [1024], P('row')
- output 9: float32 [4096], P('col')
- output 10: float32 [4096, 1024], P('row', 'col')
- output 11: float32 [4096], P('row')
- output 12: float32 [1024], P('col')
All inputs are finite; a program needn't handle non-finite values.
Results may differ from a plain program's by a relative error of at most 0.001.
Values are sent between devices in bfloat16 or wider.
A program may use at most 1 GiB of HBM per device.

v0:
```python
import functools
import jax
import jax.numpy as jnp
from jax import lax
from jax.sharding import PartitionSpec as P

EPS_ONE = 1e-30
EPS_TWO = 1e-3


def matrix_step(x_block, dy_block, w_block, row_old, col_old, hyper_vals, row_size, col_size):
    beta_two = hyper_vals[0]
    rho_step = hyper_vals[1]
    clip_thr = hyper_vals[2]
    m_total = w_block.shape[0] * row_size
    n_total = w_block.shape[1] * col_size
    part_grad = jnp.einsum('tm,tn->mn', x_block, dy_block, preferred_element_type=jnp.float32)
    grad_block = lax.psum(part_grad, 'dp')
    sq_grad = grad_block * grad_block + EPS_ONE
    row_sum = lax.psum(jnp.sum(sq_grad, axis=1), 'col')
    col_sum = lax.psum(jnp.sum(sq_grad, axis=0), 'row')
    new_row = beta_two * row_old + (1.0 - beta_two) * (row_sum / n_total)
    new_col = beta_two * col_old + (1.0 - beta_two) * (col_sum / m_total)
    row_total = lax.psum(jnp.sum(new_row), 'row')
    second_est = new_row[:, None] * new_col[None, :] / row_total
    update = grad_block / jnp.sqrt(second_est)
    upd_rms = jnp.sqrt(lax.psum(jnp.sum(update * update), ('row', 'col')) / (m_total * n_total))
    update = update / jnp.maximum(1.0, upd_rms / clip_thr)
    w_rms = jnp.sqrt(lax.psum(jnp.sum(w_block * w_block), ('row', 'col')) / (m_total * n_total))
    step_size = rho_step * jnp.maximum(EPS_TWO, w_rms)
    return (w_block - step_size * update, new_row, new_col)


def solution(mesh):
    row_size = mesh.shape['row']
    col_size = mesh.shape['col']
    act_spec = P('dp', 'row')
    grad_spec = P('dp', 'col')
    w_spec = P('row', 'col')
    row_spec = P('row')
    col_spec = P('col')
    in_specs = (act_spec, grad_spec, act_spec, grad_spec, grad_spec, act_spec, grad_spec,
                w_spec, w_spec, w_spec, w_spec,
                row_spec, col_spec, row_spec, col_spec, row_spec, col_spec, row_spec, col_spec, P())
    out_specs = (w_spec, row_spec, col_spec) * 4

    def per_device(x_attn, dy_attn, x_mlp, dy_gate, dy_up, h_mlp, dy_out, w_attn, w_gate, w_up, w_down,
                   r_attn, c_attn, r_gate, c_gate, r_up, c_up, r_down, c_down, hyper_params):
        apply_one = functools.partial(matrix_step, hyper_vals=hyper_params, row_size=row_size, col_size=col_size)
        return (apply_one(x_attn, dy_attn, w_attn, r_attn, c_attn)
                + apply_one(x_mlp, dy_gate, w_gate, r_gate, c_gate)
                + apply_one(x_mlp, dy_up, w_up, r_up, c_up)
                + apply_one(h_mlp, dy_out, w_down, r_down, c_down))

    return jax.shard_map(per_device, mesh=mesh, in_specs=in_specs, out_specs=out_specs, check_vma=False)
```

profile of v0, /device:TPU:0, one launch (start us, length us, event | category | flops | bytes accessed | tf_op | source)
XLA Modules:
  0.0 476.7 jit_solution(2495399741865726528)
XLA Ops:
  7.2 25.0 %fusion.14 = f32[512,2048]{1,0:T(8,128)} fusion(bf16[8192,512]{1,0:T(8,128)(2,1)} %param.22, bf16[8192,2048]{1,0:T(8,128)(2,1)} %param.23), kind=kOutput, calls=%fused_computation.42 | convolution fusion | flops 17179869184 | bytes 46137344 | tf_op jit(solution)/shard_map/tm,tn->mn/dot_general | solution.py:17
  32.2 22.6 %fusion.15 = f32[512,2048]{1,0:T(8,128)} fusion(bf16[8192,512]{1,0:T(8,128)(2,1)S(1)} %copy-done.28, bf16[8192,2048]{1,0:T(8,128)(2,1)} %param.24), kind=kOutput, calls=%fused_computation.43 | convolution fusion | flops 17179869184 | bytes 46137344 | tf_op jit(solution)/shard_map/tm,tn->mn/dot_general | solution.py:17
  54.8 22.4 %fusion.16 = f32[2048,512]{1,0:T(8,128)} fusion(bf16[8192,2048]{1,0:T(8,128)(2,1)} %param.25, bf16[8192,512]{1,0:T(8,128)(2,1)S(1)} %bitcast.12), kind=kOutput, calls=%fused_computation.44 | convolution fusion | flops 17179869184 | bytes 46137344 | tf_op jit(solution)/shard_map/tm,tn->mn/dot_general | solution.py:17
  77.2 11.2 %fusion.13 = f32[512,512]{1,0:T(8,128)} fusion(bf16[8192,512]{1,0:T(8,128)(2,1)} %param.20, bf16[8192,512]{1,0:T(8,128)(2,1)} %param.21), kind=kOutput, calls=%fused_computation.41 | convolution fusion | flops 4294967296 | bytes 17825792 | tf_op jit(solution)/shard_map/tm,tn->mn/dot_general | solution.py:17
  88.5 0.6 copy-done.22
  89.1 0.6 fusion.12
  90.4 0.9 multiply_reduce_fusion.7
  91.3 4.3 multiply_reduce_fusion.1
  95.6 1.7 multiply_reduce_fusion.3
  97.3 1.6 multiply_reduce_fusion.5
  98.9 297.3 %all-reduce.6.cloned.1.call-done = (f32[512,512]{1,0:T(8,128)}, f32[512,2048]{1,0:T(8,128)}, f32[512,2048]{1,0:T(8,128)}, f32[2048,512]{1,0:T(8,128)}) async-done(((f32[512,512]{1,0:T(8,128)}, f32[512,2048]{1,0:T(8,128)}, f32[512,2048]{1,0:T(8,128)}, f32[2048,512]{1,0:T(8,128)}), (f32[512,512]{1,0:T(8,128)}, f32[512,2048]{1,0:T(8,128)}, f32[512,2048]{1,0:T(8,128)}, ...) | async-done | bytes 13631504 | tf_op jit(solution)/shard_map/psum | solution.py:18
  396.3 3.1 fusion.4
  399.8 0.8 fusion.2
  401.0 0.8 fusion
  402.0 8.1 %all-reduce.2 = (f32[512]{0:T(512)S(1)}, f32[512]{0:T(512)S(1)}, f32[512]{0:T(512)S(1)}, f32[2048]{0:T(1024)S(1)}) all-reduce(f32[512]{0:T(512)S(1)} %get-tuple-element.19, f32[512]{0:T(512)S(1)} %get-tuple-element.17, f32[512]{0:T(512)S(1)} %get-tuple-element.15, ...), channel_id=1, replica_groups=mesh['dp'=2,'col'=2,'row'=2] {'col'}, use_global_device_ids=true, to_apply=%region_4.0 | all-reduce | flops 3584 | bytes 28672 | tf_op jit(solution)/shard_map/psum | solution.py:20
  410.1 1.2 fusion.8
  411.3 1.2 fusion.11
  412.6 1.2 fusion.9
  413.8 1.2 fusion.10
  415.1 4.6 all-reduce.1
  419.7 0.8 multiply_add_fusion.7
  420.5 0.8 multiply_add_fusion.5
  421.4 0.7 multiply_add_fusion.6
  422.1 0.7 multiply_add_fusion.10
  422.8 5.2 %multiply_reduce_fusion = f32[]{:T(128)} fusion(f32[2048,512]{1,0:T(8,128)} %get-tuple-element.43, f32[]{:T(128)} %get-tuple-element.34, f32[512]{0:T(512)S(1)} %multiply_add_fusion.7, f32[2048]{0:T(1024)S(1)} %get-tuple-element.45), kind=kLoop, calls=%fused_computation.1 | loop fusion | flops 5242879 | bytes 4204552 | tf_op jit(solution)/shard_map/reduce_sum | solution.py:27
  427.9 3.1 multiply_reduce_fusion.2
  431.1 3.0 multiply_reduce_fusion.4
  434.1 1.7 multiply_reduce_fusion.6
  435.8 7.2 %all-reduce = (f32[]{:T(128)}, f32[]{:T(128)}, f32[]{:T(128)}, f32[]{:T(128)}, f32[]{:T(128)}, /*index=5*/f32[]{:T(128)}, f32[]{:T(128)}, f32[]{:T(128)}) all-reduce(f32[]{:T(128)} %multiply_reduce_fusion.6, f32[]{:T(128)} %multiply_reduce_fusion.7, f32[]{:T(128)} %multiply_reduce_fusion.4, ...), channel_id=1, replica_groups=mesh['dp'=2,'col'=2,'row'=2] {'row','col'}, use_global_device_ids=true, to_apply=%region_10.0 | all-reduce | flops 8 | bytes 64 | tf_op jit(solution)/shard_map/psum | solution.py:27
  453.1 6.6 %multiply_subtract_fusion = f32[2048,512]{1,0:T(8,128)} fusion(f32[2048,512]{1,0:T(8,128)} %param.30, f32[]{:T(128)S(6)} %max.31, f32[]{:T(128)S(6)} %mul.249, f32[2048,512]{1,0:T(8,128)} %get-tuple-element.43, f32[]{:T(128)} %get-tuple-element.34, f32[512]{0:T(512)S(1)} %multiply_add_fusion.7, f32[2048]{0:T(1024)S(1)} %get-tuple-element.45), kind=kLoop, calls=%fused_computation | loop fusion | flops 6291456 | bytes 12593164 | tf_op jit(solution)/shard_map/sub | solution.py:31
  459.6 2.7 multiply_subtract_fusion.3
  462.4 7.5 %multiply_subtract_fusion.1 = (f32[512,2048]{1,0:T(8,128)}, f32[512,2048]{1,0:T(8,128)}) fusion(f32[512,2048]{1,0:T(8,128)} %param.29, f32[]{:T(128)S(6)} %max.29, f32[]{:T(128)S(6)} %mul.236, f32[512,2048]{1,0:T(8,128)S(1)} %copy-done.5, f32[]{:T(128)} %get-tuple-element.32, f32[2048]{0:T(1024)S(1)} %multiply_add_fusion.5, f32[512]{0:T(512)S(1)} %get-tuple-element.47, ...), kind=kLoop, calls=%fused_computation.5 | loop fusion | flops 12582912 | bytes 25186328 | tf_op jit(solution)/shard_map/sub | solution.py:31
  (65 shorter events, 1.2 us)
Async XLA Ops:
  7.2 389.1 %all-reduce.6.cloned.1.call-start = ((), (), s32[]{:S(2)}) async-start(), calls=%async_computation | async-start | bytes 27262976 | tf_op jit(solution)/shard_map/psum | solution.py:18
  7.2 25.0 %copy-start.28 = (bf16[8192,512]{1,0:T(8,128)(2,1)S(1)}, bf16[8192,512]{1,0:T(8,128)(2,1)}, u32[]{:S(2)}) copy-start(bf16[8192,512]{1,0:T(8,128)(2,1)} %param.22) | copy-start | bytes 25165828
  7.2 47.6 %slice-start = ((s8[8388608]{0:T(1024)(128)(4,1)}), s8[4194304]{0:T(1024)(128)(4,1)S(1)}, s32[]{:S(2)}) async-start(s8[8388608]{0:T(1024)(128)(4,1)} %bitcast.11), calls=%async_computation.1 | async-start | bytes 8388608
  32.2 22.6 %slice-start.1 = ((s8[8388608]{0:T(1024)(128)(4,1)}), s8[4194304]{0:T(1024)(128)(4,1)S(1)}, s32[]{:S(2)}) async-start(s8[8388608]{0:T(1024)(128)(4,1)} %bitcast.11), calls=%async_computation.2 | async-start | bytes 8388608
  88.5 0.7 copy-start.22
  88.5 1.9 copy-start.10
  90.4 5.2 %copy-start.8 = (f32[512,2048]{1,0:T(8,128)S(1)}, f32[512,2048]{1,0:T(8,128)}, u32[]{:S(2)}) copy-start(f32[512,2048]{1,0:T(8,128)} %param.29) | copy-start | bytes 12582916
  91.3 6.0 %copy-start.6 = (f32[512,2048]{1,0:T(8,128)S(1)}, f32[512,2048]{1,0:T(8,128)}, u32[]{:S(2)}) copy-start(f32[512,2048]{1,0:T(8,128)} %param.28) | copy-start | bytes 12582916
  396.3 3.4 copy-start.3
  396.3 4.7 copy-start
  399.7 2.1 copy-start.9
  399.7 10.4 %copy-start.19 = (f32[2048]{0:T(1024)S(1)}, f32[2048]{0:T(1024)}, u32[]{:S(2)}) copy-start(f32[2048]{0:T(1024)} %param.37) | copy-start | bytes 24580
  399.7 11.6 %copy-start.25 = (f32[512]{0:T(512)S(1)}, f32[512]{0:T(512)}, u32[]{:S(2)}) copy-start(f32[512]{0:T(512)} %param.31) | copy-start | bytes 6148
  399.7 12.9 %copy-start.26 = (f32[512]{0:T(512)S(1)}, f32[512]{0:T(512)}, u32[]{:S(2)}) copy-start(f32[512]{0:T(512)} %param.35) | copy-start | bytes 6148
  399.7 14.1 %copy-start.27 = (f32[512]{0:T(512)S(1)}, f32[512]{0:T(512)}, u32[]{:S(2)}) copy-start(f32[512]{0:T(512)} %param.33) | copy-start | bytes 6148
  399.7 20.0 %copy-start.23 = (f32[512]{0:T(512)S(1)}, f32[512]{0:T(512)}, u32[]{:S(2)}) copy-start(f32[512]{0:T(512)} %param.38) | copy-start | bytes 6148
  399.7 20.8 %copy-start.20 = (f32[2048]{0:T(1024)S(1)}, f32[2048]{0:T(1024)}, u32[]{:S(2)}) copy-start(f32[2048]{0:T(1024)} %param.36) | copy-start | bytes 24580
  399.8 21.6 %copy-start.21 = (f32[2048]{0:T(1024)S(1)}, f32[2048]{0:T(1024)}, u32[]{:S(2)}) copy-start(f32[2048]{0:T(1024)} %param.34) | copy-start | bytes 24580
  399.8 22.3 %copy-start.24 = (f32[512]{0:T(512)S(1)}, f32[512]{0:T(512)}, u32[]{:S(2)}) copy-start(f32[512]{0:T(512)} %param.32) | copy-start | bytes 6148
  411.3 41.7 %copy-start.13 = (f32[2048]{0:T(1024)}, f32[2048]{0:T(1024)S(1)}, u32[]{:S(2)}) copy-start(f32[2048]{0:T(1024)S(1)} %get-tuple-element.45) | copy-start | bytes 24580
  412.6 47.1 %copy-start.16 = (f32[512]{0:T(512)}, f32[512]{0:T(512)S(1)}, u32[]{:S(2)}) copy-start(f32[512]{0:T(512)S(1)} %get-tuple-element.51) | copy-start | bytes 6148
  413.8 48.5 %copy-start.17 = (f32[512]{0:T(512)}, f32[512]{0:T(512)S(1)}, u32[]{:S(2)}) copy-start(f32[512]{0:T(512)S(1)} %get-tuple-element.47) | copy-start | bytes 6148
  415.1 47.2 %copy-start.18 = (f32[512]{0:T(512)}, f32[512]{0:T(512)S(1)}, u32[]{:S(2)}) copy-start(f32[512]{0:T(512)S(1)} %get-tuple-element.49) | copy-start | bytes 6148
  419.7 8.2 %copy-start.4 = (f32[512,2048]{1,0:T(8,128)S(1)}, f32[512,2048]{1,0:T(8,128)}, u32[]{:S(2)}) copy-start(f32[512,2048]{1,0:T(8,128)} %get-tuple-element.42) | copy-start | bytes 12582916
  420.5 32.5 %copy-start.14 = (f32[512]{0:T(512)}, f32[512]{0:T(512)S(1)}, u32[]{:S(2)}) copy-start(f32[512]{0:T(512)S(1)} %multiply_add_fusion.7) | copy-start | bytes 6148
  421.4 41.0 %copy-start.11 = (f32[2048]{0:T(1024)}, f32[2048]{0:T(1024)S(1)}, u32[]{:S(2)}) copy-start(f32[2048]{0:T(1024)S(1)} %multiply_add_fusion.5) | copy-start | bytes 24580
  422.1 40.3 %copy-start.12 = (f32[2048]{0:T(1024)}, f32[2048]{0:T(1024)S(1)}, u32[]{:S(2)}) copy-start(f32[2048]{0:T(1024)S(1)} %multiply_add_fusion.6) | copy-start | bytes 24580
  422.7 36.9 %copy-start.15 = (f32[512]{0:T(512)}, f32[512]{0:T(512)S(1)}, u32[]{:S(2)}) copy-start(f32[512]{0:T(512)S(1)} %multiply_add_fusion.10) | copy-start | bytes 6148
  422.7 8.3 %copy-start.1 = (f32[512,2048]{1,0:T(8,128)S(1)}, f32[512,2048]{1,0:T(8,128)}, u32[]{:S(2)}) copy-start(f32[512,2048]{1,0:T(8,128)} %get-tuple-element.41) | copy-start | bytes 12582916
  453.0 9.3 %copy-start.2 = (f32[512,2048]{1,0:T(8,128)S(1)}, f32[512,2048]{1,0:T(8,128)}, u32[]{:S(2)}) copy-start(f32[512,2048]{1,0:T(8,128)} %get-tuple-element.41) | copy-start | bytes 12582916
  453.1 9.3 %copy-start.5 = (f32[512,2048]{1,0:T(8,128)S(1)}, f32[512,2048]{1,0:T(8,128)}, u32[]{:S(2)}) copy-start(f32[512,2048]{1,0:T(8,128)} %get-tuple-element.42) | copy-start | bytes 12582916
  453.1 9.3 %copy-start.7 = (f32[512,2048]{1,0:T(8,128)S(1)}, f32[512,2048]{1,0:T(8,128)}, u32[]{:S(2)}) copy-start(f32[512,2048]{1,0:T(8,128)} %param.28) | copy-start | bytes 12582916
Sparse Core Ops, SparseCore 0:
  88.6 307.5 all-reduce.5
where the time goes:
time: 477 us
  waiting for transfers between devices  297 us (62%)
  matrix products  81.2 us (17%)
  other arithmetic  51.1 us (11%)
  between operations  25 us (5%)
  blocking collectives  19.9 us (4%)
    psum x1, waiting for transfers between devices, matrix_step(): grad_block = lax.psum(part_grad, 'dp')  297 us
    dot_general x4, matrix products, matrix_step(): jnp.einsum('tm,tn->mn', x_block, dy_block, preferred_element_type=jnp.flo...  81.2 us
    sub x3, other arithmetic, matrix_step(): return (w_block - step_size * update, new_row, new_col)  16.7 us
    reduce_sum x4, other arithmetic, matrix_step(): jnp.sum(update * update)  13 us
  transfers between devices with their start and end apart: 1, of which 1 were waited for; matrix products, arithmetic and copies ran while one was open for 2% of the time, Pallas kernels for 0%

commit v1 on v0

v1 whole, which is shorter than its diff:
```python
import jax
import jax.numpy as jnp
from jax import lax
from jax.sharding import PartitionSpec as P

EPS_ONE = 1e-30
EPS_TWO = 1e-3
SWAP = [(0, 1), (1, 0)]


def swap_sum(value, axis):
    return value + lax.ppermute(value, axis, SWAP)


def plane_sum(value):
    return swap_sum(swap_sum(value, 'row'), 'col')


def finish(part_grad, recv_grad, w_block, row_old, col_old, hyper_vals):
    beta_two = hyper_vals[0]
    rho_step = hyper_vals[1]
    clip_thr = hyper_vals[2]
    m_total = w_block.shape[0] * 2
    n_total = w_block.shape[1] * 2
    grad_block = part_grad + recv_grad
    sq_grad = grad_block * grad_block + EPS_ONE
    row_sum = swap_sum(jnp.sum(sq_grad, axis=1), 'col')
    col_sum = swap_sum(jnp.sum(sq_grad, axis=0), 'row')
    new_row = beta_two * row_old + (1.0 - beta_two) * (row_sum / n_total)
    new_col = beta_two * col_old + (1.0 - beta_two) * (col_sum / m_total)
    row_total = swap_sum(jnp.sum(new_row), 'row')
    second_est = new_row[:, None] * new_col[None, :] / row_total
    update = grad_block / jnp.sqrt(second_est)
    upd_rms = jnp.sqrt(plane_sum(jnp.sum(update * update)) / (m_total * n_total))
    update = update / jnp.maximum(1.0, upd_rms / clip_thr)
    w_rms = jnp.sqrt(plane_sum(jnp.sum(w_block * w_block)) / (m_total * n_total))
    step_size = rho_step * jnp.maximum(EPS_TWO, w_rms)
    return (w_block - step_size * update, new_row, new_col)


def solution(mesh):
    act_spec = P('dp', 'row')
    grad_spec = P('dp', 'col')
    w_spec = P('row', 'col')
    row_spec = P('row')
    col_spec = P('col')
    in_specs = (act_spec, grad_spec, act_spec, grad_spec, grad_spec, act_spec, grad_spec,
                w_spec, w_spec, w_spec, w_spec,
                row_spec, col_spec, row_spec, col_spec, row_spec, col_spec, row_spec, col_spec, P())
    out_specs = (w_spec, row_spec, col_spec) * 4

    def per_device(x_attn, dy_attn, x_mlp, dy_gate, dy_up, h_mlp, dy_out, w_attn, w_gate, w_up, w_down,
                   r_attn, c_attn, r_gate, c_gate, r_up, c_up, r_down, c_down, hyper_params):
        results = []
        for x_block, dy_block, w_block, row_old, col_old in (
                (x_mlp, dy_gate, w_gate, r_gate, c_gate),
                (x_mlp, dy_up, w_up, r_up, c_up),
                (h_mlp, dy_out, w_down, r_down, c_down),
                (x_attn, dy_attn, w_attn, r_attn, c_attn)):
            part_grad = jnp.einsum('tm,tn->mn', x_block, dy_block, preferred_element_type=jnp.float32)
            recv_grad = lax.ppermute(part_grad, 'dp', SWAP)
            results.append(finish(part_grad, recv_grad, w_block, row_old, col_old, hyper_params))
        gate, up, down, attn = results
        return attn + gate + up + down

    return jax.shard_map(per_device, mesh=mesh, in_specs=in_specs, out_specs=out_specs, check_vma=False)
```

time: 477 us -> 436 us (0.914)
  waiting for transfers between devices: 297 us -> 231 us
  starting transfers between devices: 0.04 us -> 31.9 us
  blocking collectives: 19.9 us -> 0 us
  other arithmetic: 51.1 us -> 65.3 us
    psum x1 -> x0, waiting for transfers between devices: 297 us -> none  [matrix_step(): grad_block = lax.psum(part_grad, 'dp')]
    ppermute x0 -> x32, waiting for transfers between devices: none -> 231 us  [the longest x4 227 us: per_device(): recv_grad = lax.ppermute(part_grad, 'dp', SWAP)]
    ppermute x0 -> x32, starting transfers between devices: none -> 31.9 us  [the longest x28 26.3 us: swap_sum(): return value + lax.ppermute(value, axis, SWAP)]
    psum x3 -> x0, blocking collectives: 19.9 us -> none  [the longest x1 8.07 us: matrix_step(): row_sum = lax.psum(jnp.sum(sq_grad, axis=1), 'col')]
    reduce_sum x16, other arithmetic: 31.4 us -> 45.6 us  [the longest x4 20.4 us: finish(): col_sum = swap_sum(jnp.sum(sq_grad, axis=0), 'row')]
    sub x3 -> x4, other arithmetic: 16.7 us -> 17 us  [finish(): return (w_block - step_size * update, new_row, new_col)]
  transfers between devices with their start and end apart: 1 -> 32, of which waited for: 1 -> 7; matrix products, arithmetic and copies ran while one was open for 2% -> 26% of each run, Pallas kernels for 0% -> 0%
where the time goes in v1:
time: 436 us; the launch traced here: 435 us
  waiting for transfers between devices  231 us (53%)
  matrix products  77.3 us (18%)
  other arithmetic  65.3 us (15%)
  starting transfers between devices  31.9 us (7%)
  between operations  27.7 us (6%)
    ppermute x4, waiting for transfers between devices, per_device(): recv_grad = lax.ppermute(part_grad, 'dp', SWAP)  227 us
    dot_general x4, matrix products, per_device(): jnp.einsum('tm,tn->mn', x_block, dy_block, preferred_element_type=jnp.flo...  77.3 us
    ppermute x28, starting transfers between devices, swap_sum(): return value + lax.ppermute(value, axis, SWAP)  26.3 us
    reduce_sum x4, other arithmetic, finish(): col_sum = swap_sum(jnp.sum(sq_grad, axis=0), 'row')  20.4 us
    sub x4, other arithmetic, finish(): return (w_block - step_size * update, new_row, new_col)  17 us
    reduce_sum x4, other arithmetic, finish(): jnp.sum(update * update)  11.6 us
  transfers between devices with their start and end apart: 32, of which 7 were waited for; matrix products, arithmetic and copies ran while one was open for 26% of the time, Pallas kernels for 0%

profile of v1, /device:TPU:0, one launch (start us, length us, event | category | flops | bytes accessed | tf_op | source)
XLA Modules:
  0.0 435.2 jit_solution(11107490024368986692)
XLA Ops:
  0.7 25.0 %fusion.16 = f32[2048,512]{1,0:T(8,128)} fusion(bf16[8192,2048]{1,0:T(8,128)(2,1)} %param.25, bf16[8192,512]{1,0:T(8,128)(2,1)} %param.26), kind=kOutput, calls=%fused_computation.44 | convolution fusion | flops 17179869184 | bytes 46137344 | tf_op jit(solution)/shard_map/tm,tn->mn/dot_general | solution.py:60
  25.6 3.4 collective-permute-start.26
  29.0 22.6 %fusion.15 = f32[512,2048]{1,0:T(8,128)} fusion(bf16[8192,512]{1,0:T(8,128)(2,1)S(1)} %copy-done.24, bf16[8192,2048]{1,0:T(8,128)(2,1)} %param.24), kind=kOutput, calls=%fused_computation.43 | convolution fusion | flops 17179869184 | bytes 46137344 | tf_op jit(solution)/shard_map/tm,tn->mn/dot_general | solution.py:60
  51.6 22.6 %fusion.14 = f32[512,2048]{1,0:T(8,128)} fusion(bf16[8192,512]{1,0:T(8,128)(2,1)S(1)} %copy-done.24, bf16[8192,2048]{1,0:T(8,128)(2,1)} %param.23), kind=kOutput, calls=%fused_computation.42 | convolution fusion | flops 17179869184 | bytes 46137344 | tf_op jit(solution)/shard_map/tm,tn->mn/dot_general | solution.py:60
  74.1 1.9 collective-permute-start.10
  76.0 7.2 %fusion.13 = f32[512,512]{1,0:T(8,128)S(1)} fusion(bf16[8192,512]{1,0:T(8,128)(2,1)S(1)} %bitcast.12, bf16[8192,512]{1,0:T(8,128)(2,1)} %param.21), kind=kOutput, calls=%fused_computation.41 | convolution fusion | flops 4294967296 | bytes 17825792 | tf_op jit(solution)/shard_map/tm,tn->mn/dot_general | solution.py:60
  83.6 1.7 multiply_reduce_fusion.1
  87.5 4.3 multiply_reduce_fusion.3
  91.7 1.7 multiply_reduce_fusion.5
  95.2 226.6 %collective-permute-done.2 = f32[512,512]{1,0:T(8,128)S(1)} collective-permute-done((f32[512,512]{1,0:T(8,128)S(1)}, f32[512,512]{1,0:T(8,128)S(1)}, u32[]{:S(2)}, u32[]{:S(2)}) %collective-permute-start.2) | collective-permute-done | bytes 1048608 | tf_op jit(solution)/shard_map/ppermute | solution.py:61
  322.8 1.5 fusion.6
  324.3 1.7 collective-permute-start.3
  328.9 1.6 collective-permute-start.25
  332.5 2.4 collective-permute-start.17
  336.0 2.4 collective-permute-start.9
  340.4 2.3 collective-permute-start.1
  352.7 2.4 collective-permute-start.7
  357.6 1.3 multiply_subtract_fusion.3
  358.9 6.3 %fusion.4 = (f32[512]{0:T(512)S(1)}, f32[2048]{0:T(1024)S(1)}, f32[2048,512]{1,0:T(8,128)}) fusion(f32[2048,512]{1,0:T(8,128)} %fusion.16, f32[2048,512]{1,0:T(8,128)} %collective-permute-done.26), kind=kLoop, calls=%fused_computation.19 | loop fusion | flops 5240320 | bytes 12593152 | tf_op jit(solution)/shard_map/reduce_sum | solution.py:28
  366.3 6.3 %fusion.2 = (f32[2048]{0:T(1024)S(1)}, f32[512]{0:T(512)S(1)}, f32[512,2048]{1,0:T(8,128)}) fusion(f32[512,2048]{1,0:T(8,128)} %fusion.15, f32[512,2048]{1,0:T(8,128)} %collective-permute-done.18), kind=kLoop, calls=%fused_computation.17 | loop fusion | flops 5240320 | bytes 12593152 | tf_op jit(solution)/shard_map/reduce_sum | solution.py:28
  373.8 6.3 %fusion = (f32[2048]{0:T(1024)S(1)}, f32[512]{0:T(512)S(1)}, f32[512,2048]{1,0:T(8,128)}) fusion(f32[512,2048]{1,0:T(8,128)} %fusion.14, f32[512,2048]{1,0:T(8,128)} %collective-permute-done.10), kind=kLoop, calls=%fused_computation.15 | loop fusion | flops 5240320 | bytes 12593152 | tf_op jit(solution)/shard_map/reduce_sum | solution.py:28
  382.4 1.3 collective-permute-done.11
  388.7 1.4 fusion.8
  390.8 4.1 multiply_reduce_fusion.2
  396.0 2.4 multiply_reduce_fusion.4
  399.7 4.1 multiply_reduce_fusion
  405.6 2.4 collective-permute-start.23
  409.3 2.3 collective-permute-start.15
  412.9 2.4 collective-permute-start.31
  418.1 7.2 %multiply_subtract_fusion.1 = f32[512,2048]{1,0:T(8,128)} fusion(f32[512,2048]{1,0:T(8,128)} %param.29, f32[]{:T(128)S(6)} %max.29, f32[]{:T(128)S(6)} %mul.236, f32[512,2048]{1,0:T(8,128)} %get-tuple-element.25, f32[]{:T(128)S(6)} %add.169, f32[2048]{0:T(1024)S(1)} %multiply_add_fusion.5, f32[512]{0:T(512)S(1)} %get-tuple-element.24), kind=kLoop, calls=%fused_computation.5 | loop fusion | flops 6291456 | bytes 12593164 | tf_op jit(solution)/shard_map/sub | solution.py:38
  425.3 3.2 multiply_subtract_fusion.2
  429.8 5.4 %multiply_subtract_fusion = f32[2048,512]{1,0:T(8,128)} fusion(f32[2048,512]{1,0:T(8,128)} %param.30, f32[]{:T(128)S(6)} %max.31, f32[]{:T(128)S(6)} %mul.249, f32[2048,512]{1,0:T(8,128)} %get-tuple-element.22, f32[]{:T(128)S(6)} %add.181, f32[512]{0:T(512)S(1)} %multiply_add_fusion.7, f32[2048]{0:T(1024)S(1)} %get-tuple-element.21), kind=kLoop, calls=%fused_computation | loop fusion | flops 6291456 | bytes 12593164 | tf_op jit(solution)/shard_map/sub | solution.py:38
  (116 shorter events, 20.2 us)
Async XLA Ops:
  25.6 333.3 %collective-permute-start.26 = (f32[2048,512]{1,0:T(8,128)}, f32[2048,512]{1,0:T(8,128)}, u32[]{:S(2)}, u32[]{:S(2)}) collective-permute-start(f32[2048,512]{1,0:T(8,128)} %fusion.16), channel_id=1, source_target_pairs={{0,4},{4,0},{1,5},{5,1},{2,6},{6,2},{3,7},{7,3}} | collective-permute-start | bytes 12582920 | tf_op jit(solution)/shard_map/ppermute | solution.py:61
  51.6 314.7 %collective-permute-start.18 = (f32[512,2048]{1,0:T(8,128)}, f32[512,2048]{1,0:T(8,128)}, u32[]{:S(2)}, u32[]{:S(2)}) collective-permute-start(f32[512,2048]{1,0:T(8,128)} %fusion.15), channel_id=1, source_target_pairs={{0,4},{4,0},{1,5},{5,1},{2,6},{6,2},{3,7},{7,3}} | collective-permute-start | bytes 12582920 | tf_op jit(solution)/shard_map/ppermute | solution.py:61
  74.1 299.6 %collective-permute-start.10 = (f32[512,2048]{1,0:T(8,128)}, f32[512,2048]{1,0:T(8,128)}, u32[]{:S(2)}, u32[]{:S(2)}) collective-permute-start(f32[512,2048]{1,0:T(8,128)} %fusion.14), channel_id=1, source_target_pairs={{0,4},{4,0},{1,5},{5,1},{2,6},{6,2},{3,7},{7,3}} | collective-permute-start | bytes 12582920 | tf_op jit(solution)/shard_map/ppermute | solution.py:61
  83.2 238.6 %collective-permute-start.2 = (f32[512,512]{1,0:T(8,128)S(1)}, f32[512,512]{1,0:T(8,128)S(1)}, u32[]{:S(2)}, u32[]{:S(2)}) collective-permute-start(f32[512,512]{1,0:T(8,128)S(1)} %fusion.13), channel_id=1, source_target_pairs={{0,4},{4,0},{1,5},{5,1},{2,6},{6,2},{3,7},{7,3}} | collective-permute-start | bytes 3145736 | tf_op jit(solution)/shard_map/ppermute | solution.py:61
  85.3 8.1 %collective-permute-start.24 = (f32[]{:T(128)}, f32[]{:T(128)}, u32[]{:S(2)}, u32[]{:S(2)}) collective-permute-start(f32[]{:T(128)} %multiply_reduce_fusion.1), channel_id=1, source_target_pairs={{0,1},{1,0},{2,3},{3,2},{4,5},{5,4},{6,7},{7,6}} | collective-permute-start | bytes 20 | tf_op jit(solution)/shard_map/ppermute | solution.py:12
  93.4 230.9 %collective-permute-start.16 = (f32[]{:T(128)}, f32[]{:T(128)}, u32[]{:S(2)}, u32[]{:S(2)}) collective-permute-start(f32[]{:T(128)} %multiply_reduce_fusion.3), channel_id=1, source_target_pairs={{0,1},{1,0},{2,3},{3,2},{4,5},{5,4},{6,7},{7,6}} | collective-permute-start | bytes 20 | tf_op jit(solution)/shard_map/ppermute | solution.py:12
  322.8 4.5 %collective-permute-start.8 = (f32[]{:T(128)}, f32[]{:T(128)}, u32[]{:S(2)}, u32[]{:S(2)}) collective-permute-start(f32[]{:T(128)} %multiply_reduce_fusion.5), channel_id=1, source_target_pairs={{0,1},{1,0},{2,3},{3,2},{4,5},{5,4},{6,7},{7,6}} | collective-permute-start | bytes 20 | tf_op jit(solution)/shard_map/ppermute | solution.py:12
  324.3 21.0 %collective-permute-start.3 = (f32[512]{0:T(512)S(1)}, f32[512]{0:T(512)S(1)}, u32[]{:S(2)}, u32[]{:S(2)}) collective-permute-start(f32[512]{0:T(512)S(1)} %get-tuple-element.19), channel_id=1, source_target_pairs={{0,2},{2,0},{1,3},{3,1},{4,6},{6,4},{5,7},{7,5}} | collective-permute-start | bytes 6152 | tf_op jit(solution)/shard_map/ppermute | solution.py:12
  327.3 1.5 collective-permute-start
  328.9 3.6 collective-permute-start.25
  332.5 3.6 collective-permute-start.17
  336.0 4.3 collective-permute-start.9
  340.4 3.6 collective-permute-start.1
  345.3 1.8 collective-permute-start.4
  346.6 1.3 collective-permute-start.5
  350.3 1.1 collective-permute-start.6
  352.7 3.6 collective-permute-start.7
  365.2 23.5 %collective-permute-start.27 = (f32[2048]{0:T(1024)S(1)}, f32[2048]{0:T(1024)S(1)}, u32[]{:S(2)}, u32[]{:S(2)}) collective-permute-start(f32[2048]{0:T(1024)S(1)} %get-tuple-element.13), channel_id=1, source_target_pairs={{0,2},{2,0},{1,3},{3,1},{4,6},{6,4},{5,7},{7,5}} | collective-permute-start | bytes 24584 | tf_op jit(solution)/shard_map/ppermute | solution.py:12
  366.3 18.6 %collective-permute-start.28 = (f32[512]{0:T(512)S(1)}, f32[512]{0:T(512)S(1)}, u32[]{:S(2)}, u32[]{:S(2)}) collective-permute-start(f32[512]{0:T(512)S(1)} %get-tuple-element.12), channel_id=1, source_target_pairs={{0,1},{1,0},{2,3},{3,2},{4,5},{5,4},{6,7},{7,6}} | collective-permute-start | bytes 6152 | tf_op jit(solution)/shard_map/ppermute | solution.py:12
  372.6 8.6 %collective-permute-start.19 = (f32[512]{0:T(512)S(1)}, f32[512]{0:T(512)S(1)}, u32[]{:S(2)}, u32[]{:S(2)}) collective-permute-start(f32[512]{0:T(512)S(1)} %get-tuple-element.15), channel_id=1, source_target_pairs={{0,2},{2,0},{1,3},{3,1},{4,6},{6,4},{5,7},{7,5}} | collective-permute-start | bytes 6152 | tf_op jit(solution)/shard_map/ppermute | solution.py:12
  373.5 16.6 %collective-permute-start.20 = (f32[2048]{0:T(1024)S(1)}, f32[2048]{0:T(1024)S(1)}, u32[]{:S(2)}, u32[]{:S(2)}) collective-permute-start(f32[2048]{0:T(1024)S(1)} %get-tuple-element.14), channel_id=1, source_target_pairs={{0,1},{1,0},{2,3},{3,2},{4,5},{5,4},{6,7},{7,6}} | collective-permute-start | bytes 24584 | tf_op jit(solution)/shard_map/ppermute | solution.py:12
  380.1 3.6 collective-permute-start.11
  381.1 14.2 %collective-permute-start.12 = (f32[2048]{0:T(1024)S(1)}, f32[2048]{0:T(1024)S(1)}, u32[]{:S(2)}, u32[]{:S(2)}) collective-permute-start(f32[2048]{0:T(1024)S(1)} %get-tuple-element.16), channel_id=1, source_target_pairs={{0,1},{1,0},{2,3},{3,2},{4,5},{5,4},{6,7},{7,6}} | collective-permute-start | bytes 24584 | tf_op jit(solution)/shard_map/ppermute | solution.py:12
  383.6 2.4 collective-permute-start.21
  384.9 2.4 collective-permute-start.13
  390.1 8.4 %collective-permute-start.29 = (f32[]{:T(128)}, f32[]{:T(128)}, u32[]{:S(2)}, u32[]{:S(2)}) collective-permute-start(f32[]{:T(128)} %get-tuple-element.20), channel_id=1, source_target_pairs={{0,1},{1,0},{2,3},{3,2},{4,5},{5,4},{6,7},{7,6}} | collective-permute-start | bytes 20 | tf_op jit(solution)/shard_map/ppermute | solution.py:12
  394.9 9.5 %collective-permute-start.22 = (f32[]{:T(128)}, f32[]{:T(128)}, u32[]{:S(2)}, u32[]{:S(2)}) collective-permute-start(f32[]{:T(128)} %multiply_reduce_fusion.2), channel_id=1, source_target_pairs={{0,1},{1,0},{2,3},{3,2},{4,5},{5,4},{6,7},{7,6}} | collective-permute-start | bytes 20 | tf_op jit(solution)/shard_map/ppermute | solution.py:12
  398.4 9.5 %collective-permute-start.14 = (f32[]{:T(128)}, f32[]{:T(128)}, u32[]{:S(2)}, u32[]{:S(2)}) collective-permute-start(f32[]{:T(128)} %multiply_reduce_fusion.4), channel_id=1, source_target_pairs={{0,1},{1,0},{2,3},{3,2},{4,5},{5,4},{6,7},{7,6}} | collective-permute-start | bytes 20 | tf_op jit(solution)/shard_map/ppermute | solution.py:12
  403.8 7.8 %collective-permute-start.30 = (f32[]{:T(128)}, f32[]{:T(128)}, u32[]{:S(2)}, u32[]{:S(2)}) collective-permute-start(f32[]{:T(128)} %multiply_reduce_fusion), channel_id=1, source_target_pairs={{0,1},{1,0},{2,3},{3,2},{4,5},{5,4},{6,7},{7,6}} | collective-permute-start | bytes 20 | tf_op jit(solution)/shard_map/ppermute | solution.py:12
  405.6 9.7 %collective-permute-start.23 = (f32[]{:T(128)}, f32[]{:T(128)}, u32[]{:S(2)}, u32[]{:S(2)}) collective-permute-start(f32[]{:T(128)} %add.170), channel_id=1, source_target_pairs={{0,2},{2,0},{1,3},{3,1},{4,6},{6,4},{5,7},{7,5}} | collective-permute-start | bytes 20 | tf_op jit(solution)/shard_map/ppermute | solution.py:12
  409.3 7.3 %collective-permute-start.15 = (f32[]{:T(128)}, f32[]{:T(128)}, u32[]{:S(2)}, u32[]{:S(2)}) collective-permute-start(f32[]{:T(128)} %add.159), channel_id=1, source_target_pairs={{0,2},{2,0},{1,3},{3,1},{4,6},{6,4},{5,7},{7,5}} | collective-permute-start | bytes 20 | tf_op jit(solution)/shard_map/ppermute | solution.py:12
  412.9 15.6 %collective-permute-start.31 = (f32[]{:T(128)}, f32[]{:T(128)}, u32[]{:S(2)}, u32[]{:S(2)}) collective-permute-start(f32[]{:T(128)} %add.182), channel_id=1, source_target_pairs={{0,2},{2,0},{1,3},{3,1},{4,6},{6,4},{5,7},{7,5}} | collective-permute-start | bytes 20 | tf_op jit(solution)/shard_map/ppermute | solution.py:12
  (27 other events, 980.3 us)

commit v2 on v0

v2 whole, which is shorter than its diff:
```python
import functools
import jax
import jax.numpy as jnp
from jax import lax
from jax.experimental import pallas as pl
from jax.experimental.pallas import tpu as pltpu
from jax.sharding import PartitionSpec as P

EPS_ONE = 1e-30
EPS_TWO = 1e-3
SWAP = [(0, 1), (1, 0)]
MESH = pl.DeviceIdType.MESH
LANES = 128
NAMES = ('gate', 'up', 'down', 'attn')
GATE_WIDTHS = (256, 768, 1024)


def peers():
    row_other = 1 - lax.axis_index('row')
    col_other = 1 - lax.axis_index('col')
    return ({'row': row_other}, {'col': col_other}, {'row': row_other, 'col': col_other})


def stats_kernel(n_token, widths, step, m_total, n_total, *refs):
    n_piece = len(widths)
    refs = refs[n_token:]
    hyper, w_sq, row_old, col_old = refs[:4]
    parts = refs[4:4 + n_piece]
    recvs = refs[4 + n_piece:4 + 2 * n_piece]
    (grad, row_scale, col_scale, new_row, new_col,
     row_acc, row_col, send_row, send_col, recv_row, recv_col, send_val, recv_val,
     vec_send, vec_recv, val_send, val_recv) = refs[4 + 2 * n_piece:]
    rows, cols = grad.shape
    others = peers()
    row_peer, col_peer, _ = others

    barrier = pltpu.get_barrier_semaphore()
    for other in others:
        pl.semaphore_signal(barrier, inc=1, device_id=other, device_id_type=MESH)

    def first(i, col_acc):
        band = pl.ds(pl.multiple_of(i * step, step), step)
        lane_sum = jnp.zeros((step, LANES), jnp.float32)
        sums = []
        start = 0
        for part, recv, width in zip(parts, recvs, widths):
            piece = part[band, :] + recv[band, :]
            grad[band, start:start + width] = piece
            sq = piece * piece + EPS_ONE
            for k in range(width // LANES):
                lane_sum = lane_sum + sq[:, k * LANES:(k + 1) * LANES]
            sums.append(sq.reshape(step // 8, 8, width).sum(axis=0))
            start += width
        row_acc[band, :] = lane_sum
        return tuple(a + s for a, s in zip(col_acc, sums))

    col_acc = lax.fori_loop(0, rows // step, first, tuple(jnp.zeros((8, w), jnp.float32) for w in widths))
    start = 0
    for acc, width in zip(col_acc, widths):
        send_col[:, start:start + width] = jnp.sum(acc, axis=0, keepdims=True)
        start += width
    for k in range(rows // LANES):
        tile = row_acc[k * LANES:(k + 1) * LANES, :].T
        send_row[:, k * LANES:(k + 1) * LANES] = jnp.sum(tile, axis=0, keepdims=True)
    pl.semaphore_wait(barrier, 3)
    row_copy = pltpu.make_async_remote_copy(send_row, recv_row, vec_send.at[0], vec_recv.at[0],
                                            device_id=col_peer, device_id_type=MESH)
    col_copy = pltpu.make_async_remote_copy(send_col, recv_col, vec_send.at[1], vec_recv.at[1],
                                            device_id=row_peer, device_id_type=MESH)
    row_copy.start()
    col_copy.start()
    row_copy.wait()
    col_copy.wait()
    beta_two = hyper[0]
    row_now = beta_two * row_old[...] + (1.0 - beta_two) * ((send_row[...] + recv_row[...]) / n_total)
    col_now = beta_two * col_old[...] + (1.0 - beta_two) * ((send_col[...] + recv_col[...]) / m_total)
    new_row[...] = row_now
    new_col[...] = col_now
    row_inv = 1.0 / jnp.sqrt(row_now)
    col_inv = 1.0 / jnp.sqrt(col_now)
    col_scale[...] = col_inv
    for k in range(rows // LANES):
        tile = jnp.broadcast_to(row_inv[:, k * LANES:(k + 1) * LANES], (LANES, LANES))
        row_col[k * LANES:(k + 1) * LANES, :] = tile.T

    def second(i, col_acc):
        band = pl.ds(pl.multiple_of(i * step, step), step)
        scale = row_col[band, :]
        sums = []
        for k in range(cols // LANES):
            upd = grad[band, k * LANES:(k + 1) * LANES] * scale
            sums.append((upd * upd).reshape(step // 8, 8, LANES).sum(axis=0))
        return tuple(a + s for a, s in zip(col_acc, sums))

    col_acc = lax.fori_loop(0, rows // step, second,
                            tuple(jnp.zeros((8, LANES), jnp.float32) for _ in range(cols // LANES)))
    lane_sum = jnp.zeros((8, LANES), jnp.float32)
    col_sq = col_inv * col_inv
    for k, acc in enumerate(col_acc):
        lane_sum = lane_sum + acc * col_sq[:, k * LANES:(k + 1) * LANES]
    upd_sq = jnp.sum(lane_sum)
    row_part = jnp.sum(row_now)
    which = lax.broadcasted_iota(jnp.int32, (8, LANES), 0)
    send_val[...] = jnp.where(which == 0, upd_sq, jnp.where(which == 1, row_part, w_sq[0, 0]))
    copies = [pltpu.make_async_remote_copy(send_val, recv_val.at[k], val_send.at[k], val_recv.at[k],
                                           device_id=other, device_id_type=MESH)
              for k, other in enumerate(others)]
    for copy in copies:
        copy.start()
    for copy in copies:
        copy.wait()
    pair = send_val[...] + recv_val[0]
    total = pair + (recv_val[1] + recv_val[2])
    size = m_total * n_total
    row_total = pair[1:2, :1]
    upd_rms = jnp.sqrt(row_total * total[0:1, :1] / size)
    w_rms = jnp.sqrt(total[2:3, :1] / size)
    clip = jnp.maximum(1.0, upd_rms / hyper[2])
    factor = hyper[1] * jnp.maximum(EPS_TWO, w_rms) * jnp.sqrt(row_total) / clip
    row_scale[...] = row_inv * factor


def statistics(tokens, parts, recvs, w_sq, row_old, col_old, hyper, index):
    rows = parts[0].shape[0]
    widths = tuple(p.shape[1] for p in parts)
    cols = sum(widths)
    n_piece = len(parts)
    vmem = pl.BlockSpec(memory_space=pltpu.VMEM)
    smem = pl.BlockSpec(memory_space=pltpu.SMEM)
    anyw = pl.BlockSpec(memory_space=pl.ANY)
    f32 = jnp.float32
    return pl.pallas_call(
        functools.partial(stats_kernel, len(tokens), widths, 16, 2 * rows, 2 * cols),
        out_shape=[jax.ShapeDtypeStruct(s, f32) for s in ((rows, cols), (1, rows), (1, cols), (1, rows), (1, cols))],
        in_specs=[anyw] * len(tokens) + [smem] * 2 + [vmem] * (2 + 2 * n_piece),
        out_specs=[vmem] * 5,
        scratch_shapes=[
            pltpu.VMEM((rows, LANES), f32), pltpu.VMEM((rows, LANES), f32),
            pltpu.VMEM((1, rows), f32), pltpu.VMEM((1, cols), f32),
            pltpu.VMEM((1, rows), f32), pltpu.VMEM((1, cols), f32),
            pltpu.VMEM((8, LANES), f32), pltpu.VMEM((3, 8, LANES), f32),
            pltpu.SemaphoreType.DMA((2,)), pltpu.SemaphoreType.DMA((2,)),
            pltpu.SemaphoreType.DMA((3,)), pltpu.SemaphoreType.DMA((3,)),
        ],
        compiler_params=pltpu.CompilerParams(collective_id=index, has_side_effects=True,
                                             vmem_limit_bytes=32 * 1024 * 1024),
        cost_estimate=pl.CostEstimate(flops=8 * rows * cols * 100, bytes_accessed=12 * rows * cols, transcendentals=0),
    )(*tokens, hyper, w_sq.reshape(1, 1), row_old.reshape(1, rows), col_old.reshape(1, cols), *parts, *recvs)


def solution(mesh):
    act_spec = P('dp', 'row')
    grad_spec = P('dp', 'col')
    w_spec = P('row', 'col')
    row_spec = P('row')
    col_spec = P('col')
    in_specs = (act_spec, grad_spec, act_spec, grad_spec, grad_spec, act_spec, grad_spec,
                w_spec, w_spec, w_spec, w_spec,
                row_spec, col_spec, row_spec, col_spec, row_spec, col_spec, row_spec, col_spec, P())
    out_specs = (w_spec, row_spec, col_spec) * 4

    def product(x_block, dy_block):
        return jnp.einsum('tm,tn->mn', x_block, dy_block, preferred_element_type=jnp.float32)

    def per_device(x_attn, dy_attn, x_mlp, dy_gate, dy_up, h_mlp, dy_out, w_attn, w_gate, w_up, w_down,
                   r_attn, c_attn, r_gate, c_gate, r_up, c_up, r_down, c_down, hyper_params):
        order = []
        parts = {name: [] for name in NAMES}
        recvs = {name: [] for name in NAMES}
        start = 0
        for width in GATE_WIDTHS:
            order.append(('gate', x_mlp, dy_gate[:, start:start + width]))
            start += width
        order += [('up', x_mlp, dy_up), ('down', h_mlp, dy_out), ('attn', x_attn, dy_attn)]
        before = None
        for name, x_block, dy_block in order:
            if before is not None:
                x_block, before = lax.optimization_barrier((x_block, before))
            before = product(x_block, dy_block)
            recvs[name].append(lax.ppermute(before, 'dp', SWAP))
            parts[name].append(before)
        results = {}
        tokens = [parts['up'][0], parts['down'][0], parts['attn'][0]]
        weights = {'gate': w_gate, 'up': w_up, 'down': w_down, 'attn': w_attn}
        stats = {'gate': (r_gate, c_gate), 'up': (r_up, c_up), 'down': (r_down, c_down), 'attn': (r_attn, c_attn)}
        for index, name in enumerate(NAMES):
            weight = weights[name]
            rows, cols = weight.shape
            grad, row_scale, col_scale, new_row, new_col = statistics(
                tokens, parts[name], recvs[name], jnp.sum(weight * weight), *stats[name], hyper_params, index)
            new_weight = weight - (grad * row_scale.reshape(rows, 1)) * col_scale
            results[name] = (new_weight, new_row.reshape(rows), new_col.reshape(cols))
            tokens = [new_weight]
        return results['attn'] + results['gate'] + results['up'] + results['down']

    return jax.shard_map(per_device, mesh=mesh, in_specs=in_specs, out_specs=out_specs, check_vma=False)
```

time: 477 us -> 377 us (0.79)
  waiting for transfers between devices: 297 us -> 226 us
  Pallas kernels: 0 us -> 42.4 us
  other arithmetic: 51.1 us -> 8.72 us
  between operations: 25 us -> 0.98 us
  blocking collectives: 19.9 us -> 0 us
  starting transfers between devices: 0.04 us -> 9.16 us
    psum x1 -> x0, waiting for transfers between devices: 297 us -> none  [matrix_step(): grad_block = lax.psum(part_grad, 'dp')]
    ppermute x0 -> x6, waiting for transfers between devices: none -> 226 us  [per_device(): recvs[name].append(lax.ppermute(before, 'dp', SWAP))]
    pallas_call x0 -> x4, Pallas kernels: none -> 42.4 us  [statistics(): pl.pallas_call(functools.partial(stats_kernel, len(tokens), widths, 16, 2...]
    reduce_sum x16 -> x4, other arithmetic: 31.4 us -> 5.9 us  [per_device(): jnp.sum(weight * weight)]
    psum x3 -> x0, blocking collectives: 19.9 us -> none  [the longest x1 8.07 us: matrix_step(): row_sum = lax.psum(jnp.sum(sq_grad, axis=1), 'col')]
    sub x3 -> x4, other arithmetic: 16.7 us -> 2.83 us  [per_device(): new_weight = weight - grad * row_scale.reshape(rows, 1) * col_scale]
    ppermute x0 -> x6, starting transfers between devices: none -> 9.16 us  [per_device(): recvs[name].append(lax.ppermute(before, 'dp', SWAP))]
    dot_general x4 -> x6, matrix products: 81.2 us -> 84.4 us  [product(): jnp.einsum('tm,tn->mn', x_block, dy_block, preferred_element_type=jnp.flo...]
  transfers between devices with their start and end apart: 1 -> 6, of which waited for: 1 -> 1; matrix products, arithmetic and copies ran while one was open for 2% -> 11% of each run, Pallas kernels for 0% -> 9%
where the time goes in v2:
time: 377 us
  waiting for transfers between devices  226 us (60%)
  matrix products  84.4 us (22%)
  Pallas kernels  42.4 us (11%)
  starting transfers between devices  9.16 us (2%)
  other arithmetic  8.72 us (2%)
  local copies, waits for them, and re-layouts  5.06 us (1%)
    ppermute x6, waiting for transfers between devices, per_device(): recvs[name].append(lax.ppermute(before, 'dp', SWAP))  226 us
    dot_general x6, matrix products, product(): jnp.einsum('tm,tn->mn', x_block, dy_block, preferred_element_type=jnp.flo...  84.4 us
    pallas_call x4, Pallas kernels, statistics(): pl.pallas_call(functools.partial(stats_kernel, len(tokens), widths, 16, 2...  42.4 us
    ppermute x6, starting transfers between devices, per_device(): recvs[name].append(lax.ppermute(before, 'dp', SWAP))  9.16 us
  transfers between devices with their start and end apart: 6, of which 1 were waited for; matrix products, arithmetic and copies ran while one was open for 11% of the time, Pallas kernels for 9%

profile of v2, /device:TPU:0, one launch (start us, length us, event | category | flops | bytes accessed | tf_op | source)
XLA Modules:
  0.0 376.6 jit_solution(12136448462742606920)
XLA Ops:
  0.7 7.1 %fusion.4.refs_7_ = f32[512,256]{1,0:T(8,128)S(1)} fusion(bf16[8192,512]{1,0:T(8,128)(2,1)} %param.22, bf16[8192,2048]{1,0:T(8,128)(2,1)} %param.23), kind=kOutput, calls=%fused_computation.10 | convolution fusion | flops 2147483648 | bytes 13107200 | tf_op jit(solution)/shard_map/tm,tn->mn/dot_general | solution.py:163
  7.8 9.4 %fusion.2.refs_8_ = f32[512,768]{1,0:T(8,128)S(1)} fusion(bf16[8192,512]{1,0:T(8,128)(2,1)S(1)} %copy-done.18, bf16[8192,2048]{1,0:T(8,128)(2,1)} %param.23), kind=kOutput, calls=%fused_computation.2 | convolution fusion | flops 6442450944 | bytes 22544384 | tf_op jit(solution)/shard_map/tm,tn->mn/dot_general | solution.py:163
  17.2 11.9 %fusion.refs_9_ = f32[512,1024]{1,0:T(8,128)S(1)} fusion(bf16[8192,512]{1,0:T(8,128)(2,1)S(1)} %copy-done.18, bf16[8192,2048]{1,0:T(8,128)(2,1)} %param.23), kind=kOutput, calls=%fused_computation | convolution fusion | flops 8589934592 | bytes 27262976 | tf_op jit(solution)/shard_map/tm,tn->mn/dot_general | solution.py:163
  29.1 21.5 %fusion.6.refs_0_.refs_5_ = f32[512,2048]{1,0:T(8,128)S(1)} fusion(bf16[8192,512]{1,0:T(8,128)(2,1)S(1)} %copy-done.18, bf16[8192,2048]{1,0:T(8,128)(2,1)} %param.24), kind=kOutput, calls=%fused_computation.14 | convolution fusion | flops 17179869184 | bytes 46137344 | tf_op jit(solution)/shard_map/tm,tn->mn/dot_general | solution.py:163
  50.7 3.3 collective-permute-start.3
  54.0 24.8 %fusion.7.refs_1_.refs_5_ = f32[2048,512]{1,0:T(8,128)S(1)} fusion(bf16[8192,2048]{1,0:T(8,128)(2,1)} %param.25, bf16[8192,512]{1,0:T(8,128)(2,1)} %param.26), kind=kOutput, calls=%fused_computation.15 | convolution fusion | flops 17179869184 | bytes 46137344 | tf_op jit(solution)/shard_map/tm,tn->mn/dot_general | solution.py:163
  78.8 0.4 collective-permute-start.4
  79.2 1.7 collective-permute-start.2
  81.2 1.7 collective-permute-start
  82.9 0.9 multiply_reduce_fusion.3
  83.8 1.7 multiply_reduce_fusion.2
  85.5 9.6 %fusion.8.refs_2_.refs_5_ = f32[512,512]{1,0:T(8,128)S(1)} fusion(bf16[8192,512]{1,0:T(8,128)(2,1)} %param.20, bf16[8192,512]{1,0:T(8,128)(2,1)} %param.21), kind=kOutput, calls=%fused_computation.16 | convolution fusion | flops 4294967296 | bytes 17825792 | tf_op jit(solution)/shard_map/tm,tn->mn/dot_general | solution.py:163
  95.2 1.7 multiply_reduce_fusion.1
  96.8 1.7 multiply_reduce_fusion
  98.5 225.9 %collective-permute-done.refs_10_ = f32[512,256]{1,0:T(8,128)S(1)} collective-permute-done((f32[512,256]{1,0:T(8,128)S(1)}, f32[512,256]{1,0:T(8,128)S(1)}, u32[]{:S(2)}, u32[]{:S(2)}) %collective-permute-start) | collective-permute-done | bytes 524320 | tf_op jit(solution)/shard_map/ppermute | solution.py:180
  324.4 1.7 collective-permute-start.5
  326.2 9.0 %shard_map.283 = (f32[512,2048]{1,0:T(8,128)S(1)}, f32[1,512]{1,0:T(1,128)S(1)}, f32[1,2048]{1,0:T(1,128)S(1)}, f32[1,512]{1,0:T(1,128)S(1)}, f32[1,2048]{1,0:T(1,128)S(1)}) custom-call(f32[512,2048]{1,0:T(8,128)S(1)} %fusion.6.refs_0_.refs_5_, f32[2048,512]{1,0:T(8,128)S(1)} %fusion.7.refs_1_.refs_5_, f32[512,512]{1,0:T(8,128)S(1)} %fusion.8.refs_2_.refs_5_, ...), custom_call_target="tpu_custom_call" | custom-call | flops 838860800 | bytes 12582912 | tf_op jit(solution)/shard_map/pallas_call | solution.py:132
  335.2 0.6 multiply_subtract_fusion.2.refs_0_
  335.8 11.1 %shard_map.284 = (f32[512,2048]{1,0:T(8,128)S(1)}, f32[1,512]{1,0:T(1,128)S(1)}, f32[1,2048]{1,0:T(1,128)S(1)}, f32[1,512]{1,0:T(1,128)S(1)}, f32[1,2048]{1,0:T(1,128)S(1)}) custom-call(f32[512,2048]{1,0:T(8,128)S(1)} %multiply_subtract_fusion.2.refs_0_, f32[3]{0:T(128)S(1)} %copy-done.6, f32[1,1]{1,0:T(1,128)} %bitcast.5.refs_2_, f32[1,512]{1,0:T(1,128)S(1)} %bitcast.47, ...), custom_call_target="tpu_custom_call" | custom-call | flops 838860800 | bytes 12582912 | tf_op jit(solution)/shard_map/pallas_call | solution.py:132
  347.0 0.6 multiply_subtract_fusion.1.refs_0_
  347.7 13.5 %shard_map.285 = (f32[2048,512]{1,0:T(8,128)S(1)}, f32[1,2048]{1,0:T(1,128)S(1)}, f32[1,512]{1,0:T(1,128)S(1)}, f32[1,2048]{1,0:T(1,128)S(1)}, f32[1,512]{1,0:T(1,128)S(1)}) custom-call(f32[512,2048]{1,0:T(8,128)S(1)} %multiply_subtract_fusion.1.refs_0_, f32[3]{0:T(128)S(1)} %copy-done.6, f32[1,1]{1,0:T(1,128)} %bitcast.10.refs_2_, f32[1,2048]{1,0:T(1,128)S(1)} %bitcast.39, ...), custom_call_target="tpu_custom_call" | custom-call | flops 838860800 | bytes 12582912 | tf_op jit(solution)/shard_map/pallas_call | solution.py:132
  361.3 0.6 multiply_subtract_fusion.refs_0_
  362.0 8.7 %shard_map.286 = (f32[512,512]{1,0:T(8,128)S(1)}, f32[1,512]{1,0:T(1,128)S(1)}, f32[1,512]{1,0:T(1,128)S(1)}, f32[1,512]{1,0:T(1,128)S(1)}, f32[1,512]{1,0:T(1,128)S(1)}) custom-call(f32[2048,512]{1,0:T(8,128)S(1)} %multiply_subtract_fusion.refs_0_, f32[3]{0:T(128)S(1)} %copy-done.6, f32[1,1]{1,0:T(1,128)} %bitcast.15.refs_2_, f32[1,512]{1,0:T(1,128)S(1)} %bitcast.49, ...), custom_call_target="tpu_custom_call" | custom-call | flops 209715200 | bytes 3145728 | tf_op jit(solution)/shard_map/pallas_call | solution.py:132
  370.7 1.2 multiply_subtract_fusion.3
  371.9 0.6 copy.40
  372.5 0.6 copy.41
  373.1 0.6 copy.42
  373.7 0.6 copy.43
  374.3 0.6 copy.44
  374.8 0.6 copy.45
  375.4 0.6 copy.46
  376.0 0.6 copy.47
  (44 shorter events, 0.7 us)
Async XLA Ops:
  0.6 7.1 %copy-start.18 = (bf16[8192,512]{1,0:T(8,128)(2,1)S(1)}, bf16[8192,512]{1,0:T(8,128)(2,1)}, u32[]{:S(2)}) copy-start(bf16[8192,512]{1,0:T(8,128)(2,1)} %param.22) | copy-start | bytes 25165828
  50.7 32.2 %copy-start.16 = (f32[512,512]{1,0:T(8,128)S(1)}, f32[512,512]{1,0:T(8,128)}, u32[]{:S(2)}) copy-start(f32[512,512]{1,0:T(8,128)} %param.27) | copy-start | bytes 3145732
  50.7 33.1 %copy-start.12 = (f32[512,2048]{1,0:T(8,128)S(1)}, f32[512,2048]{1,0:T(8,128)}, u32[]{:S(2)}) copy-start(f32[512,2048]{1,0:T(8,128)} %param.28) | copy-start | bytes 12582916
  50.7 285.0 %collective-permute-start.3 = (f32[512,2048]{1,0:T(8,128)S(1)}, f32[512,2048]{1,0:T(8,128)}, u32[]{:S(2)}, u32[]{:S(2)}) collective-permute-start(f32[512,2048]{1,0:T(8,128)S(1)} %fusion.6.refs_0_.refs_5_), channel_id=1, source_target_pairs={{0,4},{4,0},{1,5},{5,1},{2,6},{6,2},{3,7},{7,3}} | collective-permute-start | bytes 12582920 | tf_op jit(solution)/shard_map/ppermute | solution.py:180
  78.8 268.8 %collective-permute-start.4 = (f32[2048,512]{1,0:T(8,128)S(1)}, f32[2048,512]{1,0:T(8,128)}, u32[]{:S(2)}, u32[]{:S(2)}) collective-permute-start(f32[2048,512]{1,0:T(8,128)S(1)} %fusion.7.refs_1_.refs_5_), channel_id=1, source_target_pairs={{0,4},{4,0},{1,5},{5,1},{2,6},{6,2},{3,7},{7,3}} | collective-permute-start | bytes 12582920 | tf_op jit(solution)/shard_map/ppermute | solution.py:180
  79.2 246.9 %collective-permute-start.2 = (f32[512,1024]{1,0:T(8,128)S(1)}, f32[512,1024]{1,0:T(8,128)S(1)}, u32[]{:S(2)}, u32[]{:S(2)}) collective-permute-start(f32[512,1024]{1,0:T(8,128)S(1)} %fusion.refs_9_), channel_id=1, source_target_pairs={{0,4},{4,0},{1,5},{5,1},{2,6},{6,2},{3,7},{7,3}} | collective-permute-start | bytes 6291464 | tf_op jit(solution)/shard_map/ppermute | solution.py:180
  80.9 245.2 %collective-permute-start.1 = (f32[512,768]{1,0:T(8,128)S(1)}, f32[512,768]{1,0:T(8,128)S(1)}, u32[]{:S(2)}, u32[]{:S(2)}) collective-permute-start(f32[512,768]{1,0:T(8,128)S(1)} %fusion.2.refs_8_), channel_id=1, source_target_pairs={{0,4},{4,0},{1,5},{5,1},{2,6},{6,2},{3,7},{7,3}} | collective-permute-start | bytes 4718600 | tf_op jit(solution)/shard_map/ppermute | solution.py:180
  81.2 243.1 %collective-permute-start = (f32[512,256]{1,0:T(8,128)S(1)}, f32[512,256]{1,0:T(8,128)S(1)}, u32[]{:S(2)}, u32[]{:S(2)}) collective-permute-start(f32[512,256]{1,0:T(8,128)S(1)} %fusion.4.refs_7_), channel_id=1, source_target_pairs={{0,4},{4,0},{1,5},{5,1},{2,6},{6,2},{3,7},{7,3}} | collective-permute-start | bytes 1572872 | tf_op jit(solution)/shard_map/ppermute | solution.py:180
  85.5 9.7 %copy-start.13 = (f32[512,2048]{1,0:T(8,128)S(1)}, f32[512,2048]{1,0:T(8,128)}, u32[]{:S(2)}) copy-start(f32[512,2048]{1,0:T(8,128)} %param.29) | copy-start | bytes 12582916
  85.5 11.4 %copy-start.14 = (f32[2048,512]{1,0:T(8,128)S(1)}, f32[2048,512]{1,0:T(8,128)}, u32[]{:S(2)}) copy-start(f32[2048,512]{1,0:T(8,128)} %param.30) | copy-start | bytes 12582916
  95.1 231.0 %copy-start.3 = (f32[2048]{0:T(1024)S(1)}, f32[2048]{0:T(1024)}, u32[]{:S(2)}) copy-start(f32[2048]{0:T(1024)} %param.34) | copy-start | bytes 24580
  95.1 231.0 %copy-start.6 = (f32[3]{0:T(128)S(1)}, f32[3]{0:T(128)}, u32[]{:S(2)}) copy-start(f32[3]{0:T(128)} %refs_1_.5) | copy-start | bytes 40
  95.2 231.0 %copy-start.7 = (f32[512]{0:T(512)S(1)}, f32[512]{0:T(512)}, u32[]{:S(2)}) copy-start(f32[512]{0:T(512)} %param.33) | copy-start | bytes 6148
  324.4 37.5 %collective-permute-start.5 = (f32[512,512]{1,0:T(8,128)S(1)}, f32[512,512]{1,0:T(8,128)S(1)}, u32[]{:S(2)}, u32[]{:S(2)}) collective-permute-start(f32[512,512]{1,0:T(8,128)S(1)} %fusion.8.refs_2_.refs_5_), channel_id=1, source_target_pairs={{0,4},{4,0},{1,5},{5,1},{2,6},{6,2},{3,7},{7,3}} | collective-permute-start | bytes 3145736 | tf_op jit(solution)/shard_map/ppermute | solution.py:180
  335.1 0.7 copy-start.4
  335.1 0.7 copy-start.8
  335.7 11.3 %copy-start = (f32[512,2048]{1,0:T(8,128)}, f32[512,2048]{1,0:T(8,128)S(1)}, u32[]{:S(2)}) copy-start(f32[512,2048]{1,0:T(8,128)S(1)} %multiply_subtract_fusion.2.refs_0_) | copy-start | bytes 12582916
  347.0 0.7 copy-start.5
  347.0 0.7 copy-start.9
  347.6 13.7 %copy-start.1 = (f32[512,2048]{1,0:T(8,128)}, f32[512,2048]{1,0:T(8,128)S(1)}, u32[]{:S(2)}) copy-start(f32[512,2048]{1,0:T(8,128)S(1)} %multiply_subtract_fusion.1.refs_0_) | copy-start | bytes 12582916
  347.7 13.6 %copy-start.15 = (f32[2048,512]{1,0:T(8,128)S(1)}, f32[2048,512]{1,0:T(8,128)}, u32[]{:S(2)}) copy-start(f32[2048,512]{1,0:T(8,128)} %param.30) | copy-start | bytes 12582916
  361.3 0.7 copy-start.10
  361.3 0.7 copy-start.11
  361.9 10.1 %copy-start.2 = (f32[2048,512]{1,0:T(8,128)}, f32[2048,512]{1,0:T(8,128)S(1)}, u32[]{:S(2)}) copy-start(f32[2048,512]{1,0:T(8,128)S(1)} %multiply_subtract_fusion.refs_0_) | copy-start | bytes 12582916
  361.9 8.9 %copy-start.17 = (f32[512,512]{1,0:T(8,128)S(1)}, f32[512,512]{1,0:T(8,128)}, u32[]{:S(2)}) copy-start(f32[512,512]{1,0:T(8,128)} %param.27) | copy-start | bytes 3145732

commit v3 on v2

--- a/solution.py
+++ b/solution.py
@@ -12,7 +12,8 @@
 MESH = pl.DeviceIdType.MESH
 LANES = 128
 NAMES = ('gate', 'up', 'down', 'attn')
-GATE_WIDTHS = (256, 768, 1024)
+GATE_BOXES = ((0, 0, 256, 256), (256, 0, 256, 256), (0, 256, 512, 256), (0, 512, 512, 512), (0, 1024, 512, 1024))
+N_HEAD = 3
 
 
 def peers():
@@ -21,15 +22,16 @@
     return ({'row': row_other}, {'col': col_other}, {'row': row_other, 'col': col_other})
 
 
-def stats_kernel(n_token, widths, step, m_total, n_total, *refs):
-    n_piece = len(widths)
+def stats_kernel(n_token, boxes, step, m_total, n_total, *refs):
+    n_piece = len(boxes)
     refs = refs[n_token:]
     hyper, w_sq, row_old, col_old = refs[:4]
     parts = refs[4:4 + n_piece]
     recvs = refs[4 + n_piece:4 + 2 * n_piece]
     (grad, row_scale, col_scale, new_row, new_col,
      row_acc, row_col, send_row, send_col, recv_row, recv_col, send_val, recv_val,
-     vec_send, vec_recv, val_send, val_recv) = refs[4 + 2 * n_piece:]
+     vec_send, vec_recv, val_send, val_recv) = refs[4 + 2 * n_piece:4 + 2 * n_piece + 17]
+    staged = refs[4 + 2 * n_piece + 17:]
     rows, cols = grad.shape
     others = peers()
     row_peer, col_peer, _ = others
@@ -38,27 +40,32 @@
     for other in others:
         pl.semaphore_signal(barrier, inc=1, device_id=other, device_id_type=MESH)
 
+    part, recv = parts[0], recvs[0]
+    if staged:
+        part, recv, load = staged
+        loads = []
+        for k, (top, left) in enumerate(boxes):
+            box = (pl.ds(top, parts[k].shape[0]), pl.ds(left, parts[k].shape[1]))
+            loads.append(pltpu.make_async_copy(parts[k], part.at[box], load.at[2 * k]))
+            loads.append(pltpu.make_async_copy(recvs[k], recv.at[box], load.at[2 * k + 1]))
+        for copy in loads:
+            copy.start()
+        for copy in loads:
+            copy.wait()
+
     def first(i, col_acc):
         band = pl.ds(pl.multiple_of(i * step, step), step)
-        lane_sum = jnp.zeros((step, LANES), jnp.float32)
-        sums = []
-        start = 0
-        for part, recv, width in zip(parts, recvs, widths):
-            piece = part[band, :] + recv[band, :]
-            grad[band, start:start + width] = piece
-            sq = piece * piece + EPS_ONE
-            for k in range(width // LANES):
-                lane_sum = lane_sum + sq[:, k * LANES:(k + 1) * LANES]
-            sums.append(sq.reshape(step // 8, 8, width).sum(axis=0))
-            start += width
+        piece = part[band, :] + recv[band, :]
+        grad[band, :] = piece
+        sq = piece * piece + EPS_ONE
+        lane_sum = sq[:, :LANES]
+        for j in range(1, cols // LANES):
+            lane_sum = lane_sum + sq[:, j * LANES:(j + 1) * LANES]
         row_acc[band, :] = lane_sum
-        return tuple(a + s for a, s in zip(col_acc, sums))
-
-    col_acc = lax.fori_loop(0, rows // step, first, tuple(jnp.zeros((8, w), jnp.float32) for w in widths))
-    start = 0
-    for acc, width in zip(col_acc, widths):
-        send_col[:, start:start + width] = jnp.sum(acc, axis=0, keepdims=True)
-        start += width
+        return col_acc + sq.reshape(step // 8, 8, cols).sum(axis=0)
+
+    col_acc = lax.fori_loop(0, rows // step, first, jnp.zeros((8, cols), jnp.float32))
+    send_col[...] = jnp.sum(col_acc, axis=0, keepdims=True)
     for k in range(rows // LANES):
         tile = row_acc[k * LANES:(k + 1) * LANES, :].T
         send_row[:, k * LANES:(k + 1) * LANES] = jnp.sum(tile, axis=0, keepdims=True)
@@ -120,19 +127,105 @@
     row_scale[...] = row_inv * factor
 
 
-def statistics(tokens, parts, recvs, w_sq, row_old, col_old, hyper, index):
-    rows = parts[0].shape[0]
-    widths = tuple(p.shape[1] for p in parts)
-    cols = sum(widths)
+def head_kernel(row_start, col_start, x_ref, dy_ref, out, x_buf, dy_buf, x_sem, dy_sem):
+    n_step = x_sem.shape[0]
+    depth = x_buf.shape[0] // n_step
+    rows, cols = out.shape
+    copies = []
+    for k in range(n_step):
+        band = pl.ds(k * depth, depth)
+        copies.append((
+            pltpu.make_async_copy(x_ref.at[band, pl.ds(row_start, rows)], x_buf.at[band, :], x_sem.at[k]),
+            pltpu.make_async_copy(dy_ref.at[band, pl.ds(col_start, cols)], dy_buf.at[band, :], dy_sem.at[k])))
+        copies[-1][0].start()
+        copies[-1][1].start()
+    for k in range(n_step):
+        band = pl.ds(k * depth, depth)
+        copies[k][0].wait()
+        copies[k][1].wait()
+        term = lax.dot_general(x_buf[band, :], dy_buf[band, :], (((0,), (0,)), ((), ())),
+                               preferred_element_type=jnp.float32)
+        if k == 0:
+            out[...] = term
+        else:
+            out[...] += term
+
+
+def head_product(x_block, dy_block, row_start, rows, col_start, cols):
+    tokens = x_block.shape[0]
+    anyw = pl.BlockSpec(memory_space=pl.ANY)
+    return pl.pallas_call(
+        functools.partial(head_kernel, row_start, col_start),
+        out_shape=jax.ShapeDtypeStruct((rows, cols), jnp.float32),
+        in_specs=[anyw, anyw],
+        out_specs=pl.BlockSpec(memory_space=pltpu.VMEM),
+        scratch_shapes=[pltpu.VMEM((tokens, rows), x_block.dtype), pltpu.VMEM((tokens, cols), dy_block.dtype),
+                        pltpu.SemaphoreType.DMA((8,)), pltpu.SemaphoreType.DMA((8,))],
+        compiler_params=pltpu.CompilerParams(vmem_limit_bytes=58 * 1024 * 1024),
+        cost_estimate=pl.CostEstimate(flops=2 * tokens * rows * cols, bytes_accessed=2 * tokens * (rows + cols),
+                                      transcendentals=0),
+        name="head_product",
+    )(x_block, dy_block)
+
+
+def emit_kernel(*refs):
+    half = len(refs) // 2
+    for src, dst in zip(refs[:half], refs[half:]):
+        dst[...] = src[...]
+
+
+def emit(values):
+    vmem = pl.BlockSpec(memory_space=pltpu.VMEM)
+    return pl.pallas_call(
+        emit_kernel,
+        out_shape=[jax.ShapeDtypeStruct(v.shape, v.dtype) for v in values],
+        in_specs=[vmem] * len(values), out_specs=[vmem] * len(values),
+        cost_estimate=pl.CostEstimate(flops=100000, bytes_accessed=8 * sum(v.size for v in values), transcendentals=0),
+        compiler_params=pltpu.CompilerParams(vmem_limit_bytes=1024 * 1024),
+        name="emit",
+    )(*values)
+
+
+def finish_kernel(weight, grad, row_scale, col_scale, row_in, col_in, new_weight, new_row, new_col):
+    rows = weight.shape[0]
+    new_row[...] = row_in[...]
+    new_col[...] = col_in[...]
+    for k in range(rows // LANES):
+        band = pl.ds(k * LANES, LANES)
+        scale = jnp.broadcast_to(row_scale[:, k * LANES:(k + 1) * LANES], (LANES, LANES)).T
+        for j in range(weight.shape[1] // LANES):
+            lanes = pl.ds(j * LANES, LANES)
+            new_weight[band, lanes] = weight[band, lanes] - grad[band, lanes] * scale * col_scale[:, lanes]
+
+
+def finish(weight, grad, row_scale, col_scale, new_row, new_col):
+    vmem = pl.BlockSpec(memory_space=pltpu.VMEM)
+    return pl.pallas_call(
+        finish_kernel,
+        out_shape=[jax.ShapeDtypeStruct(v.shape, v.dtype) for v in (weight, new_row, new_col)],
+        in_specs=[vmem] * 6, out_specs=[vmem] * 3,
+        cost_estimate=pl.CostEstimate(flops=100000, bytes_accessed=12 * weight.size, transcendentals=0),
+        compiler_params=pltpu.CompilerParams(vmem_limit_bytes=6 * 1024 * 1024),
+        name="finish",
+    )(weight, grad, row_scale, col_scale, new_row, new_col)
+
+
+def statistics(tokens, boxes, parts, recvs, w_sq, row_old, col_old, hyper, index):
+    rows, cols = row_old.shape[0], col_old.shape[0]
     n_piece = len(parts)
     vmem = pl.BlockSpec(memory_space=pltpu.VMEM)
     smem = pl.BlockSpec(memory_space=pltpu.SMEM)
     anyw = pl.BlockSpec(memory_space=pl.ANY)
     f32 = jnp.float32
-    return pl.pallas_call(
-        functools.partial(stats_kernel, len(tokens), widths, 16, 2 * rows, 2 * cols),
+    staged = rows * cols > 500000
+    place = pl.BlockSpec(memory_space=pltpu.HBM) if staged else vmem
+    stage = [pltpu.VMEM((rows, cols), f32)] * 2 + [pltpu.SemaphoreType.DMA((2 * n_piece,))] if staged else []
+    space = pltpu.HBM if staged else pltpu.VMEM
+    parts, recvs = ([pltpu.with_memory_space_constraint(v, space) for v in group] for group in (parts, recvs))
+    return pl.pallas_call(
+        functools.partial(stats_kernel, len(tokens), boxes, 16, 2 * rows, 2 * cols),
         out_shape=[jax.ShapeDtypeStruct(s, f32) for s in ((rows, cols), (1, rows), (1, cols), (1, rows), (1, cols))],
-        in_specs=[anyw] * len(tokens) + [smem] * 2 + [vmem] * (2 + 2 * n_piece),
+        in_specs=[anyw] * len(tokens) + [smem] * 2 + [vmem] * 2 + [place] * (2 * n_piece),
         out_specs=[vmem] * 5,
         scratch_shapes=[
             pltpu.VMEM((rows, LANES), f32), pltpu.VMEM((rows, LANES), f32),
@@ -141,9 +234,9 @@
             pltpu.VMEM((8, LANES), f32), pltpu.VMEM((3, 8, LANES), f32),
             pltpu.SemaphoreType.DMA((2,)), pltpu.SemaphoreType.DMA((2,)),
             pltpu.SemaphoreType.DMA((3,)), pltpu.SemaphoreType.DMA((3,)),
-        ],
+        ] + stage,
         compiler_params=pltpu.CompilerParams(collective_id=index, has_side_effects=True,
-                                             vmem_limit_bytes=32 * 1024 * 1024),
+                                             vmem_limit_bytes=16 * 1024 * 1024 if staged else 6 * 1024 * 1024),
         cost_estimate=pl.CostEstimate(flops=8 * rows * cols * 100, bytes_accessed=12 * rows * cols, transcendentals=0),
     )(*tokens, hyper, w_sq.reshape(1, 1), row_old.reshape(1, rows), col_old.reshape(1, cols), *parts, *recvs)
 
@@ -164,19 +257,20 @@
 
     def per_device(x_attn, dy_attn, x_mlp, dy_gate, dy_up, h_mlp, dy_out, w_attn, w_gate, w_up, w_down,
                    r_attn, c_attn, r_gate, c_gate, r_up, c_up, r_down, c_down, hyper_params):
-        order = []
+        order = [('gate', x_mlp, dy_gate, box) for box in GATE_BOXES]
+        order += [('up', x_mlp, dy_up, None), ('down', h_mlp, dy_out, None), ('attn', x_attn, dy_attn, None)]
         parts = {name: [] for name in NAMES}
         recvs = {name: [] for name in NAMES}
-        start = 0
-        for width in GATE_WIDTHS:
-            order.append(('gate', x_mlp, dy_gate[:, start:start + width]))
-            start += width
-        order += [('up', x_mlp, dy_up), ('down', h_mlp, dy_out), ('attn', x_attn, dy_attn)]
         before = None
-        for name, x_block, dy_block in order:
+        for number, (name, x_block, dy_block, box) in enumerate(order):
             if before is not None:
                 x_block, before = lax.optimization_barrier((x_block, before))
-            before = product(x_block, dy_block)
+            if number < N_HEAD:
+                before = head_product(x_block, dy_block, box[0], box[2], box[1], box[3])
+            elif box is not None:
+                before = product(x_block, dy_block[:, box[1]:box[1] + box[3]])
+            else:
+                before = product(x_block, dy_block)
             recvs[name].append(lax.ppermute(before, 'dp', SWAP))
             parts[name].append(before)
         results = {}
@@ -187,10 +281,14 @@
             weight = weights[name]
             rows, cols = weight.shape
             grad, row_scale, col_scale, new_row, new_col = statistics(
-                tokens, parts[name], recvs[name], jnp.sum(weight * weight), *stats[name], hyper_params, index)
-            new_weight = weight - (grad * row_scale.reshape(rows, 1)) * col_scale
+                tokens, tuple(b[:2] for b in GATE_BOXES) if name == 'gate' else ((0, 0),), parts[name], recvs[name], jnp.sum(weight * weight), *stats[name], hyper_params, index)
+            if index < 3:
+                new_weight = weight - (grad * row_scale.reshape(rows, 1)) * col_scale
+                new_row, new_col = emit((new_row, new_col))
+            else:
+                new_weight, new_row, new_col = finish(weight, grad, row_scale, col_scale, new_row, new_col)
             results[name] = (new_weight, new_row.reshape(rows), new_col.reshape(cols))
-            tokens = [new_weight]
+            tokens = [new_weight, new_row, new_col]
         return results['attn'] + results['gate'] + results['up'] + results['down']
 
     return jax.shard_map(per_device, mesh=mesh, in_specs=in_specs, out_specs=out_specs, check_vma=False)

time: 377 us -> 399 us (1.058)
  Pallas kernels: 42.4 us -> 66.9 us
    pallas_call x4 -> x11, Pallas kernels: 42.4 us -> 66.9 us  [the longest x4 46.8 us: statistics(): pl.pallas_call(functools.partial(stats_kernel, len(tokens), boxes, 16, 2...]
    dot_general x6 -> x5, matrix products: 84.4 us -> 81.4 us  [product(): jnp.einsum('tm,tn->mn', x_block, dy_block, preferred_element_type=jnp.flo...]
    ppermute x6 -> x8, starting transfers between devices: 9.16 us -> 12 us  [per_device(): recvs[name].append(lax.ppermute(before, 'dp', SWAP))]
    ppermute x6 -> x8, waiting for transfers between devices: 226 us -> 227 us  [per_device(): recvs[name].append(lax.ppermute(before, 'dp', SWAP))]
  transfers between devices with their start and end apart: 6 -> 8, of which waited for: 1 -> 3; matrix products, arithmetic and copies ran while one was open for 11% -> 10% of each run, Pallas kernels for 9% -> 10%
where the time goes in v3:
time: 399 us
  waiting for transfers between devices  227 us (57%)
  matrix products  81.4 us (20%)
  Pallas kernels  66.9 us (17%)
  starting transfers between devices  12 us (3%)
  other arithmetic  7.63 us (2%)
    ppermute x8, waiting for transfers between devices, per_device(): recvs[name].append(lax.ppermute(before, 'dp', SWAP))  227 us
    dot_general x5, matrix products, product(): jnp.einsum('tm,tn->mn', x_block, dy_block, preferred_element_type=jnp.flo...  81.4 us
    pallas_call x4, Pallas kernels, statistics(): pl.pallas_call(functools.partial(stats_kernel, len(tokens), boxes, 16, 2...  46.8 us
    pallas_call x3, Pallas kernels, head_product(): pl.pallas_call(functools.partial(head_kernel, row_start, col_start), out_...  17.1 us
    ppermute x8, starting transfers between devices, per_device(): recvs[name].append(lax.ppermute(before, 'dp', SWAP))  12 us
  transfers between devices with their start and end apart: 8, of which 3 were waited for; matrix products, arithmetic and copies ran while one was open for 10% of the time, Pallas kernels for 10%

profile of v3, /device:TPU:0, one launch (start us, length us, event | category | flops | bytes accessed | tf_op | source)
XLA Modules:
  0.0 399.0 jit_solution(6046598424918530710)
XLA Ops:
  0.6 4.9 %head_product.3.refs_7_ = f32[256,256]{1,0:T(8,128)} custom-call(bf16[8192,512]{1,0:T(8,128)(2,1)} %x_ref.3, bf16[8192,2048]{1,0:T(8,128)(2,1)} %dy_ref.5), custom_call_target="tpu_custom_call" | custom-call | flops 1073741824 | bytes 8388608 | tf_op jit(solution)/shard_map/head_product/pallas_call | solution.py:157
  5.6 4.9 %head_product.4.refs_8_ = f32[256,256]{1,0:T(8,128)} custom-call(bf16[8192,512]{1,0:T(8,128)(2,1)} %x_ref.3, bf16[8192,2048]{1,0:T(8,128)(2,1)} %dy_ref.5), custom_call_target="tpu_custom_call" | custom-call | flops 1073741824 | bytes 8388608 | tf_op jit(solution)/shard_map/head_product/pallas_call | solution.py:157
  10.5 7.3 %head_product.5.refs_9_ = f32[512,256]{1,0:T(8,128)} custom-call(bf16[8192,512]{1,0:T(8,128)(2,1)} %x_ref.3, bf16[8192,2048]{1,0:T(8,128)(2,1)} %dy_ref.5), custom_call_target="tpu_custom_call" | custom-call | flops 2147483648 | bytes 12582912 | tf_op jit(solution)/shard_map/head_product/pallas_call | solution.py:157
  17.8 10.6 %fusion.2.refs_10_ = f32[512,512]{1,0:T(8,128)S(1)} fusion(bf16[8192,512]{1,0:T(8,128)(2,1)} %x_ref.3, bf16[8192,2048]{1,0:T(8,128)(2,1)} %dy_ref.5), kind=kOutput, calls=%fused_computation.2 | convolution fusion | flops 4294967296 | bytes 17825792 | tf_op jit(solution)/shard_map/tm,tn->mn/dot_general | solution.py:256
  28.4 16.2 %fusion.refs_11_ = f32[512,1024]{1,0:T(8,128)} fusion(bf16[8192,512]{1,0:T(8,128)(2,1)} %x_ref.3, bf16[8192,2048]{1,0:T(8,128)(2,1)} %dy_ref.5), kind=kOutput, calls=%fused_computation | convolution fusion | flops 8589934592 | bytes 27262976 | tf_op jit(solution)/shard_map/tm,tn->mn/dot_general | solution.py:256
  44.6 21.5 %fusion.4.refs_0_.refs_7_ = f32[512,2048]{1,0:T(8,128)S(1)} fusion(bf16[8192,512]{1,0:T(8,128)(2,1)S(1)} %bitcast.55, bf16[8192,2048]{1,0:T(8,128)(2,1)} %param.24), kind=kOutput, calls=%fused_computation.11 | convolution fusion | flops 17179869184 | bytes 46137344 | tf_op jit(solution)/shard_map/tm,tn->mn/dot_general | solution.py:256
  66.1 3.4 collective-permute-start.5
  69.5 23.6 %fusion.5.refs_1_.refs_7_ = f32[2048,512]{1,0:T(8,128)S(1)} fusion(bf16[8192,2048]{1,0:T(8,128)(2,1)} %param.25, bf16[8192,512]{1,0:T(8,128)(2,1)} %param.26), kind=kOutput, calls=%fused_computation.12 | convolution fusion | flops 17179869184 | bytes 46137344 | tf_op jit(solution)/shard_map/tm,tn->mn/dot_general | solution.py:256
  93.2 1.6 collective-permute-start.6
  95.2 1.6 collective-permute-start.3
  97.3 9.5 %fusion.6.refs_2_.refs_7_ = f32[512,512]{1,0:T(8,128)S(1)} fusion(bf16[8192,512]{1,0:T(8,128)(2,1)} %param.20, bf16[8192,512]{1,0:T(8,128)(2,1)} %param.21), kind=kOutput, calls=%fused_computation.13 | convolution fusion | flops 4294967296 | bytes 17825792 | tf_op jit(solution)/shard_map/tm,tn->mn/dot_general | solution.py:256
  106.8 0.9 multiply_reduce_fusion.3
  107.7 215.3 %collective-permute-done.1.refs_13_ = f32[256,256]{1,0:T(8,128)S(1)} collective-permute-done((f32[256,256]{1,0:T(8,128)S(1)}, f32[256,256]{1,0:T(8,128)S(1)}, u32[]{:S(2)}, u32[]{:S(2)}) %collective-permute-start.1) | collective-permute-done | bytes 262176 | tf_op jit(solution)/shard_map/ppermute | solution.py:274
  323.0 1.7 collective-permute-start
  324.7 1.7 multiply_reduce_fusion.2
  326.4 4.0 %collective-permute-done.refs_12_ = f32[256,256]{1,0:T(8,128)S(1)} collective-permute-done((f32[256,256]{1,0:T(8,128)S(1)}, f32[256,256]{1,0:T(8,128)S(1)}, u32[]{:S(2)}, u32[]{:S(2)}) %collective-permute-start) | collective-permute-done | bytes 262176 | tf_op jit(solution)/shard_map/ppermute | solution.py:274
  330.4 1.5 collective-permute-start.2
  331.9 1.7 multiply_reduce_fusion.1
  333.6 1.7 multiply_reduce_fusion
  335.3 7.4 %collective-permute-done.2.refs_14_ = f32[512,256]{1,0:T(8,128)S(1)} collective-permute-done((f32[512,256]{1,0:T(8,128)S(1)}, f32[512,256]{1,0:T(8,128)S(1)}, u32[]{:S(2)}, u32[]{:S(2)}) %collective-permute-start.2) | collective-permute-done | bytes 524320 | tf_op jit(solution)/shard_map/ppermute | solution.py:274
  342.6 1.3 collective-permute-start.7
  344.0 0.9 copy-done.30
  345.0 0.7 copy-done.25
  345.6 12.2 %shard_map.283 = (f32[512,2048]{1,0:T(8,128)S(1)}, f32[1,512]{1,0:T(1,128)S(1)}, f32[1,2048]{1,0:T(1,128)S(1)}, f32[1,512]{1,0:T(1,128)S(1)}, f32[1,2048]{1,0:T(1,128)S(1)}) custom-call(f32[512,2048]{1,0:T(8,128)S(1)} %fusion.4.refs_0_.refs_7_, f32[2048,512]{1,0:T(8,128)S(1)} %fusion.5.refs_1_.refs_7_, f32[512,512]{1,0:T(8,128)S(1)} %fusion.6.refs_2_.refs_7_, ...), custom_call_target="tpu_custom_call" | custom-call | flops 838860800 | bytes 12582912 | tf_op jit(solution)/shard_map/pallas_call | solution.py:225
  359.2 12.2 %shard_map.284 = (f32[512,2048]{1,0:T(8,128)S(1)}, f32[1,512]{1,0:T(1,128)S(1)}, f32[1,2048]{1,0:T(1,128)S(1)}, f32[1,512]{1,0:T(1,128)S(1)}, f32[1,2048]{1,0:T(1,128)S(1)}) custom-call(f32[512,2048]{1,0:T(8,128)S(1)} %multiply_subtract_fusion.2.refs_0_, f32[1,512]{1,0:T(1,128)S(1)} %copy-done.18, f32[1,2048]{1,0:T(1,128)S(1)} %copy-done.9, ...), custom_call_target="tpu_custom_call" | custom-call | flops 838860800 | bytes 12582912 | tf_op jit(solution)/shard_map/pallas_call | solution.py:225
  372.0 0.6 emit.4
  372.6 0.7 copy-done.10
  373.4 0.7 copy-done.19
  374.1 13.8 %shard_map.285 = (f32[2048,512]{1,0:T(8,128)S(1)}, f32[1,2048]{1,0:T(1,128)S(1)}, f32[1,512]{1,0:T(1,128)S(1)}, f32[1,2048]{1,0:T(1,128)S(1)}, f32[1,512]{1,0:T(1,128)S(1)}) custom-call(f32[512,2048]{1,0:T(8,128)S(1)} %multiply_subtract_fusion.1.refs_0_, f32[1,512]{1,0:T(1,128)S(1)} %copy-done.19, f32[1,2048]{1,0:T(1,128)S(1)} %copy-done.10, ...), custom_call_target="tpu_custom_call" | custom-call | flops 838860800 | bytes 12582912 | tf_op jit(solution)/shard_map/pallas_call | solution.py:225
  388.5 0.6 multiply_subtract_fusion.refs_0_
  389.2 8.6 %shard_map.286 = (f32[512,512]{1,0:T(8,128)S(1)}, f32[1,512]{1,0:T(1,128)S(1)}, f32[1,512]{1,0:T(1,128)S(1)}, f32[1,512]{1,0:T(1,128)S(1)}, f32[1,512]{1,0:T(1,128)S(1)}) custom-call(f32[2048,512]{1,0:T(8,128)S(1)} %multiply_subtract_fusion.refs_0_, f32[1,2048]{1,0:T(1,128)S(1)} %copy-done.11, f32[1,512]{1,0:T(1,128)S(1)} %copy-done.20, f32[3]{0:T(128)S(1)} %copy-done.12, ...), custom_call_target="tpu_custom_call" | custom-call | flops 209715200 | bytes 3145728 | tf_op jit(solution)/shard_map/pallas_call | solution.py:225
  397.9 1.2 finish.1
  (80 shorter events, 3.6 us)
Async XLA Ops:
  17.8 26.9 %slice-start = ((s8[8388608]{0:T(1024)(128)(4,1)}), s8[4194304]{0:T(1024)(128)(4,1)S(1)}, s32[]{:S(2)}) async-start(s8[8388608]{0:T(1024)(128)(4,1)} %bitcast.54), calls=%async_computation | async-start | bytes 8388608
  28.4 66.8 %copy-start.29 = (f32[512,512]{1,0:T(8,128)}, f32[512,512]{1,0:T(8,128)S(1)}, u32[]{:S(2)}) copy-start(f32[512,512]{1,0:T(8,128)S(1)} %fusion.2.refs_10_) | copy-start | bytes 3145732
  28.4 16.2 %slice-start.1 = ((s8[8388608]{0:T(1024)(128)(4,1)}), s8[4194304]{0:T(1024)(128)(4,1)S(1)}, s32[]{:S(2)}) async-start(s8[8388608]{0:T(1024)(128)(4,1)} %bitcast.54), calls=%async_computation.1 | async-start | bytes 8388608
  66.1 277.9 %copy-start.2 = (f32[512,2048]{1,0:T(8,128)}, f32[512,2048]{1,0:T(8,128)S(1)}, u32[]{:S(2)}) copy-start(f32[512,2048]{1,0:T(8,128)S(1)} %fusion.4.refs_0_.refs_7_) | copy-start | bytes 12582916
  66.1 30.7 %copy-start.28 = (f32[256,256]{1,0:T(8,128)S(1)}, f32[256,256]{1,0:T(8,128)}, u32[]{:S(2)}) copy-start(f32[256,256]{1,0:T(8,128)} %head_product.4.refs_8_) | copy-start | bytes 786436
  66.1 292.9 %collective-permute-start.5 = (f32[512,2048]{1,0:T(8,128)S(1)}, f32[512,2048]{1,0:T(8,128)}, u32[]{:S(2)}, u32[]{:S(2)}) collective-permute-start(f32[512,2048]{1,0:T(8,128)S(1)} %fusion.4.refs_0_.refs_7_), channel_id=1, source_target_pairs={{0,4},{4,0},{1,5},{5,1},{2,6},{6,2},{3,7},{7,3}} | collective-permute-start | bytes 12582920 | tf_op jit(solution)/shard_map/ppermute | solution.py:274
  93.1 250.9 %copy-start = (f32[2048,512]{1,0:T(8,128)}, f32[2048,512]{1,0:T(8,128)S(1)}, u32[]{:S(2)}) copy-start(f32[2048,512]{1,0:T(8,128)S(1)} %fusion.5.refs_1_.refs_7_) | copy-start | bytes 12582916
  93.2 13.6 %copy-start.5 = (f32[512,512]{1,0:T(8,128)S(1)}, f32[512,512]{1,0:T(8,128)}, u32[]{:S(2)}) copy-start(f32[512,512]{1,0:T(8,128)} %weight.1) | copy-start | bytes 3145732
  93.2 229.8 %copy-start.27 = (f32[256,256]{1,0:T(8,128)S(1)}, f32[256,256]{1,0:T(8,128)}, u32[]{:S(2)}) copy-start(f32[256,256]{1,0:T(8,128)} %head_product.3.refs_7_) | copy-start | bytes 786436
  93.2 231.5 %copy-start.21 = (f32[512,2048]{1,0:T(8,128)S(1)}, f32[512,2048]{1,0:T(8,128)}, u32[]{:S(2)}) copy-start(f32[512,2048]{1,0:T(8,128)} %param.28) | copy-start | bytes 12582916
  93.2 279.4 %collective-permute-start.6 = (f32[2048,512]{1,0:T(8,128)S(1)}, f32[2048,512]{1,0:T(8,128)}, u32[]{:S(2)}, u32[]{:S(2)}) collective-permute-start(f32[2048,512]{1,0:T(8,128)S(1)} %fusion.5.refs_1_.refs_7_), channel_id=1, source_target_pairs={{0,4},{4,0},{1,5},{5,1},{2,6},{6,2},{3,7},{7,3}} | collective-permute-start | bytes 12582920 | tf_op jit(solution)/shard_map/ppermute | solution.py:274
  94.8 249.2 %collective-permute-start.4 = (f32[512,1024]{1,0:T(8,128)}, f32[512,1024]{1,0:T(8,128)S(1)}, u32[]{:S(2)}, u32[]{:S(2)}) collective-permute-start(f32[512,1024]{1,0:T(8,128)} %fusion.refs_11_), channel_id=1, source_target_pairs={{0,4},{4,0},{1,5},{5,1},{2,6},{6,2},{3,7},{7,3}} | collective-permute-start | bytes 6291464 | tf_op jit(solution)/shard_map/ppermute | solution.py:274
  95.2 248.7 %collective-permute-start.3 = (f32[512,512]{1,0:T(8,128)S(1)}, f32[512,512]{1,0:T(8,128)S(1)}, u32[]{:S(2)}, u32[]{:S(2)}) collective-permute-start(f32[512,512]{1,0:T(8,128)S(1)} %fusion.2.refs_10_), channel_id=1, source_target_pairs={{0,4},{4,0},{1,5},{5,1},{2,6},{6,2},{3,7},{7,3}} | collective-permute-start | bytes 3145736 | tf_op jit(solution)/shard_map/ppermute | solution.py:274
  96.8 226.2 %collective-permute-start.1 = (f32[256,256]{1,0:T(8,128)S(1)}, f32[256,256]{1,0:T(8,128)S(1)}, u32[]{:S(2)}, u32[]{:S(2)}) collective-permute-start(f32[256,256]{1,0:T(8,128)S(1)} %copy-done.28), channel_id=1, source_target_pairs={{0,4},{4,0},{1,5},{5,1},{2,6},{6,2},{3,7},{7,3}} | collective-permute-start | bytes 786440 | tf_op jit(solution)/shard_map/ppermute | solution.py:274
  106.8 223.6 %copy-start.26 = (f32[512,256]{1,0:T(8,128)S(1)}, f32[512,256]{1,0:T(8,128)}, u32[]{:S(2)}) copy-start(f32[512,256]{1,0:T(8,128)} %head_product.5.refs_9_) | copy-start | bytes 1572868
  106.8 225.1 %copy-start.22 = (f32[512,2048]{1,0:T(8,128)S(1)}, f32[512,2048]{1,0:T(8,128)}, u32[]{:S(2)}) copy-start(f32[512,2048]{1,0:T(8,128)} %param.29) | copy-start | bytes 12582916
  107.7 225.9 %copy-start.23 = (f32[2048,512]{1,0:T(8,128)S(1)}, f32[2048,512]{1,0:T(8,128)}, u32[]{:S(2)}) copy-start(f32[2048,512]{1,0:T(8,128)} %param.30) | copy-start | bytes 12582916
  323.0 10.6 %copy-start.32 = (f32[256,256]{1,0:T(8,128)}, f32[256,256]{1,0:T(8,128)S(1)}, u32[]{:S(2)}) copy-start(f32[256,256]{1,0:T(8,128)S(1)} %collective-permute-done.1.refs_13_) | copy-start | bytes 786436
  323.0 7.5 %collective-permute-start = (f32[256,256]{1,0:T(8,128)S(1)}, f32[256,256]{1,0:T(8,128)S(1)}, u32[]{:S(2)}, u32[]{:S(2)}) collective-permute-start(f32[256,256]{1,0:T(8,128)S(1)} %copy-done.27), channel_id=1, source_target_pairs={{0,4},{4,0},{1,5},{5,1},{2,6},{6,2},{3,7},{7,3}} | collective-permute-start | bytes 786440 | tf_op jit(solution)/shard_map/ppermute | solution.py:274
  326.4 19.3 %copy-start.6 = (f32[2048]{0:T(1024)S(1)}, f32[2048]{0:T(1024)}, u32[]{:S(2)}) copy-start(f32[2048]{0:T(1024)} %param.34) | copy-start | bytes 24580
  326.4 19.3 %copy-start.12 = (f32[3]{0:T(128)S(1)}, f32[3]{0:T(128)}, u32[]{:S(2)}) copy-start(f32[3]{0:T(128)} %refs_3_.7) | copy-start | bytes 40
  326.4 19.3 %copy-start.13 = (f32[512]{0:T(512)S(1)}, f32[512]{0:T(512)}, u32[]{:S(2)}) copy-start(f32[512]{0:T(512)} %param.33) | copy-start | bytes 6148
  330.4 4.8 %copy-start.33 = (f32[256,256]{1,0:T(8,128)}, f32[256,256]{1,0:T(8,128)S(1)}, u32[]{:S(2)}) copy-start(f32[256,256]{1,0:T(8,128)S(1)} %collective-permute-done.refs_12_) | copy-start | bytes 786436
  330.4 12.2 %collective-permute-start.2 = (f32[512,256]{1,0:T(8,128)S(1)}, f32[512,256]{1,0:T(8,128)S(1)}, u32[]{:S(2)}, u32[]{:S(2)}) collective-permute-start(f32[512,256]{1,0:T(8,128)S(1)} %copy-done.26), channel_id=1, source_target_pairs={{0,4},{4,0},{1,5},{5,1},{2,6},{6,2},{3,7},{7,3}} | collective-permute-start | bytes 1572872 | tf_op jit(solution)/shard_map/ppermute | solution.py:274
  342.6 1.4 copy-start.31
  342.6 46.5 %collective-permute-start.7 = (f32[512,512]{1,0:T(8,128)S(1)}, f32[512,512]{1,0:T(8,128)S(1)}, u32[]{:S(2)}, u32[]{:S(2)}) collective-permute-start(f32[512,512]{1,0:T(8,128)S(1)} %fusion.6.refs_2_.refs_7_), channel_id=1, source_target_pairs={{0,4},{4,0},{1,5},{5,1},{2,6},{6,2},{3,7},{7,3}} | collective-permute-start | bytes 3145736 | tf_op jit(solution)/shard_map/ppermute | solution.py:274
  344.0 1.7 copy-start.25
  359.0 12.3 %copy-start.1 = (f32[512,2048]{1,0:T(8,128)}, f32[512,2048]{1,0:T(8,128)S(1)}, u32[]{:S(2)}) copy-start(f32[512,2048]{1,0:T(8,128)S(1)} %multiply_subtract_fusion.2.refs_0_) | copy-start | bytes 12582916
  371.4 1.2 copy-start.8
  372.0 15.9 %copy-start.3 = (f32[512,2048]{1,0:T(8,128)}, f32[512,2048]{1,0:T(8,128)S(1)}, u32[]{:S(2)}) copy-start(f32[512,2048]{1,0:T(8,128)S(1)} %multiply_subtract_fusion.1.refs_0_) | copy-start | bytes 12582916
  374.1 14.4 %copy-start.24 = (f32[2048,512]{1,0:T(8,128)S(1)}, f32[2048,512]{1,0:T(8,128)}, u32[]{:S(2)}) copy-start(f32[2048,512]{1,0:T(8,128)} %param.30) | copy-start | bytes 12582916
  389.1 9.9 %copy-start.4 = (f32[2048,512]{1,0:T(8,128)}, f32[2048,512]{1,0:T(8,128)S(1)}, u32[]{:S(2)}) copy-start(f32[2048,512]{1,0:T(8,128)S(1)} %multiply_subtract_fusion.refs_0_) | copy-start | bytes 12582916
  (12 other events, 9.3 us)

commit v4 on v3

--- a/solution.py
+++ b/solution.py
@@ -12,8 +12,9 @@
 MESH = pl.DeviceIdType.MESH
 LANES = 128
 NAMES = ('gate', 'up', 'down', 'attn')
-GATE_BOXES = ((0, 0, 256, 256), (256, 0, 256, 256), (0, 256, 512, 256), (0, 512, 512, 512), (0, 1024, 512, 1024))
+GATE_BOXES = ((0, 0, 256, 256), (256, 0, 256, 512), (0, 256, 256, 256), (0, 512, 512, 512), (0, 1024, 512, 1024))
 N_HEAD = 3
+HEAD_LIMIT = 58 * 1024 * 1024
 
 
 def peers():
@@ -22,16 +23,16 @@
     return ({'row': row_other}, {'col': col_other}, {'row': row_other, 'col': col_other})
 
 
-def stats_kernel(n_token, boxes, step, m_total, n_total, *refs):
+def stats_kernel(n_token, boxes, near, direct, step, m_total, n_total, *refs):
     n_piece = len(boxes)
     refs = refs[n_token:]
     hyper, w_sq, row_old, col_old = refs[:4]
     parts = refs[4:4 + n_piece]
     recvs = refs[4 + n_piece:4 + 2 * n_piece]
-    (grad, row_scale, col_scale, new_row, new_col,
-     row_acc, row_col, send_row, send_col, recv_row, recv_col, send_val, recv_val,
-     vec_send, vec_recv, val_send, val_recv) = refs[4 + 2 * n_piece:4 + 2 * n_piece + 17]
-    staged = refs[4 + 2 * n_piece + 17:]
+    (grad, row_scale, new_row, new_col,
+     row_acc, send_row, send_col, recv_row, recv_col, send_val, recv_val,
+     vec_send, vec_recv, val_send, val_recv) = refs[4 + 2 * n_piece:4 + 2 * n_piece + 15]
+    staged = refs[4 + 2 * n_piece + 15:]
     rows, cols = grad.shape
     others = peers()
     row_peer, col_peer, _ = others
@@ -46,10 +47,21 @@
         loads = []
         for k, (top, left) in enumerate(boxes):
             box = (pl.ds(top, parts[k].shape[0]), pl.ds(left, parts[k].shape[1]))
-            loads.append(pltpu.make_async_copy(parts[k], part.at[box], load.at[2 * k]))
             loads.append(pltpu.make_async_copy(recvs[k], recv.at[box], load.at[2 * k + 1]))
+            if k >= near:
+                loads.append(pltpu.make_async_copy(parts[k], part.at[box], load.at[2 * k]))
         for copy in loads:
             copy.start()
+        for k, (top, left) in enumerate(boxes[:near]):
+            width = parts[k].shape[1]
+
+            def place(i, carry):
+                src = pl.ds(pl.multiple_of(i * step, step), step)
+                dst = pl.ds(pl.multiple_of(top + i * step, step), step)
+                part[dst, left:left + width] = parts[k][src, :]
+                return carry
+
+            lax.fori_loop(0, parts[k].shape[0] // step, place, 0)
         for copy in loads:
             copy.wait()
 
@@ -76,55 +88,68 @@
                                             device_id=row_peer, device_id_type=MESH)
     row_copy.start()
     col_copy.start()
+    beta_two = hyper[0]
+
+    col_copy.wait()
+    col_now = beta_two * col_old[...] + (1.0 - beta_two) * ((send_col[...] + recv_col[...]) / m_total)
+    new_col[...] = col_now
+    col_inv = 1.0 / jnp.sqrt(col_now)
+
+    def second(i, carry):
+        band = pl.ds(pl.multiple_of(i * step, step), step)
+        upd = grad[band, :] * col_inv
+        grad[band, :] = upd
+        sq = upd * upd
+        lane_sum = sq[:, :LANES]
+        for j in range(1, cols // LANES):
+            lane_sum = lane_sum + sq[:, j * LANES:(j + 1) * LANES]
+        row_acc[band, :] = lane_sum
+        return carry
+
+    lax.fori_loop(0, rows // step, second, 0)
+    sums = [jnp.sum(row_acc[k * LANES:(k + 1) * LANES, :].T, axis=0, keepdims=True) for k in range(rows // LANES)]
+
     row_copy.wait()
-    col_copy.wait()
-    beta_two = hyper[0]
     row_now = beta_two * row_old[...] + (1.0 - beta_two) * ((send_row[...] + recv_row[...]) / n_total)
-    col_now = beta_two * col_old[...] + (1.0 - beta_two) * ((send_col[...] + recv_col[...]) / m_total)
     new_row[...] = row_now
-    new_col[...] = col_now
     row_inv = 1.0 / jnp.sqrt(row_now)
-    col_inv = 1.0 / jnp.sqrt(col_now)
-    col_scale[...] = col_inv
+    upd_sq = jnp.zeros((1, LANES), jnp.float32)
+    row_part = jnp.zeros((1, LANES), jnp.float32)
     for k in range(rows // LANES):
-        tile = jnp.broadcast_to(row_inv[:, k * LANES:(k + 1) * LANES], (LANES, LANES))
-        row_col[k * LANES:(k + 1) * LANES, :] = tile.T
-
-    def second(i, col_acc):
-        band = pl.ds(pl.multiple_of(i * step, step), step)
-        scale = row_col[band, :]
-        sums = []
-        for k in range(cols // LANES):
-            upd = grad[band, k * LANES:(k + 1) * LANES] * scale
-            sums.append((upd * upd).reshape(step // 8, 8, LANES).sum(axis=0))
-        return tuple(a + s for a, s in zip(col_acc, sums))
-
-    col_acc = lax.fori_loop(0, rows // step, second,
-                            tuple(jnp.zeros((8, LANES), jnp.float32) for _ in range(cols // LANES)))
-    lane_sum = jnp.zeros((8, LANES), jnp.float32)
-    col_sq = col_inv * col_inv
-    for k, acc in enumerate(col_acc):
-        lane_sum = lane_sum + acc * col_sq[:, k * LANES:(k + 1) * LANES]
-    upd_sq = jnp.sum(lane_sum)
-    row_part = jnp.sum(row_now)
+        inv = row_inv[:, k * LANES:(k + 1) * LANES]
+        upd_sq = upd_sq + sums[k] * (inv * inv)
+        row_part = row_part + row_now[:, k * LANES:(k + 1) * LANES]
     which = lax.broadcasted_iota(jnp.int32, (8, LANES), 0)
-    send_val[...] = jnp.where(which == 0, upd_sq, jnp.where(which == 1, row_part, w_sq[0, 0]))
+    lane = lax.broadcasted_iota(jnp.int32, (8, LANES), 1)
+    send_val[...] = jnp.where(which == 0, upd_sq, jnp.where(which == 1, row_part,
+                                                            jnp.where(lane == 0, w_sq[0, 0], 0.0)))
     copies = [pltpu.make_async_remote_copy(send_val, recv_val.at[k], val_send.at[k], val_recv.at[k],
                                            device_id=other, device_id_type=MESH)
               for k, other in enumerate(others)]
     for copy in copies:
         copy.start()
+    if direct:
+        for k in range(rows // LANES):
+            band = pl.ds(k * LANES, LANES)
+            scale = jnp.broadcast_to(row_inv[:, k * LANES:(k + 1) * LANES], (LANES, LANES)).T
+            for j in range(cols // LANES):
+                lanes = pl.ds(j * LANES, LANES)
+                grad[band, lanes] = grad[band, lanes] * scale
     for copy in copies:
         copy.wait()
     pair = send_val[...] + recv_val[0]
-    total = pair + (recv_val[1] + recv_val[2])
+    total = jnp.sum(pair + (recv_val[1] + recv_val[2]), axis=1, keepdims=True)
+    pair = jnp.sum(pair, axis=1, keepdims=True)
     size = m_total * n_total
-    row_total = pair[1:2, :1]
-    upd_rms = jnp.sqrt(row_total * total[0:1, :1] / size)
-    w_rms = jnp.sqrt(total[2:3, :1] / size)
+    row_total = pair[1:2, :]
+    upd_rms = jnp.sqrt(row_total * total[0:1, :] / size)
+    w_rms = jnp.sqrt(total[2:3, :] / size)
     clip = jnp.maximum(1.0, upd_rms / hyper[2])
     factor = hyper[1] * jnp.maximum(EPS_TWO, w_rms) * jnp.sqrt(row_total) / clip
-    row_scale[...] = row_inv * factor
+    if direct:
+        row_scale[...] = jnp.broadcast_to(factor, (1, LANES))
+    else:
+        row_scale[...] = row_inv * factor
 
 
 def head_kernel(row_start, col_start, x_ref, dy_ref, out, x_buf, dy_buf, x_sem, dy_sem):
@@ -161,11 +186,11 @@
         out_specs=pl.BlockSpec(memory_space=pltpu.VMEM),
         scratch_shapes=[pltpu.VMEM((tokens, rows), x_block.dtype), pltpu.VMEM((tokens, cols), dy_block.dtype),
                         pltpu.SemaphoreType.DMA((8,)), pltpu.SemaphoreType.DMA((8,))],
-        compiler_params=pltpu.CompilerParams(vmem_limit_bytes=58 * 1024 * 1024),
+        compiler_params=pltpu.CompilerParams(vmem_limit_bytes=HEAD_LIMIT if (row_start, col_start) != (0, 0) else 14 * 1024 * 1024),
         cost_estimate=pl.CostEstimate(flops=2 * tokens * rows * cols, bytes_accessed=2 * tokens * (rows + cols),
                                       transcendentals=0),
         name="head_product",
-    )(x_block, dy_block)
+    )(pltpu.with_memory_space_constraint(x_block, pltpu.HBM), pltpu.with_memory_space_constraint(dy_block, pltpu.HBM))
 
 
 def emit_kernel(*refs):
@@ -186,31 +211,28 @@
     )(*values)
 
 
-def finish_kernel(weight, grad, row_scale, col_scale, row_in, col_in, new_weight, new_row, new_col):
-    rows = weight.shape[0]
+def finish_kernel(weight, update, factor, row_in, col_in, new_weight, new_row, new_col):
     new_row[...] = row_in[...]
     new_col[...] = col_in[...]
-    for k in range(rows // LANES):
-        band = pl.ds(k * LANES, LANES)
-        scale = jnp.broadcast_to(row_scale[:, k * LANES:(k + 1) * LANES], (LANES, LANES)).T
-        for j in range(weight.shape[1] // LANES):
-            lanes = pl.ds(j * LANES, LANES)
-            new_weight[band, lanes] = weight[band, lanes] - grad[band, lanes] * scale * col_scale[:, lanes]
-
-
-def finish(weight, grad, row_scale, col_scale, new_row, new_col):
+    scale = factor[...]
+    for j in range(weight.shape[1] // LANES):
+        lanes = pl.ds(j * LANES, LANES)
+        new_weight[:, lanes] = weight[:, lanes] - update[:, lanes] * scale
+
+
+def finish(weight, update, factor, new_row, new_col):
     vmem = pl.BlockSpec(memory_space=pltpu.VMEM)
     return pl.pallas_call(
         finish_kernel,
         out_shape=[jax.ShapeDtypeStruct(v.shape, v.dtype) for v in (weight, new_row, new_col)],
-        in_specs=[vmem] * 6, out_specs=[vmem] * 3,
+        in_specs=[vmem] * 5, out_specs=[vmem] * 3,
         cost_estimate=pl.CostEstimate(flops=100000, bytes_accessed=12 * weight.size, transcendentals=0),
         compiler_params=pltpu.CompilerParams(vmem_limit_bytes=6 * 1024 * 1024),
         name="finish",
-    )(weight, grad, row_scale, col_scale, new_row, new_col)
-
-
-def statistics(tokens, boxes, parts, recvs, w_sq, row_old, col_old, hyper, index):
+    )(weight, update, factor, new_row, new_col)
+
+
+def statistics(tokens, boxes, near, parts, recvs, w_sq, row_old, col_old, hyper, index):
     rows, cols = row_old.shape[0], col_old.shape[0]
     n_piece = len(parts)
     vmem = pl.BlockSpec(memory_space=pltpu.VMEM)
@@ -218,17 +240,20 @@
     anyw = pl.BlockSpec(memory_space=pl.ANY)
     f32 = jnp.float32
     staged = rows * cols > 500000
-    place = pl.BlockSpec(memory_space=pltpu.HBM) if staged else vmem
+    near = near if staged else 1
+    spaces = [pltpu.VMEM if k < near else pltpu.HBM for k in range(n_piece)]
+    spaces += [pltpu.HBM if staged else pltpu.VMEM] * n_piece
+    places = [pl.BlockSpec(memory_space=v) for v in spaces]
     stage = [pltpu.VMEM((rows, cols), f32)] * 2 + [pltpu.SemaphoreType.DMA((2 * n_piece,))] if staged else []
-    space = pltpu.HBM if staged else pltpu.VMEM
-    parts, recvs = ([pltpu.with_memory_space_constraint(v, space) for v in group] for group in (parts, recvs))
+    halves = [pltpu.with_memory_space_constraint(v, space) for v, space in zip(parts + recvs, spaces)]
+    shapes = ((rows, cols), (1, rows if staged else LANES), (1, rows), (1, cols))
     return pl.pallas_call(
-        functools.partial(stats_kernel, len(tokens), boxes, 16, 2 * rows, 2 * cols),
-        out_shape=[jax.ShapeDtypeStruct(s, f32) for s in ((rows, cols), (1, rows), (1, cols), (1, rows), (1, cols))],
-        in_specs=[anyw] * len(tokens) + [smem] * 2 + [vmem] * 2 + [place] * (2 * n_piece),
-        out_specs=[vmem] * 5,
+        functools.partial(stats_kernel, len(tokens), boxes, near, not staged, 16, 2 * rows, 2 * cols),
+        out_shape=[jax.ShapeDtypeStruct(s, f32) for s in shapes],
+        in_specs=[anyw] * len(tokens) + [smem] * 2 + [vmem] * 2 + places,
+        out_specs=[vmem] * 4,
         scratch_shapes=[
-            pltpu.VMEM((rows, LANES), f32), pltpu.VMEM((rows, LANES), f32),
+            pltpu.VMEM((rows, LANES), f32),
             pltpu.VMEM((1, rows), f32), pltpu.VMEM((1, cols), f32),
             pltpu.VMEM((1, rows), f32), pltpu.VMEM((1, cols), f32),
             pltpu.VMEM((8, LANES), f32), pltpu.VMEM((3, 8, LANES), f32),
@@ -238,7 +263,7 @@
         compiler_params=pltpu.CompilerParams(collective_id=index, has_side_effects=True,
                                              vmem_limit_bytes=16 * 1024 * 1024 if staged else 6 * 1024 * 1024),
         cost_estimate=pl.CostEstimate(flops=8 * rows * cols * 100, bytes_accessed=12 * rows * cols, transcendentals=0),
-    )(*tokens, hyper, w_sq.reshape(1, 1), row_old.reshape(1, rows), col_old.reshape(1, cols), *parts, *recvs)
+    )(*tokens, hyper, w_sq.reshape(1, 1), row_old.reshape(1, rows), col_old.reshape(1, cols), *halves)
 
 
 def solution(mesh):
@@ -280,13 +305,15 @@
         for index, name in enumerate(NAMES):
             weight = weights[name]
             rows, cols = weight.shape
-            grad, row_scale, col_scale, new_row, new_col = statistics(
-                tokens, tuple(b[:2] for b in GATE_BOXES) if name == 'gate' else ((0, 0),), parts[name], recvs[name], jnp.sum(weight * weight), *stats[name], hyper_params, index)
+            grad, row_scale, new_row, new_col = statistics(
+                tokens, tuple(b[:2] for b in GATE_BOXES) if name == 'gate' else ((0, 0),),
+                N_HEAD if name == 'gate' else 0, parts[name], recvs[name],
+                jnp.sum(weight * weight), *stats[name], hyper_params, index)
             if index < 3:
-                new_weight = weight - (grad * row_scale.reshape(rows, 1)) * col_scale
+                new_weight = weight - grad * row_scale.reshape(rows, 1)
                 new_row, new_col = emit((new_row, new_col))
             else:
-                new_weight, new_row, new_col = finish(weight, grad, row_scale, col_scale, new_row, new_col)
+                new_weight, new_row, new_col = finish(weight, grad, row_scale, new_row, new_col)
             results[name] = (new_weight, new_row.reshape(rows), new_col.reshape(cols))
             tokens = [new_weight, new_row, new_col]
         return results['attn'] + results['gate'] + results['up'] + results['down']

time: 399 us -> 395 us (0.990)
  Pallas kernels: 66.9 us -> 62.2 us
where the time goes in v4:
time: 395 us
  waiting for transfers between devices  226 us (57%)
  matrix products  81 us (21%)
  Pallas kernels  62.2 us (16%)
  starting transfers between devices  12 us (3%)
  other arithmetic  7.34 us (2%)
  local copies, waits for them, and re-layouts  5.14 us (1%)
    ppermute x8, waiting for transfers between devices, per_device(): recvs[name].append(lax.ppermute(before, 'dp', SWAP))  226 us
    dot_general x5, matrix products, product(): jnp.einsum('tm,tn->mn', x_block, dy_block, preferred_element_type=jnp.flo...  81 us
    pallas_call x4, Pallas kernels, statistics(): pl.pallas_call(functools.partial(stats_kernel, len(tokens), boxes, near,...  44.1 us
    pallas_call x3, Pallas kernels, head_product(): pl.pallas_call(functools.partial(head_kernel, row_start, col_start), out_...  15.2 us
    ppermute x8, starting transfers between devices, per_device(): recvs[name].append(lax.ppermute(before, 'dp', SWAP))  12 us
  transfers between devices with their start and end apart: 8, of which 3 were waited for; matrix products, arithmetic and copies ran while one was open for 10% of the time, Pallas kernels for 10%

profile of v4, /device:TPU:0, one launch (start us, length us, event | category | flops | bytes accessed | tf_op | source)
XLA Modules:
  0.0 395.3 jit_solution(14757914975739553540)
XLA Ops:
  0.6 4.2 %head_product.3.refs_7_ = f32[256,256]{1,0:T(8,128)S(1)} custom-call(bf16[8192,512]{1,0:T(8,128)(2,1)} %x_ref.3, bf16[8192,2048]{1,0:T(8,128)(2,1)} %dy_ref.5), custom_call_target="tpu_custom_call" | custom-call | flops 1073741824 | bytes 8388608 | tf_op jit(solution)/shard_map/head_product/pallas_call | solution.py:182
  4.8 6.1 %head_product.4.refs_8_ = f32[256,512]{1,0:T(8,128)} custom-call(bf16[8192,512]{1,0:T(8,128)(2,1)} %x_ref.3, bf16[8192,2048]{1,0:T(8,128)(2,1)} %dy_ref.5), custom_call_target="tpu_custom_call" | custom-call | flops 2147483648 | bytes 12582912 | tf_op jit(solution)/shard_map/head_product/pallas_call | solution.py:182
  10.9 4.9 %head_product.5.refs_9_ = f32[256,256]{1,0:T(8,128)} custom-call(bf16[8192,512]{1,0:T(8,128)(2,1)} %x_ref.3, bf16[8192,2048]{1,0:T(8,128)(2,1)} %dy_ref.5), custom_call_target="tpu_custom_call" | custom-call | flops 1073741824 | bytes 8388608 | tf_op jit(solution)/shard_map/head_product/pallas_call | solution.py:182
  15.8 10.6 %fusion.2.refs_10_ = f32[512,512]{1,0:T(8,128)S(1)} fusion(bf16[8192,512]{1,0:T(8,128)(2,1)} %x_ref.3, bf16[8192,2048]{1,0:T(8,128)(2,1)} %dy_ref.5), kind=kOutput, calls=%fused_computation.2 | convolution fusion | flops 4294967296 | bytes 17825792 | tf_op jit(solution)/shard_map/tm,tn->mn/dot_general | solution.py:281
  26.5 14.8 %fusion.refs_11_ = f32[512,1024]{1,0:T(8,128)S(1)} fusion(bf16[8192,512]{1,0:T(8,128)(2,1)} %x_ref.3, bf16[8192,2048]{1,0:T(8,128)(2,1)} %dy_ref.5), kind=kOutput, calls=%fused_computation | convolution fusion | flops 8589934592 | bytes 27262976 | tf_op jit(solution)/shard_map/tm,tn->mn/dot_general | solution.py:281
  41.3 22.2 %fusion.4.refs_0_.refs_7_ = f32[512,2048]{1,0:T(8,128)S(1)} fusion(bf16[8192,512]{1,0:T(8,128)(2,1)S(1)} %bitcast.49, bf16[8192,2048]{1,0:T(8,128)(2,1)} %param.24), kind=kOutput, calls=%fused_computation.11 | convolution fusion | flops 17179869184 | bytes 46137344 | tf_op jit(solution)/shard_map/tm,tn->mn/dot_general | solution.py:281
  63.6 3.4 collective-permute-start.5
  66.9 23.6 %fusion.5.refs_1_.refs_7_ = f32[2048,512]{1,0:T(8,128)S(1)} fusion(bf16[8192,2048]{1,0:T(8,128)(2,1)} %param.25, bf16[8192,512]{1,0:T(8,128)(2,1)} %param.26), kind=kOutput, calls=%fused_computation.12 | convolution fusion | flops 17179869184 | bytes 46137344 | tf_op jit(solution)/shard_map/tm,tn->mn/dot_general | solution.py:281
  90.6 1.6 collective-permute-start.6
  92.7 1.6 collective-permute-start.3
  94.7 9.8 %fusion.6.refs_2_.refs_7_ = f32[512,512]{1,0:T(8,128)S(1)} fusion(bf16[8192,512]{1,0:T(8,128)(2,1)} %param.20, bf16[8192,512]{1,0:T(8,128)(2,1)} %param.21), kind=kOutput, calls=%fused_computation.13 | convolution fusion | flops 4294967296 | bytes 17825792 | tf_op jit(solution)/shard_map/tm,tn->mn/dot_general | solution.py:281
  104.6 0.9 multiply_reduce_fusion.3
  105.5 214.9 %collective-permute-done.2.refs_14_ = f32[256,256]{1,0:T(8,128)S(1)} collective-permute-done((f32[256,256]{1,0:T(8,128)S(1)}, f32[256,256]{1,0:T(8,128)S(1)}, u32[]{:S(2)}, u32[]{:S(2)}) %collective-permute-start.2) | collective-permute-done | bytes 262176 | tf_op jit(solution)/shard_map/ppermute | solution.py:299
  320.4 1.7 collective-permute-start
  322.1 1.7 multiply_reduce_fusion.2
  323.8 4.0 %collective-permute-done.refs_12_ = f32[256,256]{1,0:T(8,128)S(1)} collective-permute-done((f32[256,256]{1,0:T(8,128)S(1)}, f32[256,256]{1,0:T(8,128)S(1)}, u32[]{:S(2)}, u32[]{:S(2)}) %collective-permute-start) | collective-permute-done | bytes 262176 | tf_op jit(solution)/shard_map/ppermute | solution.py:299
  327.9 1.5 collective-permute-start.1
  329.3 1.7 multiply_reduce_fusion.1
  331.0 1.7 multiply_reduce_fusion
  332.7 7.4 %collective-permute-done.1.refs_13_ = f32[256,512]{1,0:T(8,128)S(1)} collective-permute-done((f32[256,512]{1,0:T(8,128)S(1)}, f32[256,512]{1,0:T(8,128)S(1)}, u32[]{:S(2)}, u32[]{:S(2)}) %collective-permute-start.1) | collective-permute-done | bytes 524320 | tf_op jit(solution)/shard_map/ppermute | solution.py:299
  340.1 1.3 collective-permute-start.7
  341.5 0.9 copy-done.31
  342.4 0.7 copy-done.29
  343.1 11.1 %shard_map.283 = (f32[512,2048]{1,0:T(8,128)S(1)}, f32[1,512]{1,0:T(1,128)S(1)}, f32[1,512]{1,0:T(1,128)S(1)}, f32[1,2048]{1,0:T(1,128)S(1)}) custom-call(f32[512,2048]{1,0:T(8,128)S(1)} %fusion.4.refs_0_.refs_7_, f32[2048,512]{1,0:T(8,128)S(1)} %fusion.5.refs_1_.refs_7_, f32[512,512]{1,0:T(8,128)S(1)} %fusion.6.refs_2_.refs_7_, f32[3]{0:T(128)S(1)} %copy-done.14, ...), custom_call_target="tpu_custom_call" | custom-call | flops 838860800 | bytes 12582912 | tf_op jit(solution)/shard_map/pallas_call | solution.py:250
  354.2 0.6 emit.3
  355.5 12.7 %shard_map.284 = (f32[512,2048]{1,0:T(8,128)S(1)}, f32[1,512]{1,0:T(1,128)S(1)}, f32[1,512]{1,0:T(1,128)S(1)}, f32[1,2048]{1,0:T(1,128)S(1)}) custom-call(f32[512,2048]{1,0:T(8,128)S(1)} %multiply_subtract_fusion.2.refs_0_, f32[1,512]{1,0:T(1,128)S(1)} %copy-done.20, f32[1,2048]{1,0:T(1,128)S(1)} %copy-done.11, f32[3]{0:T(128)S(1)} %copy-done.14, ...), custom_call_target="tpu_custom_call" | custom-call | flops 838860800 | bytes 12582912 | tf_op jit(solution)/shard_map/pallas_call | solution.py:250
  369.4 2.3 copy-done.12
  371.7 0.7 copy-done.21
  372.4 12.3 %shard_map.285 = (f32[2048,512]{1,0:T(8,128)S(1)}, f32[1,2048]{1,0:T(1,128)S(1)}, f32[1,2048]{1,0:T(1,128)S(1)}, f32[1,512]{1,0:T(1,128)S(1)}) custom-call(f32[512,2048]{1,0:T(8,128)S(1)} %multiply_subtract_fusion.1.refs_0_, f32[1,512]{1,0:T(1,128)S(1)} %copy-done.21, f32[1,2048]{1,0:T(1,128)S(1)} %copy-done.12, f32[3]{0:T(128)S(1)} %copy-done.14, ...), custom_call_target="tpu_custom_call" | custom-call | flops 838860800 | bytes 12582912 | tf_op jit(solution)/shard_map/pallas_call | solution.py:250
  384.8 0.6 emit.5
  386.1 8.0 %shard_map.286 = (f32[512,512]{1,0:T(8,128)S(1)}, f32[1,128]{1,0:T(1,128)S(1)}, f32[1,512]{1,0:T(1,128)S(1)}, f32[1,512]{1,0:T(1,128)S(1)}) custom-call(f32[2048,512]{1,0:T(8,128)S(1)} %multiply_subtract_fusion.refs_0_, f32[1,2048]{1,0:T(1,128)S(1)} %copy-done.13, f32[1,512]{1,0:T(1,128)S(1)} %copy-done.22, f32[3]{0:T(128)S(1)} %copy-done.14, ...), custom_call_target="tpu_custom_call" | custom-call | flops 209715200 | bytes 3145728 | tf_op jit(solution)/shard_map/pallas_call | solution.py:250
  394.0 1.2 finish.1
  (82 shorter events, 3.5 us)
Async XLA Ops:
  15.8 25.4 %slice-start = ((s8[8388608]{0:T(1024)(128)(4,1)}), s8[4194304]{0:T(1024)(128)(4,1)S(1)}, s32[]{:S(2)}) async-start(s8[8388608]{0:T(1024)(128)(4,1)} %bitcast.48), calls=%async_computation | async-start | bytes 8388608
  26.4 66.2 %copy-start.30 = (f32[512,512]{1,0:T(8,128)}, f32[512,512]{1,0:T(8,128)S(1)}, u32[]{:S(2)}) copy-start(f32[512,512]{1,0:T(8,128)S(1)} %fusion.2.refs_10_) | copy-start | bytes 3145732
  26.5 14.8 %slice-start.1 = ((s8[8388608]{0:T(1024)(128)(4,1)}), s8[4194304]{0:T(1024)(128)(4,1)S(1)}, s32[]{:S(2)}) async-start(s8[8388608]{0:T(1024)(128)(4,1)} %bitcast.48), calls=%async_computation.1 | async-start | bytes 8388608
  41.3 50.9 %copy-start.28 = (f32[512,1024]{1,0:T(8,128)}, f32[512,1024]{1,0:T(8,128)S(1)}, u32[]{:S(2)}) copy-start(f32[512,1024]{1,0:T(8,128)S(1)} %fusion.refs_11_) | copy-start | bytes 6291460
  63.5 277.9 %copy-start.1 = (f32[512,2048]{1,0:T(8,128)}, f32[512,2048]{1,0:T(8,128)S(1)}, u32[]{:S(2)}) copy-start(f32[512,2048]{1,0:T(8,128)S(1)} %fusion.4.refs_0_.refs_7_) | copy-start | bytes 12582916
  63.5 30.7 %copy-start.7 = (f32[256,256]{1,0:T(8,128)S(1)}, f32[256,256]{1,0:T(8,128)}, u32[]{:S(2)}) copy-start(f32[256,256]{1,0:T(8,128)} %head_product.5.refs_9_) | copy-start | bytes 786436
  63.6 291.8 %collective-permute-start.5 = (f32[512,2048]{1,0:T(8,128)S(1)}, f32[512,2048]{1,0:T(8,128)}, u32[]{:S(2)}, u32[]{:S(2)}) collective-permute-start(f32[512,2048]{1,0:T(8,128)S(1)} %fusion.4.refs_0_.refs_7_), channel_id=1, source_target_pairs={{0,4},{4,0},{1,5},{5,1},{2,6},{6,2},{3,7},{7,3}} | collective-permute-start | bytes 12582920 | tf_op jit(solution)/shard_map/ppermute | solution.py:299
  90.6 250.9 %copy-start = (f32[2048,512]{1,0:T(8,128)}, f32[2048,512]{1,0:T(8,128)S(1)}, u32[]{:S(2)}) copy-start(f32[2048,512]{1,0:T(8,128)S(1)} %fusion.5.refs_1_.refs_7_) | copy-start | bytes 12582916
  90.6 13.9 %copy-start.5 = (f32[512,512]{1,0:T(8,128)S(1)}, f32[512,512]{1,0:T(8,128)}, u32[]{:S(2)}) copy-start(f32[512,512]{1,0:T(8,128)} %weight.1) | copy-start | bytes 3145732
  90.6 231.5 %copy-start.23 = (f32[512,2048]{1,0:T(8,128)S(1)}, f32[512,2048]{1,0:T(8,128)}, u32[]{:S(2)}) copy-start(f32[512,2048]{1,0:T(8,128)} %param.28) | copy-start | bytes 12582916
  90.6 237.3 %copy-start.6 = (f32[256,512]{1,0:T(8,128)S(1)}, f32[256,512]{1,0:T(8,128)}, u32[]{:S(2)}) copy-start(f32[256,512]{1,0:T(8,128)} %head_product.4.refs_8_) | copy-start | bytes 1572868
  90.6 238.7 %copy-start.24 = (f32[512,2048]{1,0:T(8,128)S(1)}, f32[512,2048]{1,0:T(8,128)}, u32[]{:S(2)}) copy-start(f32[512,2048]{1,0:T(8,128)} %param.29) | copy-start | bytes 12582916
  90.6 278.7 %collective-permute-start.6 = (f32[2048,512]{1,0:T(8,128)S(1)}, f32[2048,512]{1,0:T(8,128)}, u32[]{:S(2)}, u32[]{:S(2)}) collective-permute-start(f32[2048,512]{1,0:T(8,128)S(1)} %fusion.5.refs_1_.refs_7_), channel_id=1, source_target_pairs={{0,4},{4,0},{1,5},{5,1},{2,6},{6,2},{3,7},{7,3}} | collective-permute-start | bytes 12582920 | tf_op jit(solution)/shard_map/ppermute | solution.py:299
  92.2 249.2 %collective-permute-start.4 = (f32[512,1024]{1,0:T(8,128)S(1)}, f32[512,1024]{1,0:T(8,128)S(1)}, u32[]{:S(2)}, u32[]{:S(2)}) collective-permute-start(f32[512,1024]{1,0:T(8,128)S(1)} %fusion.refs_11_), channel_id=1, source_target_pairs={{0,4},{4,0},{1,5},{5,1},{2,6},{6,2},{3,7},{7,3}} | collective-permute-start | bytes 6291464 | tf_op jit(solution)/shard_map/ppermute | solution.py:299
  92.7 248.7 %collective-permute-start.3 = (f32[512,512]{1,0:T(8,128)S(1)}, f32[512,512]{1,0:T(8,128)S(1)}, u32[]{:S(2)}, u32[]{:S(2)}) collective-permute-start(f32[512,512]{1,0:T(8,128)S(1)} %fusion.2.refs_10_), channel_id=1, source_target_pairs={{0,4},{4,0},{1,5},{5,1},{2,6},{6,2},{3,7},{7,3}} | collective-permute-start | bytes 3145736 | tf_op jit(solution)/shard_map/ppermute | solution.py:299
  94.2 226.2 %collective-permute-start.2 = (f32[256,256]{1,0:T(8,128)S(1)}, f32[256,256]{1,0:T(8,128)S(1)}, u32[]{:S(2)}, u32[]{:S(2)}) collective-permute-start(f32[256,256]{1,0:T(8,128)S(1)} %copy-done.7), channel_id=1, source_target_pairs={{0,4},{4,0},{1,5},{5,1},{2,6},{6,2},{3,7},{7,3}} | collective-permute-start | bytes 786440 | tf_op jit(solution)/shard_map/ppermute | solution.py:299
  104.5 226.5 %copy-start.26 = (f32[2048,512]{1,0:T(8,128)S(1)}, f32[2048,512]{1,0:T(8,128)}, u32[]{:S(2)}) copy-start(f32[2048,512]{1,0:T(8,128)} %param.30) | copy-start | bytes 12582916
  104.5 238.6 %copy-start.8 = (f32[2048]{0:T(1024)S(1)}, f32[2048]{0:T(1024)}, u32[]{:S(2)}) copy-start(f32[2048]{0:T(1024)} %param.34) | copy-start | bytes 24580
  104.5 238.5 %copy-start.14 = (f32[3]{0:T(128)S(1)}, f32[3]{0:T(128)}, u32[]{:S(2)}) copy-start(f32[3]{0:T(128)} %refs_3_.7) | copy-start | bytes 40
  104.6 238.5 %copy-start.15 = (f32[512]{0:T(512)S(1)}, f32[512]{0:T(512)}, u32[]{:S(2)}) copy-start(f32[512]{0:T(512)} %param.33) | copy-start | bytes 6148
  320.4 21.1 %copy-start.33 = (f32[256,256]{1,0:T(8,128)}, f32[256,256]{1,0:T(8,128)S(1)}, u32[]{:S(2)}) copy-start(f32[256,256]{1,0:T(8,128)S(1)} %collective-permute-done.2.refs_14_) | copy-start | bytes 786436
  320.4 7.5 %collective-permute-start = (f32[256,256]{1,0:T(8,128)S(1)}, f32[256,256]{1,0:T(8,128)S(1)}, u32[]{:S(2)}, u32[]{:S(2)}) collective-permute-start(f32[256,256]{1,0:T(8,128)S(1)} %head_product.3.refs_7_), channel_id=1, source_target_pairs={{0,4},{4,0},{1,5},{5,1},{2,6},{6,2},{3,7},{7,3}} | collective-permute-start | bytes 786440 | tf_op jit(solution)/shard_map/ppermute | solution.py:299
  327.9 13.6 %copy-start.34 = (f32[256,256]{1,0:T(8,128)}, f32[256,256]{1,0:T(8,128)S(1)}, u32[]{:S(2)}) copy-start(f32[256,256]{1,0:T(8,128)S(1)} %collective-permute-done.refs_12_) | copy-start | bytes 786436
  327.9 12.2 %collective-permute-start.1 = (f32[256,512]{1,0:T(8,128)S(1)}, f32[256,512]{1,0:T(8,128)S(1)}, u32[]{:S(2)}, u32[]{:S(2)}) collective-permute-start(f32[256,512]{1,0:T(8,128)S(1)} %copy-done.6), channel_id=1, source_target_pairs={{0,4},{4,0},{1,5},{5,1},{2,6},{6,2},{3,7},{7,3}} | collective-permute-start | bytes 1572872 | tf_op jit(solution)/shard_map/ppermute | solution.py:299
  340.1 45.8 %collective-permute-start.7 = (f32[512,512]{1,0:T(8,128)S(1)}, f32[512,512]{1,0:T(8,128)S(1)}, u32[]{:S(2)}, u32[]{:S(2)}) collective-permute-start(f32[512,512]{1,0:T(8,128)S(1)} %fusion.6.refs_2_.refs_7_), channel_id=1, source_target_pairs={{0,4},{4,0},{1,5},{5,1},{2,6},{6,2},{3,7},{7,3}} | collective-permute-start | bytes 3145736 | tf_op jit(solution)/shard_map/ppermute | solution.py:299
  341.4 1.7 copy-start.29
  355.3 13.4 %copy-start.2 = (f32[512,2048]{1,0:T(8,128)}, f32[512,2048]{1,0:T(8,128)S(1)}, u32[]{:S(2)}) copy-start(f32[512,2048]{1,0:T(8,128)S(1)} %multiply_subtract_fusion.2.refs_0_) | copy-start | bytes 12582916
  355.3 12.9 %copy-start.25 = (f32[512,2048]{1,0:T(8,128)S(1)}, f32[512,2048]{1,0:T(8,128)}, u32[]{:S(2)}) copy-start(f32[512,2048]{1,0:T(8,128)} %param.29) | copy-start | bytes 12582916
  368.3 17.1 %copy-start.27 = (f32[2048,512]{1,0:T(8,128)S(1)}, f32[2048,512]{1,0:T(8,128)}, u32[]{:S(2)}) copy-start(f32[2048,512]{1,0:T(8,128)} %param.30) | copy-start | bytes 12582916
  368.7 17.1 %copy-start.3 = (f32[512,2048]{1,0:T(8,128)}, f32[512,2048]{1,0:T(8,128)S(1)}, u32[]{:S(2)}) copy-start(f32[512,2048]{1,0:T(8,128)S(1)} %multiply_subtract_fusion.1.refs_0_) | copy-start | bytes 12582916
  369.4 2.4 copy-start.12
  385.9 9.4 %copy-start.4 = (f32[2048,512]{1,0:T(8,128)}, f32[2048,512]{1,0:T(8,128)S(1)}, u32[]{:S(2)}) copy-start(f32[2048,512]{1,0:T(8,128)S(1)} %multiply_subtract_fusion.refs_0_) | copy-start | bytes 12582916
  (13 other events, 12.7 us)

commit v5 on v4

--- a/solution.py
+++ b/solution.py
@@ -12,7 +12,7 @@
 MESH = pl.DeviceIdType.MESH
 LANES = 128
 NAMES = ('gate', 'up', 'down', 'attn')
-GATE_BOXES = ((0, 0, 256, 256), (256, 0, 256, 512), (0, 256, 256, 256), (0, 512, 512, 512), (0, 1024, 512, 1024))
+GATE_BOXES = ((0, 0, 256, 384), (256, 0, 256, 384), (0, 384, 512, 256), (0, 640, 512, 384), (0, 1024, 512, 1024))
 N_HEAD = 3
 HEAD_LIMIT = 58 * 1024 * 1024
 
@@ -26,7 +26,7 @@
 def stats_kernel(n_token, boxes, near, direct, step, m_total, n_total, *refs):
     n_piece = len(boxes)
     refs = refs[n_token:]
-    hyper, w_sq, row_old, col_old = refs[:4]
+    w_sq, hyper, row_old, col_old = refs[:4]
     parts = refs[4:4 + n_piece]
     recvs = refs[4 + n_piece:4 + 2 * n_piece]
     (grad, row_scale, new_row, new_col,
@@ -88,7 +88,7 @@
                                             device_id=row_peer, device_id_type=MESH)
     row_copy.start()
     col_copy.start()
-    beta_two = hyper[0]
+    beta_two = hyper[0:1, 0:1]
 
     col_copy.wait()
     col_now = beta_two * col_old[...] + (1.0 - beta_two) * ((send_col[...] + recv_col[...]) / m_total)
@@ -144,8 +144,8 @@
     row_total = pair[1:2, :]
     upd_rms = jnp.sqrt(row_total * total[0:1, :] / size)
     w_rms = jnp.sqrt(total[2:3, :] / size)
-    clip = jnp.maximum(1.0, upd_rms / hyper[2])
-    factor = hyper[1] * jnp.maximum(EPS_TWO, w_rms) * jnp.sqrt(row_total) / clip
+    clip = jnp.maximum(1.0, upd_rms / hyper[2:3, 0:1])
+    factor = hyper[1:2, 0:1] * jnp.maximum(EPS_TWO, w_rms) * jnp.sqrt(row_total) / clip
     if direct:
         row_scale[...] = jnp.broadcast_to(factor, (1, LANES))
     else:
@@ -156,24 +156,31 @@
     n_step = x_sem.shape[0]
     depth = x_buf.shape[0] // n_step
     rows, cols = out.shape
-    copies = []
-    for k in range(n_step):
-        band = pl.ds(k * depth, depth)
-        copies.append((
-            pltpu.make_async_copy(x_ref.at[band, pl.ds(row_start, rows)], x_buf.at[band, :], x_sem.at[k]),
-            pltpu.make_async_copy(dy_ref.at[band, pl.ds(col_start, cols)], dy_buf.at[band, :], dy_sem.at[k])))
-        copies[-1][0].start()
-        copies[-1][1].start()
-    for k in range(n_step):
-        band = pl.ds(k * depth, depth)
-        copies[k][0].wait()
-        copies[k][1].wait()
-        term = lax.dot_general(x_buf[band, :], dy_buf[band, :], (((0,), (0,)), ((), ())),
+
+    def copies(k):
+        band = pl.ds(pl.multiple_of(k * depth, depth), depth)
+        return (pltpu.make_async_copy(x_ref.at[band, pl.ds(row_start, rows)], x_buf.at[band, :], x_sem.at[k]),
+                pltpu.make_async_copy(dy_ref.at[band, pl.ds(col_start, cols)], dy_buf.at[band, :], dy_sem.at[k]))
+
+    def begin(k, carry):
+        for copy in copies(k):
+            copy.start()
+        return carry
+
+    def multiply(k):
+        for copy in copies(k):
+            copy.wait()
+        band = pl.ds(pl.multiple_of(k * depth, depth), depth)
+        return lax.dot_general(x_buf[band, :], dy_buf[band, :], (((0,), (0,)), ((), ())),
                                preferred_element_type=jnp.float32)
-        if k == 0:
-            out[...] = term
-        else:
-            out[...] += term
+
+    def follow(k, carry):
+        out[...] += multiply(k)
+        return carry
+
+    lax.fori_loop(0, n_step, begin, 0, unroll=True)
+    out[...] = jnp.zeros_like(out)
+    lax.fori_loop(0, n_step, follow, 0)
 
 
 def head_product(x_block, dy_block, row_start, rows, col_start, cols):
@@ -186,7 +193,7 @@
         out_specs=pl.BlockSpec(memory_space=pltpu.VMEM),
         scratch_shapes=[pltpu.VMEM((tokens, rows), x_block.dtype), pltpu.VMEM((tokens, cols), dy_block.dtype),
                         pltpu.SemaphoreType.DMA((8,)), pltpu.SemaphoreType.DMA((8,))],
-        compiler_params=pltpu.CompilerParams(vmem_limit_bytes=HEAD_LIMIT if (row_start, col_start) != (0, 0) else 14 * 1024 * 1024),
+        compiler_params=pltpu.CompilerParams(vmem_limit_bytes=HEAD_LIMIT if col_start else 14 * 1024 * 1024),
         cost_estimate=pl.CostEstimate(flops=2 * tokens * rows * cols, bytes_accessed=2 * tokens * (rows + cols),
                                       transcendentals=0),
         name="head_product",
@@ -250,7 +257,7 @@
     return pl.pallas_call(
         functools.partial(stats_kernel, len(tokens), boxes, near, not staged, 16, 2 * rows, 2 * cols),
         out_shape=[jax.ShapeDtypeStruct(s, f32) for s in shapes],
-        in_specs=[anyw] * len(tokens) + [smem] * 2 + [vmem] * 2 + places,
+        in_specs=[anyw] * len(tokens) + [smem] + [vmem] * 3 + places,
         out_specs=[vmem] * 4,
         scratch_shapes=[
             pltpu.VMEM((rows, LANES), f32),
@@ -263,7 +270,7 @@
         compiler_params=pltpu.CompilerParams(collective_id=index, has_side_effects=True,
                                              vmem_limit_bytes=16 * 1024 * 1024 if staged else 6 * 1024 * 1024),
         cost_estimate=pl.CostEstimate(flops=8 * rows * cols * 100, bytes_accessed=12 * rows * cols, transcendentals=0),
-    )(*tokens, hyper, w_sq.reshape(1, 1), row_old.reshape(1, rows), col_old.reshape(1, cols), *halves)
+    )(*tokens, w_sq.reshape(1, 1), hyper, row_old.reshape(1, rows), col_old.reshape(1, cols), *halves)
 
 
 def solution(mesh):
@@ -299,6 +306,7 @@
             recvs[name].append(lax.ppermute(before, 'dp', SWAP))
             parts[name].append(before)
         results = {}
+        hyper_rows = jnp.broadcast_to(jnp.pad(hyper_params, (0, 5))[:, None], (8, LANES))
         tokens = [parts['up'][0], parts['down'][0], parts['attn'][0]]
         weights = {'gate': w_gate, 'up': w_up, 'down': w_down, 'attn': w_attn}
         stats = {'gate': (r_gate, c_gate), 'up': (r_up, c_up), 'down': (r_down, c_down), 'attn': (r_attn, c_attn)}
@@ -308,7 +316,7 @@
             grad, row_scale, new_row, new_col = statistics(
                 tokens, tuple(b[:2] for b in GATE_BOXES) if name == 'gate' else ((0, 0),),
                 N_HEAD if name == 'gate' else 0, parts[name], recvs[name],
-                jnp.sum(weight * weight), *stats[name], hyper_params, index)
+                jnp.sum(weight * weight), *stats[name], hyper_rows, index)
             if index < 3:
                 new_weight = weight - grad * row_scale.reshape(rows, 1)
                 new_row, new_col = emit((new_row, new_col))

time: 395 us -> 390 us (0.987)
  transfers between devices with their start and end apart: 8 -> 8, of which waited for: 3 -> 3; matrix products, arithmetic and copies ran while one was open for 10% -> 10% of each run, Pallas kernels for 10% -> 9%
where the time goes in v5:
time: 390 us
  waiting for transfers between devices  223 us (57%)
  matrix products  79 us (20%)
  Pallas kernels  62.7 us (16%)
  starting transfers between devices  13.2 us (3%)
  other arithmetic  7.38 us (2%)
    ppermute x8, waiting for transfers between devices, per_device(): recvs[name].append(lax.ppermute(before, 'dp', SWAP))  223 us
    dot_general x5, matrix products, product(): jnp.einsum('tm,tn->mn', x_block, dy_block, preferred_element_type=jnp.flo...  79 us
    pallas_call x4, Pallas kernels, statistics(): pl.pallas_call(functools.partial(stats_kernel, len(tokens), boxes, near,...  42.5 us
    pallas_call x3, Pallas kernels, head_product(): pl.pallas_call(functools.partial(head_kernel, row_start, col_start), out_...  17.1 us
    ppermute x8, starting transfers between devices, per_device(): recvs[name].append(lax.ppermute(before, 'dp', SWAP))  13.2 us
  transfers between devices with their start and end apart: 8, of which 3 were waited for; matrix products, arithmetic and copies ran while one was open for 10% of the time, Pallas kernels for 9%

profile of v5, /device:TPU:0, one launch (start us, length us, event | category | flops | bytes accessed | tf_op | source)
XLA Modules:
  0.0 389.9 jit_solution(10637073598209349242)
XLA Ops:
  0.6 5.4 %head_product.3.refs_7_ = f32[256,384]{1,0:T(8,128)S(1)} custom-call(bf16[8192,512]{1,0:T(8,128)(2,1)} %x_ref.3, bf16[8192,2048]{1,0:T(8,128)(2,1)} %dy_ref.5), custom_call_target="tpu_custom_call" | custom-call | flops 1610612736 | bytes 10485760 | tf_op jit(solution)/shard_map/head_product/pallas_call | solution.py:189
  6.0 5.4 %head_product.4.refs_8_ = f32[256,384]{1,0:T(8,128)S(1)} custom-call(bf16[8192,512]{1,0:T(8,128)(2,1)} %x_ref.3, bf16[8192,2048]{1,0:T(8,128)(2,1)} %dy_ref.5), custom_call_target="tpu_custom_call" | custom-call | flops 1610612736 | bytes 10485760 | tf_op jit(solution)/shard_map/head_product/pallas_call | solution.py:189
  11.4 6.4 %head_product.5.refs_9_ = f32[512,256]{1,0:T(8,128)} custom-call(bf16[8192,512]{1,0:T(8,128)(2,1)} %x_ref.3, bf16[8192,2048]{1,0:T(8,128)(2,1)} %dy_ref.5), custom_call_target="tpu_custom_call" | custom-call | flops 2147483648 | bytes 12582912 | tf_op jit(solution)/shard_map/head_product/pallas_call | solution.py:189
  17.8 9.0 %fusion.2.refs_10_ = f32[512,384]{1,0:T(8,128)S(1)} fusion(bf16[8192,512]{1,0:T(8,128)(2,1)} %x_ref.3, bf16[8192,2048]{1,0:T(8,128)(2,1)} %dy_ref.5), kind=kOutput, calls=%fused_computation.2 | convolution fusion | flops 3221225472 | bytes 15466496 | tf_op jit(solution)/shard_map/tm,tn->mn/dot_general | solution.py:288
  26.8 14.7 %fusion.refs_11_ = f32[512,1024]{1,0:T(8,128)S(1)} fusion(bf16[8192,512]{1,0:T(8,128)(2,1)} %x_ref.3, bf16[8192,2048]{1,0:T(8,128)(2,1)} %dy_ref.5), kind=kOutput, calls=%fused_computation | convolution fusion | flops 8589934592 | bytes 27262976 | tf_op jit(solution)/shard_map/tm,tn->mn/dot_general | solution.py:288
  41.6 22.2 %fusion.4.refs_0_.refs_7_ = f32[512,2048]{1,0:T(8,128)S(1)} fusion(bf16[8192,512]{1,0:T(8,128)(2,1)S(1)} %bitcast.49, bf16[8192,2048]{1,0:T(8,128)(2,1)} %param.24), kind=kOutput, calls=%fused_computation.11 | convolution fusion | flops 17179869184 | bytes 46137344 | tf_op jit(solution)/shard_map/tm,tn->mn/dot_general | solution.py:288
  63.8 3.4 collective-permute-start.5
  67.2 23.6 %fusion.5.refs_1_.refs_7_ = f32[2048,512]{1,0:T(8,128)S(1)} fusion(bf16[8192,2048]{1,0:T(8,128)(2,1)} %param.25, bf16[8192,512]{1,0:T(8,128)(2,1)} %param.26), kind=kOutput, calls=%fused_computation.12 | convolution fusion | flops 17179869184 | bytes 46137344 | tf_op jit(solution)/shard_map/tm,tn->mn/dot_general | solution.py:288
  90.9 1.5 collective-permute-start.6
  92.9 1.5 collective-permute-start.1
  95.0 9.5 %fusion.6.refs_2_.refs_7_ = f32[512,512]{1,0:T(8,128)S(1)} fusion(bf16[8192,512]{1,0:T(8,128)(2,1)} %param.20, bf16[8192,512]{1,0:T(8,128)(2,1)} %param.21), kind=kOutput, calls=%fused_computation.13 | convolution fusion | flops 4294967296 | bytes 17825792 | tf_op jit(solution)/shard_map/tm,tn->mn/dot_general | solution.py:288
  104.5 0.9 multiply_reduce_fusion.3
  105.5 196.4 %collective-permute-done.1.refs_13_ = f32[256,384]{1,0:T(8,128)S(1)} collective-permute-done((f32[256,384]{1,0:T(8,128)S(1)}, f32[256,384]{1,0:T(8,128)S(1)}, u32[]{:S(2)}, u32[]{:S(2)}) %collective-permute-start.1) | collective-permute-done | bytes 393248 | tf_op jit(solution)/shard_map/ppermute | solution.py:306
  301.9 2.0 collective-permute-start.3
  303.9 1.7 multiply_reduce_fusion.2
  305.5 4.7 %collective-permute-done.refs_12_ = f32[256,384]{1,0:T(8,128)S(1)} collective-permute-done((f32[256,384]{1,0:T(8,128)S(1)}, f32[256,384]{1,0:T(8,128)S(1)}, u32[]{:S(2)}, u32[]{:S(2)}) %collective-permute-start) | collective-permute-done | bytes 393248 | tf_op jit(solution)/shard_map/ppermute | solution.py:306
  310.3 2.0 collective-permute-start.2
  312.3 1.7 multiply_reduce_fusion.1
  314.0 1.7 multiply_reduce_fusion
  315.7 21.8 %collective-permute-done.2.refs_14_ = f32[512,256]{1,0:T(8,128)S(1)} collective-permute-done((f32[512,256]{1,0:T(8,128)S(1)}, f32[512,256]{1,0:T(8,128)S(1)}, u32[]{:S(2)}, u32[]{:S(2)}) %collective-permute-start.2) | collective-permute-done | bytes 524320 | tf_op jit(solution)/shard_map/ppermute | solution.py:306
  337.5 1.7 collective-permute-start.7
  339.3 0.8 copy-done.29
  340.1 0.7 copy-done.27
  340.8 10.5 %shard_map.283 = (f32[512,2048]{1,0:T(8,128)S(1)}, f32[1,512]{1,0:T(1,128)S(1)}, f32[1,512]{1,0:T(1,128)S(1)}, f32[1,2048]{1,0:T(1,128)S(1)}) custom-call(f32[512,2048]{1,0:T(8,128)S(1)} %fusion.4.refs_0_.refs_7_, f32[2048,512]{1,0:T(8,128)S(1)} %fusion.5.refs_1_.refs_7_, f32[512,512]{1,0:T(8,128)S(1)} %fusion.6.refs_2_.refs_7_, f32[1,1]{1,0:T(1,128)} %bitcast.refs_3_, ...), custom_call_target="tpu_custom_call" | custom-call | flops 838860800 | bytes 12582912 | tf_op jit(solution)/shard_map/pallas_call | solution.py:257
  352.7 12.4 %shard_map.284 = (f32[512,2048]{1,0:T(8,128)S(1)}, f32[1,512]{1,0:T(1,128)S(1)}, f32[1,512]{1,0:T(1,128)S(1)}, f32[1,2048]{1,0:T(1,128)S(1)}) custom-call(f32[512,2048]{1,0:T(8,128)S(1)} %multiply_subtract_fusion.2.refs_0_, f32[1,512]{1,0:T(1,128)S(1)} %copy-done.19, f32[1,2048]{1,0:T(1,128)S(1)} %copy-done.11, f32[1,1]{1,0:T(1,128)} %bitcast.4.refs_3_, ...), custom_call_target="tpu_custom_call" | custom-call | flops 838860800 | bytes 12582912 | tf_op jit(solution)/shard_map/pallas_call | solution.py:257
  365.6 0.6 emit.4
  366.3 0.7 copy-done.12
  367.0 0.7 copy-done.20
  367.7 12.1 %shard_map.285 = (f32[2048,512]{1,0:T(8,128)S(1)}, f32[1,2048]{1,0:T(1,128)S(1)}, f32[1,2048]{1,0:T(1,128)S(1)}, f32[1,512]{1,0:T(1,128)S(1)}) custom-call(f32[512,2048]{1,0:T(8,128)S(1)} %multiply_subtract_fusion.1.refs_0_, f32[1,512]{1,0:T(1,128)S(1)} %copy-done.20, f32[1,2048]{1,0:T(1,128)S(1)} %copy-done.12, f32[1,1]{1,0:T(1,128)} %bitcast.8.refs_3_, ...), custom_call_target="tpu_custom_call" | custom-call | flops 838860800 | bytes 12582912 | tf_op jit(solution)/shard_map/pallas_call | solution.py:257
  379.8 0.6 emit.5
  381.2 7.4 %shard_map.286 = (f32[512,512]{1,0:T(8,128)S(1)}, f32[1,128]{1,0:T(1,128)S(1)}, f32[1,512]{1,0:T(1,128)S(1)}, f32[1,512]{1,0:T(1,128)S(1)}) custom-call(f32[2048,512]{1,0:T(8,128)S(1)} %multiply_subtract_fusion.refs_0_, f32[1,2048]{1,0:T(1,128)S(1)} %copy-done.8, f32[1,512]{1,0:T(1,128)S(1)} %copy-done.16, f32[1,1]{1,0:T(1,128)} %bitcast.12.refs_3_, ...), custom_call_target="tpu_custom_call" | custom-call | flops 209715200 | bytes 3145728 | tf_op jit(solution)/shard_map/pallas_call | solution.py:257
  388.6 1.2 finish.1
  (82 shorter events, 3.7 us)
Async XLA Ops:
  17.8 23.7 %slice-start = ((s8[8388608]{0:T(1024)(128)(4,1)}), s8[4194304]{0:T(1024)(128)(4,1)S(1)}, s32[]{:S(2)}) async-start(s8[8388608]{0:T(1024)(128)(4,1)} %bitcast.48), calls=%async_computation | async-start | bytes 8388608
  26.8 275.0 %copy-start.28 = (f32[512,384]{1,0:T(8,128)}, f32[512,384]{1,0:T(8,128)S(1)}, u32[]{:S(2)}) copy-start(f32[512,384]{1,0:T(8,128)S(1)} %fusion.2.refs_10_) | copy-start | bytes 2359300
  26.8 14.7 %slice-start.1 = ((s8[8388608]{0:T(1024)(128)(4,1)}), s8[4194304]{0:T(1024)(128)(4,1)S(1)}, s32[]{:S(2)}) async-start(s8[8388608]{0:T(1024)(128)(4,1)} %bitcast.48), calls=%async_computation.1 | async-start | bytes 8388608
  41.6 50.8 %copy-start.26 = (f32[512,1024]{1,0:T(8,128)}, f32[512,1024]{1,0:T(8,128)S(1)}, u32[]{:S(2)}) copy-start(f32[512,1024]{1,0:T(8,128)S(1)} %fusion.refs_11_) | copy-start | bytes 6291460
  63.8 275.5 %copy-start.4 = (f32[512,2048]{1,0:T(8,128)}, f32[512,2048]{1,0:T(8,128)S(1)}, u32[]{:S(2)}) copy-start(f32[512,2048]{1,0:T(8,128)S(1)} %fusion.4.refs_0_.refs_7_) | copy-start | bytes 12582916
  63.8 288.6 %collective-permute-start.5 = (f32[512,2048]{1,0:T(8,128)S(1)}, f32[512,2048]{1,0:T(8,128)}, u32[]{:S(2)}, u32[]{:S(2)}) collective-permute-start(f32[512,2048]{1,0:T(8,128)S(1)} %fusion.4.refs_0_.refs_7_), channel_id=1, source_target_pairs={{0,4},{4,0},{1,5},{5,1},{2,6},{6,2},{3,7},{7,3}} | collective-permute-start | bytes 12582920 | tf_op jit(solution)/shard_map/ppermute | solution.py:306
  90.8 248.5 %copy-start.3 = (f32[2048,512]{1,0:T(8,128)}, f32[2048,512]{1,0:T(8,128)S(1)}, u32[]{:S(2)}) copy-start(f32[2048,512]{1,0:T(8,128)S(1)} %fusion.5.refs_1_.refs_7_) | copy-start | bytes 12582916
  90.8 13.6 %copy-start.33 = (f32[3]{0:T(128)S(1)}, f32[3]{0:T(128)}, u32[]{:S(2)}) copy-start(f32[3]{0:T(128)} %param.39) | copy-start | bytes 40
  90.8 13.7 %copy-start.5 = (f32[512,512]{1,0:T(8,128)S(1)}, f32[512,512]{1,0:T(8,128)}, u32[]{:S(2)}) copy-start(f32[512,512]{1,0:T(8,128)} %weight.1) | copy-start | bytes 3145732
  90.9 213.0 %copy-start.21 = (f32[512,2048]{1,0:T(8,128)S(1)}, f32[512,2048]{1,0:T(8,128)}, u32[]{:S(2)}) copy-start(f32[512,2048]{1,0:T(8,128)} %param.28) | copy-start | bytes 12582916
  90.9 219.4 %copy-start.6 = (f32[512,256]{1,0:T(8,128)S(1)}, f32[512,256]{1,0:T(8,128)}, u32[]{:S(2)}) copy-start(f32[512,256]{1,0:T(8,128)} %head_product.5.refs_9_) | copy-start | bytes 1572868
  90.9 275.4 %collective-permute-start.6 = (f32[2048,512]{1,0:T(8,128)S(1)}, f32[2048,512]{1,0:T(8,128)}, u32[]{:S(2)}, u32[]{:S(2)}) collective-permute-start(f32[2048,512]{1,0:T(8,128)S(1)} %fusion.5.refs_1_.refs_7_), channel_id=1, source_target_pairs={{0,4},{4,0},{1,5},{5,1},{2,6},{6,2},{3,7},{7,3}} | collective-permute-start | bytes 12582920 | tf_op jit(solution)/shard_map/ppermute | solution.py:306
  92.4 246.8 %collective-permute-start.4 = (f32[512,1024]{1,0:T(8,128)S(1)}, f32[512,1024]{1,0:T(8,128)S(1)}, u32[]{:S(2)}, u32[]{:S(2)}) collective-permute-start(f32[512,1024]{1,0:T(8,128)S(1)} %fusion.refs_11_), channel_id=1, source_target_pairs={{0,4},{4,0},{1,5},{5,1},{2,6},{6,2},{3,7},{7,3}} | collective-permute-start | bytes 6291464 | tf_op jit(solution)/shard_map/ppermute | solution.py:306
  92.9 208.9 %collective-permute-start.1 = (f32[256,384]{1,0:T(8,128)S(1)}, f32[256,384]{1,0:T(8,128)S(1)}, u32[]{:S(2)}, u32[]{:S(2)}) collective-permute-start(f32[256,384]{1,0:T(8,128)S(1)} %head_product.4.refs_8_), channel_id=1, source_target_pairs={{0,4},{4,0},{1,5},{5,1},{2,6},{6,2},{3,7},{7,3}} | collective-permute-start | bytes 1179656 | tf_op jit(solution)/shard_map/ppermute | solution.py:306
  94.4 215.8 %collective-permute-start = (f32[256,384]{1,0:T(8,128)S(1)}, f32[256,384]{1,0:T(8,128)S(1)}, u32[]{:S(2)}, u32[]{:S(2)}) collective-permute-start(f32[256,384]{1,0:T(8,128)S(1)} %head_product.3.refs_7_), channel_id=1, source_target_pairs={{0,4},{4,0},{1,5},{5,1},{2,6},{6,2},{3,7},{7,3}} | collective-permute-start | bytes 1179656 | tf_op jit(solution)/shard_map/ppermute | solution.py:306
  104.5 207.8 %copy-start.22 = (f32[512,2048]{1,0:T(8,128)S(1)}, f32[512,2048]{1,0:T(8,128)}, u32[]{:S(2)}) copy-start(f32[512,2048]{1,0:T(8,128)} %param.29) | copy-start | bytes 12582916
  104.5 209.5 %copy-start.24 = (f32[2048,512]{1,0:T(8,128)S(1)}, f32[2048,512]{1,0:T(8,128)}, u32[]{:S(2)}) copy-start(f32[2048,512]{1,0:T(8,128)} %param.30) | copy-start | bytes 12582916
  105.5 235.3 %copy-start.7 = (f32[2048]{0:T(1024)S(1)}, f32[2048]{0:T(1024)}, u32[]{:S(2)}) copy-start(f32[2048]{0:T(1024)} %param.34) | copy-start | bytes 24580
  105.5 235.3 %copy-start.13 = (f32[512]{0:T(512)S(1)}, f32[512]{0:T(512)}, u32[]{:S(2)}) copy-start(f32[512]{0:T(512)} %param.33) | copy-start | bytes 6148
  301.8 13.8 %copy-start.31 = (f32[256,384]{1,0:T(8,128)}, f32[256,384]{1,0:T(8,128)S(1)}, u32[]{:S(2)}) copy-start(f32[256,384]{1,0:T(8,128)S(1)} %collective-permute-done.1.refs_13_) | copy-start | bytes 1179652
  301.9 37.4 %collective-permute-start.3 = (f32[512,384]{1,0:T(8,128)S(1)}, f32[512,384]{1,0:T(8,128)S(1)}, u32[]{:S(2)}, u32[]{:S(2)}) collective-permute-start(f32[512,384]{1,0:T(8,128)S(1)} %fusion.2.refs_10_), channel_id=1, source_target_pairs={{0,4},{4,0},{1,5},{5,1},{2,6},{6,2},{3,7},{7,3}} | collective-permute-start | bytes 2359304 | tf_op jit(solution)/shard_map/ppermute | solution.py:306
  310.3 29.1 %copy-start.32 = (f32[256,384]{1,0:T(8,128)}, f32[256,384]{1,0:T(8,128)S(1)}, u32[]{:S(2)}) copy-start(f32[256,384]{1,0:T(8,128)S(1)} %collective-permute-done.refs_12_) | copy-start | bytes 1179652
  310.3 27.2 %collective-permute-start.2 = (f32[512,256]{1,0:T(8,128)S(1)}, f32[512,256]{1,0:T(8,128)S(1)}, u32[]{:S(2)}, u32[]{:S(2)}) collective-permute-start(f32[512,256]{1,0:T(8,128)S(1)} %copy-done.6), channel_id=1, source_target_pairs={{0,4},{4,0},{1,5},{5,1},{2,6},{6,2},{3,7},{7,3}} | collective-permute-start | bytes 1572872 | tf_op jit(solution)/shard_map/ppermute | solution.py:306
  337.5 1.8 copy-start.30
  337.5 43.5 %collective-permute-start.7 = (f32[512,512]{1,0:T(8,128)S(1)}, f32[512,512]{1,0:T(8,128)S(1)}, u32[]{:S(2)}, u32[]{:S(2)}) collective-permute-start(f32[512,512]{1,0:T(8,128)S(1)} %fusion.6.refs_2_.refs_7_), channel_id=1, source_target_pairs={{0,4},{4,0},{1,5},{5,1},{2,6},{6,2},{3,7},{7,3}} | collective-permute-start | bytes 3145736 | tf_op jit(solution)/shard_map/ppermute | solution.py:306
  339.2 1.6 copy-start.27
  352.4 12.7 %copy-start = (f32[512,2048]{1,0:T(8,128)}, f32[512,2048]{1,0:T(8,128)S(1)}, u32[]{:S(2)}) copy-start(f32[512,2048]{1,0:T(8,128)S(1)} %multiply_subtract_fusion.2.refs_0_) | copy-start | bytes 12582916
  352.7 12.4 %copy-start.23 = (f32[512,2048]{1,0:T(8,128)S(1)}, f32[512,2048]{1,0:T(8,128)}, u32[]{:S(2)}) copy-start(f32[512,2048]{1,0:T(8,128)} %param.29) | copy-start | bytes 12582916
  365.1 1.2 copy-start.10
  365.6 14.3 %copy-start.1 = (f32[512,2048]{1,0:T(8,128)}, f32[512,2048]{1,0:T(8,128)S(1)}, u32[]{:S(2)}) copy-start(f32[512,2048]{1,0:T(8,128)S(1)} %multiply_subtract_fusion.1.refs_0_) | copy-start | bytes 12582916
  367.7 12.8 %copy-start.25 = (f32[2048,512]{1,0:T(8,128)S(1)}, f32[2048,512]{1,0:T(8,128)}, u32[]{:S(2)}) copy-start(f32[2048,512]{1,0:T(8,128)} %param.30) | copy-start | bytes 12582916
  381.0 8.9 %copy-start.2 = (f32[2048,512]{1,0:T(8,128)}, f32[2048,512]{1,0:T(8,128)S(1)}, u32[]{:S(2)}) copy-start(f32[2048,512]{1,0:T(8,128)S(1)} %multiply_subtract_fusion.refs_0_) | copy-start | bytes 12582916
  (12 other events, 9.2 us)

commit v6 on v5

--- a/solution.py
+++ b/solution.py
@@ -20,7 +20,7 @@
 def peers():
     row_other = 1 - lax.axis_index('row')
     col_other = 1 - lax.axis_index('col')
-    return ({'row': row_other}, {'col': col_other}, {'row': row_other, 'col': col_other})
+    return ({'row': row_other}, {'col': col_other})
 
 
 def stats_kernel(n_token, boxes, near, direct, step, m_total, n_total, *refs):
@@ -30,12 +30,16 @@
     parts = refs[4:4 + n_piece]
     recvs = refs[4 + n_piece:4 + 2 * n_piece]
     (grad, row_scale, new_row, new_col,
-     row_acc, send_row, send_col, recv_row, recv_col, send_val, recv_val,
-     vec_send, vec_recv, val_send, val_recv) = refs[4 + 2 * n_piece:4 + 2 * n_piece + 15]
+     row_acc, send_row, send_col, recv_row, recv_col, send_upd, recv_upd, send_val, recv_val,
+     swap_send, swap_recv) = refs[4 + 2 * n_piece:4 + 2 * n_piece + 15]
     staged = refs[4 + 2 * n_piece + 15:]
     rows, cols = grad.shape
     others = peers()
-    row_peer, col_peer, _ = others
+    row_peer, col_peer = others
+
+    def swap(k, src, dst, other):
+        return pltpu.make_async_remote_copy(src, dst, swap_send.at[k], swap_recv.at[k],
+                                            device_id=other, device_id_type=MESH)
 
     barrier = pltpu.get_barrier_semaphore()
     for other in others:
@@ -81,11 +85,9 @@
     for k in range(rows // LANES):
         tile = row_acc[k * LANES:(k + 1) * LANES, :].T
         send_row[:, k * LANES:(k + 1) * LANES] = jnp.sum(tile, axis=0, keepdims=True)
-    pl.semaphore_wait(barrier, 3)
-    row_copy = pltpu.make_async_remote_copy(send_row, recv_row, vec_send.at[0], vec_recv.at[0],
-                                            device_id=col_peer, device_id_type=MESH)
-    col_copy = pltpu.make_async_remote_copy(send_col, recv_col, vec_send.at[1], vec_recv.at[1],
-                                            device_id=row_peer, device_id_type=MESH)
+    pl.semaphore_wait(barrier, 2)
+    row_copy = swap(0, send_row, recv_row, col_peer)
+    col_copy = swap(1, send_col, recv_col, row_peer)
     row_copy.start()
     col_copy.start()
     beta_two = hyper[0:1, 0:1]
@@ -107,27 +109,21 @@
         return carry
 
     lax.fori_loop(0, rows // step, second, 0)
-    sums = [jnp.sum(row_acc[k * LANES:(k + 1) * LANES, :].T, axis=0, keepdims=True) for k in range(rows // LANES)]
+    for k in range(rows // LANES):
+        tile = row_acc[k * LANES:(k + 1) * LANES, :].T
+        send_upd[:, k * LANES:(k + 1) * LANES] = jnp.sum(tile, axis=0, keepdims=True)
+    lane = lax.broadcasted_iota(jnp.int32, (1, LANES), 1)
+    send_upd[:, rows:] = jnp.where(lane == 0, w_sq[0, 0], 0.0)
+    upd_copy = swap(2, send_upd, recv_upd, col_peer)
+    upd_copy.start()
 
     row_copy.wait()
     row_now = beta_two * row_old[...] + (1.0 - beta_two) * ((send_row[...] + recv_row[...]) / n_total)
     new_row[...] = row_now
     row_inv = 1.0 / jnp.sqrt(row_now)
-    upd_sq = jnp.zeros((1, LANES), jnp.float32)
     row_part = jnp.zeros((1, LANES), jnp.float32)
     for k in range(rows // LANES):
-        inv = row_inv[:, k * LANES:(k + 1) * LANES]
-        upd_sq = upd_sq + sums[k] * (inv * inv)
         row_part = row_part + row_now[:, k * LANES:(k + 1) * LANES]
-    which = lax.broadcasted_iota(jnp.int32, (8, LANES), 0)
-    lane = lax.broadcasted_iota(jnp.int32, (8, LANES), 1)
-    send_val[...] = jnp.where(which == 0, upd_sq, jnp.where(which == 1, row_part,
-                                                            jnp.where(lane == 0, w_sq[0, 0], 0.0)))
-    copies = [pltpu.make_async_remote_copy(send_val, recv_val.at[k], val_send.at[k], val_recv.at[k],
-                                           device_id=other, device_id_type=MESH)
-              for k, other in enumerate(others)]
-    for copy in copies:
-        copy.start()
     if direct:
         for k in range(rows // LANES):
             band = pl.ds(k * LANES, LANES)
@@ -135,13 +131,20 @@
             for j in range(cols // LANES):
                 lanes = pl.ds(j * LANES, LANES)
                 grad[band, lanes] = grad[band, lanes] * scale
-    for copy in copies:
-        copy.wait()
-    pair = send_val[...] + recv_val[0]
-    total = jnp.sum(pair + (recv_val[1] + recv_val[2]), axis=1, keepdims=True)
-    pair = jnp.sum(pair, axis=1, keepdims=True)
+    upd_copy.wait()
+    upd_both = send_upd[...] + recv_upd[...]
+    upd_sq = jnp.zeros((1, LANES), jnp.float32)
+    for k in range(rows // LANES):
+        inv = row_inv[:, k * LANES:(k + 1) * LANES]
+        upd_sq = upd_sq + upd_both[:, k * LANES:(k + 1) * LANES] * (inv * inv)
+    which = lax.broadcasted_iota(jnp.int32, (8, LANES), 0)
+    send_val[...] = jnp.where(which == 0, upd_sq, jnp.where(which == 1, row_part, upd_both[:, rows:]))
+    val_copy = swap(3, send_val, recv_val, row_peer)
+    val_copy.start()
+    val_copy.wait()
+    total = jnp.sum(send_val[...] + recv_val[...], axis=1, keepdims=True)
     size = m_total * n_total
-    row_total = pair[1:2, :]
+    row_total = total[1:2, :]
     upd_rms = jnp.sqrt(row_total * total[0:1, :] / size)
     w_rms = jnp.sqrt(total[2:3, :] / size)
     clip = jnp.maximum(1.0, upd_rms / hyper[2:3, 0:1])
@@ -157,8 +160,11 @@
     depth = x_buf.shape[0] // n_step
     rows, cols = out.shape
 
+    def at(k):
+        return k * depth if isinstance(k, int) else pl.multiple_of(k * depth, depth)
+
     def copies(k):
-        band = pl.ds(pl.multiple_of(k * depth, depth), depth)
+        band = pl.ds(at(k), depth)
         return (pltpu.make_async_copy(x_ref.at[band, pl.ds(row_start, rows)], x_buf.at[band, :], x_sem.at[k]),
                 pltpu.make_async_copy(dy_ref.at[band, pl.ds(col_start, cols)], dy_buf.at[band, :], dy_sem.at[k]))
 
@@ -170,7 +176,7 @@
     def multiply(k):
         for copy in copies(k):
             copy.wait()
-        band = pl.ds(pl.multiple_of(k * depth, depth), depth)
+        band = pl.ds(at(k), depth)
         return lax.dot_general(x_buf[band, :], dy_buf[band, :], (((0,), (0,)), ((), ())),
                                preferred_element_type=jnp.float32)
 
@@ -179,8 +185,13 @@
         return carry
 
     lax.fori_loop(0, n_step, begin, 0, unroll=True)
-    out[...] = jnp.zeros_like(out)
-    lax.fori_loop(0, n_step, follow, 0)
+    if rows < 512:
+        out[...] = multiply(0)
+        for k in range(1, n_step):
+            out[...] += multiply(k)
+    else:
+        out[...] = jnp.zeros_like(out)
+        lax.fori_loop(0, n_step, follow, 0)
 
 
 def head_product(x_block, dy_block, row_start, rows, col_start, cols):
@@ -263,9 +274,9 @@
             pltpu.VMEM((rows, LANES), f32),
             pltpu.VMEM((1, rows), f32), pltpu.VMEM((1, cols), f32),
             pltpu.VMEM((1, rows), f32), pltpu.VMEM((1, cols), f32),
-            pltpu.VMEM((8, LANES), f32), pltpu.VMEM((3, 8, LANES), f32),
-            pltpu.SemaphoreType.DMA((2,)), pltpu.SemaphoreType.DMA((2,)),
-            pltpu.SemaphoreType.DMA((3,)), pltpu.SemaphoreType.DMA((3,)),
+            pltpu.VMEM((1, rows + LANES), f32), pltpu.VMEM((1, rows + LANES), f32),
+            pltpu.VMEM((8, LANES), f32), pltpu.VMEM((8, LANES), f32),
+            pltpu.SemaphoreType.DMA((4,)), pltpu.SemaphoreType.DMA((4,)),
         ] + stage,
         compiler_params=pltpu.CompilerParams(collective_id=index, has_side_effects=True,
                                              vmem_limit_bytes=16 * 1024 * 1024 if staged else 6 * 1024 * 1024),

time: 390 us -> 391 us (level)
  transfers between devices with their start and end apart: 8 -> 8, of which waited for: 3 -> 3; matrix products, arithmetic and copies ran while one was open for 10% -> 10% of each run, Pallas kernels for 9% -> 10%
where the time goes in v6:
time: 391 us
  waiting for transfers between devices  223 us (57%)
  matrix products  79 us (20%)
  Pallas kernels  63.3 us (16%)
  starting transfers between devices  13.2 us (3%)
  other arithmetic  7.38 us (2%)
    ppermute x8, waiting for transfers between devices, per_device(): recvs[name].append(lax.ppermute(before, 'dp', SWAP))  223 us
    dot_general x5, matrix products, product(): jnp.einsum('tm,tn->mn', x_block, dy_block, preferred_element_type=jnp.flo...  79 us
    pallas_call x4, Pallas kernels, statistics(): pl.pallas_call(functools.partial(stats_kernel, len(tokens), boxes, near,...  43.4 us
    pallas_call x3, Pallas kernels, head_product(): pl.pallas_call(functools.partial(head_kernel, row_start, col_start), out_...  16.8 us
    ppermute x8, starting transfers between devices, per_device(): recvs[name].append(lax.ppermute(before, 'dp', SWAP))  13.2 us
  transfers between devices with their start and end apart: 8, of which 3 were waited for; matrix products, arithmetic and copies ran while one was open for 10% of the time, Pallas kernels for 10%

profile of v6, /device:TPU:0, one launch (start us, length us, event | category | flops | bytes accessed | tf_op | source)
XLA Modules:
  0.0 390.5 jit_solution(3079942772278880709)
XLA Ops:
  0.6 5.2 %head_product.3.refs_7_ = f32[256,384]{1,0:T(8,128)S(1)} custom-call(bf16[8192,512]{1,0:T(8,128)(2,1)} %x_ref.3, bf16[8192,2048]{1,0:T(8,128)(2,1)} %dy_ref.5), custom_call_target="tpu_custom_call" | custom-call | flops 1610612736 | bytes 10485760 | tf_op jit(solution)/shard_map/head_product/pallas_call | solution.py:200
  5.9 5.2 %head_product.4.refs_8_ = f32[256,384]{1,0:T(8,128)S(1)} custom-call(bf16[8192,512]{1,0:T(8,128)(2,1)} %x_ref.3, bf16[8192,2048]{1,0:T(8,128)(2,1)} %dy_ref.5), custom_call_target="tpu_custom_call" | custom-call | flops 1610612736 | bytes 10485760 | tf_op jit(solution)/shard_map/head_product/pallas_call | solution.py:200
  11.1 6.4 %head_product.5.refs_9_ = f32[512,256]{1,0:T(8,128)} custom-call(bf16[8192,512]{1,0:T(8,128)(2,1)} %x_ref.3, bf16[8192,2048]{1,0:T(8,128)(2,1)} %dy_ref.5), custom_call_target="tpu_custom_call" | custom-call | flops 2147483648 | bytes 12582912 | tf_op jit(solution)/shard_map/head_product/pallas_call | solution.py:200
  17.5 9.0 %fusion.2.refs_10_ = f32[512,384]{1,0:T(8,128)S(1)} fusion(bf16[8192,512]{1,0:T(8,128)(2,1)} %x_ref.3, bf16[8192,2048]{1,0:T(8,128)(2,1)} %dy_ref.5), kind=kOutput, calls=%fused_computation.2 | convolution fusion | flops 3221225472 | bytes 15466496 | tf_op jit(solution)/shard_map/tm,tn->mn/dot_general | solution.py:299
  26.5 14.7 %fusion.refs_11_ = f32[512,1024]{1,0:T(8,128)S(1)} fusion(bf16[8192,512]{1,0:T(8,128)(2,1)} %x_ref.3, bf16[8192,2048]{1,0:T(8,128)(2,1)} %dy_ref.5), kind=kOutput, calls=%fused_computation | convolution fusion | flops 8589934592 | bytes 27262976 | tf_op jit(solution)/shard_map/tm,tn->mn/dot_general | solution.py:299
  41.3 22.2 %fusion.4.refs_0_.refs_7_ = f32[512,2048]{1,0:T(8,128)S(1)} fusion(bf16[8192,512]{1,0:T(8,128)(2,1)S(1)} %bitcast.49, bf16[8192,2048]{1,0:T(8,128)(2,1)} %param.24), kind=kOutput, calls=%fused_computation.11 | convolution fusion | flops 17179869184 | bytes 46137344 | tf_op jit(solution)/shard_map/tm,tn->mn/dot_general | solution.py:299
  63.5 3.4 collective-permute-start.5
  66.9 23.6 %fusion.5.refs_1_.refs_7_ = f32[2048,512]{1,0:T(8,128)S(1)} fusion(bf16[8192,2048]{1,0:T(8,128)(2,1)} %param.25, bf16[8192,512]{1,0:T(8,128)(2,1)} %param.26), kind=kOutput, calls=%fused_computation.12 | convolution fusion | flops 17179869184 | bytes 46137344 | tf_op jit(solution)/shard_map/tm,tn->mn/dot_general | solution.py:299
  90.6 1.5 collective-permute-start.6
  92.6 1.5 collective-permute-start.1
  94.7 9.5 %fusion.6.refs_2_.refs_7_ = f32[512,512]{1,0:T(8,128)S(1)} fusion(bf16[8192,512]{1,0:T(8,128)(2,1)} %param.20, bf16[8192,512]{1,0:T(8,128)(2,1)} %param.21), kind=kOutput, calls=%fused_computation.13 | convolution fusion | flops 4294967296 | bytes 17825792 | tf_op jit(solution)/shard_map/tm,tn->mn/dot_general | solution.py:299
  104.2 0.9 multiply_reduce_fusion.3
  105.2 196.4 %collective-permute-done.1.refs_13_ = f32[256,384]{1,0:T(8,128)S(1)} collective-permute-done((f32[256,384]{1,0:T(8,128)S(1)}, f32[256,384]{1,0:T(8,128)S(1)}, u32[]{:S(2)}, u32[]{:S(2)}) %collective-permute-start.1) | collective-permute-done | bytes 393248 | tf_op jit(solution)/shard_map/ppermute | solution.py:317
  301.5 2.0 collective-permute-start.3
  303.6 1.7 multiply_reduce_fusion.2
  305.2 4.7 %collective-permute-done.refs_12_ = f32[256,384]{1,0:T(8,128)S(1)} collective-permute-done((f32[256,384]{1,0:T(8,128)S(1)}, f32[256,384]{1,0:T(8,128)S(1)}, u32[]{:S(2)}, u32[]{:S(2)}) %collective-permute-start) | collective-permute-done | bytes 393248 | tf_op jit(solution)/shard_map/ppermute | solution.py:317
  310.0 2.0 collective-permute-start.2
  312.0 1.7 multiply_reduce_fusion.1
  313.7 1.7 multiply_reduce_fusion
  315.4 21.9 %collective-permute-done.2.refs_14_ = f32[512,256]{1,0:T(8,128)S(1)} collective-permute-done((f32[512,256]{1,0:T(8,128)S(1)}, f32[512,256]{1,0:T(8,128)S(1)}, u32[]{:S(2)}, u32[]{:S(2)}) %collective-permute-start.2) | collective-permute-done | bytes 524320 | tf_op jit(solution)/shard_map/ppermute | solution.py:317
  337.2 1.7 collective-permute-start.7
  339.1 0.8 copy-done.29
  339.9 0.7 copy-done.27
  340.5 11.1 %shard_map.283 = (f32[512,2048]{1,0:T(8,128)S(1)}, f32[1,512]{1,0:T(1,128)S(1)}, f32[1,512]{1,0:T(1,128)S(1)}, f32[1,2048]{1,0:T(1,128)S(1)}) custom-call(f32[512,2048]{1,0:T(8,128)S(1)} %fusion.4.refs_0_.refs_7_, f32[2048,512]{1,0:T(8,128)S(1)} %fusion.5.refs_1_.refs_7_, f32[512,512]{1,0:T(8,128)S(1)} %fusion.6.refs_2_.refs_7_, f32[1,1]{1,0:T(1,128)} %bitcast.refs_3_, ...), custom_call_target="tpu_custom_call" | custom-call | flops 838860800 | bytes 12582912 | tf_op jit(solution)/shard_map/pallas_call | solution.py:268
  352.9 12.4 %shard_map.284 = (f32[512,2048]{1,0:T(8,128)S(1)}, f32[1,512]{1,0:T(1,128)S(1)}, f32[1,512]{1,0:T(1,128)S(1)}, f32[1,2048]{1,0:T(1,128)S(1)}) custom-call(f32[512,2048]{1,0:T(8,128)S(1)} %multiply_subtract_fusion.2.refs_0_, f32[1,512]{1,0:T(1,128)S(1)} %copy-done.19, f32[1,2048]{1,0:T(1,128)S(1)} %copy-done.11, f32[1,1]{1,0:T(1,128)} %bitcast.4.refs_3_, ...), custom_call_target="tpu_custom_call" | custom-call | flops 838860800 | bytes 12582912 | tf_op jit(solution)/shard_map/pallas_call | solution.py:268
  365.9 0.6 emit.4
  366.5 0.7 copy-done.12
  367.3 0.7 copy-done.20
  368.0 13.2 %shard_map.285 = (f32[2048,512]{1,0:T(8,128)S(1)}, f32[1,2048]{1,0:T(1,128)S(1)}, f32[1,2048]{1,0:T(1,128)S(1)}, f32[1,512]{1,0:T(1,128)S(1)}) custom-call(f32[512,2048]{1,0:T(8,128)S(1)} %multiply_subtract_fusion.1.refs_0_, f32[1,512]{1,0:T(1,128)S(1)} %copy-done.20, f32[1,2048]{1,0:T(1,128)S(1)} %copy-done.12, f32[1,1]{1,0:T(1,128)} %bitcast.8.refs_3_, ...), custom_call_target="tpu_custom_call" | custom-call | flops 838860800 | bytes 12582912 | tf_op jit(solution)/shard_map/pallas_call | solution.py:268
  381.2 0.6 emit.5
  382.5 6.7 %shard_map.286 = (f32[512,512]{1,0:T(8,128)S(1)}, f32[1,128]{1,0:T(1,128)S(1)}, f32[1,512]{1,0:T(1,128)S(1)}, f32[1,512]{1,0:T(1,128)S(1)}) custom-call(f32[2048,512]{1,0:T(8,128)S(1)} %multiply_subtract_fusion.refs_0_, f32[1,2048]{1,0:T(1,128)S(1)} %copy-done.8, f32[1,512]{1,0:T(1,128)S(1)} %copy-done.16, f32[1,1]{1,0:T(1,128)} %bitcast.12.refs_3_, ...), custom_call_target="tpu_custom_call" | custom-call | flops 209715200 | bytes 3145728 | tf_op jit(solution)/shard_map/pallas_call | solution.py:268
  389.3 1.2 finish.1
  (82 shorter events, 3.8 us)
Async XLA Ops:
  17.5 23.7 %slice-start = ((s8[8388608]{0:T(1024)(128)(4,1)}), s8[4194304]{0:T(1024)(128)(4,1)S(1)}, s32[]{:S(2)}) async-start(s8[8388608]{0:T(1024)(128)(4,1)} %bitcast.48), calls=%async_computation | async-start | bytes 8388608
  26.5 275.0 %copy-start.28 = (f32[512,384]{1,0:T(8,128)}, f32[512,384]{1,0:T(8,128)S(1)}, u32[]{:S(2)}) copy-start(f32[512,384]{1,0:T(8,128)S(1)} %fusion.2.refs_10_) | copy-start | bytes 2359300
  26.5 14.7 %slice-start.1 = ((s8[8388608]{0:T(1024)(128)(4,1)}), s8[4194304]{0:T(1024)(128)(4,1)S(1)}, s32[]{:S(2)}) async-start(s8[8388608]{0:T(1024)(128)(4,1)} %bitcast.48), calls=%async_computation.1 | async-start | bytes 8388608
  41.3 50.8 %copy-start.26 = (f32[512,1024]{1,0:T(8,128)}, f32[512,1024]{1,0:T(8,128)S(1)}, u32[]{:S(2)}) copy-start(f32[512,1024]{1,0:T(8,128)S(1)} %fusion.refs_11_) | copy-start | bytes 6291460
  63.5 275.5 %copy-start.4 = (f32[512,2048]{1,0:T(8,128)}, f32[512,2048]{1,0:T(8,128)S(1)}, u32[]{:S(2)}) copy-start(f32[512,2048]{1,0:T(8,128)S(1)} %fusion.4.refs_0_.refs_7_) | copy-start | bytes 12582916
  63.5 289.2 %collective-permute-start.5 = (f32[512,2048]{1,0:T(8,128)S(1)}, f32[512,2048]{1,0:T(8,128)}, u32[]{:S(2)}, u32[]{:S(2)}) collective-permute-start(f32[512,2048]{1,0:T(8,128)S(1)} %fusion.4.refs_0_.refs_7_), channel_id=1, source_target_pairs={{0,4},{4,0},{1,5},{5,1},{2,6},{6,2},{3,7},{7,3}} | collective-permute-start | bytes 12582920 | tf_op jit(solution)/shard_map/ppermute | solution.py:317
  90.5 248.5 %copy-start.3 = (f32[2048,512]{1,0:T(8,128)}, f32[2048,512]{1,0:T(8,128)S(1)}, u32[]{:S(2)}) copy-start(f32[2048,512]{1,0:T(8,128)S(1)} %fusion.5.refs_1_.refs_7_) | copy-start | bytes 12582916
  90.5 13.6 %copy-start.33 = (f32[3]{0:T(128)S(1)}, f32[3]{0:T(128)}, u32[]{:S(2)}) copy-start(f32[3]{0:T(128)} %param.39) | copy-start | bytes 40
  90.5 13.7 %copy-start.5 = (f32[512,512]{1,0:T(8,128)S(1)}, f32[512,512]{1,0:T(8,128)}, u32[]{:S(2)}) copy-start(f32[512,512]{1,0:T(8,128)} %weight.1) | copy-start | bytes 3145732
  90.6 213.0 %copy-start.21 = (f32[512,2048]{1,0:T(8,128)S(1)}, f32[512,2048]{1,0:T(8,128)}, u32[]{:S(2)}) copy-start(f32[512,2048]{1,0:T(8,128)} %param.28) | copy-start | bytes 12582916
  90.6 219.4 %copy-start.6 = (f32[512,256]{1,0:T(8,128)S(1)}, f32[512,256]{1,0:T(8,128)}, u32[]{:S(2)}) copy-start(f32[512,256]{1,0:T(8,128)} %head_product.5.refs_9_) | copy-start | bytes 1572868
  90.6 275.9 %collective-permute-start.6 = (f32[2048,512]{1,0:T(8,128)S(1)}, f32[2048,512]{1,0:T(8,128)}, u32[]{:S(2)}, u32[]{:S(2)}) collective-permute-start(f32[2048,512]{1,0:T(8,128)S(1)} %fusion.5.refs_1_.refs_7_), channel_id=1, source_target_pairs={{0,4},{4,0},{1,5},{5,1},{2,6},{6,2},{3,7},{7,3}} | collective-permute-start | bytes 12582920 | tf_op jit(solution)/shard_map/ppermute | solution.py:317
  92.1 246.9 %collective-permute-start.4 = (f32[512,1024]{1,0:T(8,128)S(1)}, f32[512,1024]{1,0:T(8,128)S(1)}, u32[]{:S(2)}, u32[]{:S(2)}) collective-permute-start(f32[512,1024]{1,0:T(8,128)S(1)} %fusion.refs_11_), channel_id=1, source_target_pairs={{0,4},{4,0},{1,5},{5,1},{2,6},{6,2},{3,7},{7,3}} | collective-permute-start | bytes 6291464 | tf_op jit(solution)/shard_map/ppermute | solution.py:317
  92.6 208.9 %collective-permute-start.1 = (f32[256,384]{1,0:T(8,128)S(1)}, f32[256,384]{1,0:T(8,128)S(1)}, u32[]{:S(2)}, u32[]{:S(2)}) collective-permute-start(f32[256,384]{1,0:T(8,128)S(1)} %head_product.4.refs_8_), channel_id=1, source_target_pairs={{0,4},{4,0},{1,5},{5,1},{2,6},{6,2},{3,7},{7,3}} | collective-permute-start | bytes 1179656 | tf_op jit(solution)/shard_map/ppermute | solution.py:317
  94.1 215.9 %collective-permute-start = (f32[256,384]{1,0:T(8,128)S(1)}, f32[256,384]{1,0:T(8,128)S(1)}, u32[]{:S(2)}, u32[]{:S(2)}) collective-permute-start(f32[256,384]{1,0:T(8,128)S(1)} %head_product.3.refs_7_), channel_id=1, source_target_pairs={{0,4},{4,0},{1,5},{5,1},{2,6},{6,2},{3,7},{7,3}} | collective-permute-start | bytes 1179656 | tf_op jit(solution)/shard_map/ppermute | solution.py:317
  104.2 207.8 %copy-start.22 = (f32[512,2048]{1,0:T(8,128)S(1)}, f32[512,2048]{1,0:T(8,128)}, u32[]{:S(2)}) copy-start(f32[512,2048]{1,0:T(8,128)} %param.29) | copy-start | bytes 12582916
  104.2 209.5 %copy-start.24 = (f32[2048,512]{1,0:T(8,128)S(1)}, f32[2048,512]{1,0:T(8,128)}, u32[]{:S(2)}) copy-start(f32[2048,512]{1,0:T(8,128)} %param.30) | copy-start | bytes 12582916
  105.2 235.4 %copy-start.7 = (f32[2048]{0:T(1024)S(1)}, f32[2048]{0:T(1024)}, u32[]{:S(2)}) copy-start(f32[2048]{0:T(1024)} %param.34) | copy-start | bytes 24580
  105.2 235.4 %copy-start.13 = (f32[512]{0:T(512)S(1)}, f32[512]{0:T(512)}, u32[]{:S(2)}) copy-start(f32[512]{0:T(512)} %param.33) | copy-start | bytes 6148
  301.5 13.8 %copy-start.31 = (f32[256,384]{1,0:T(8,128)}, f32[256,384]{1,0:T(8,128)S(1)}, u32[]{:S(2)}) copy-start(f32[256,384]{1,0:T(8,128)S(1)} %collective-permute-done.1.refs_13_) | copy-start | bytes 1179652
  301.5 37.4 %collective-permute-start.3 = (f32[512,384]{1,0:T(8,128)S(1)}, f32[512,384]{1,0:T(8,128)S(1)}, u32[]{:S(2)}, u32[]{:S(2)}) collective-permute-start(f32[512,384]{1,0:T(8,128)S(1)} %fusion.2.refs_10_), channel_id=1, source_target_pairs={{0,4},{4,0},{1,5},{5,1},{2,6},{6,2},{3,7},{7,3}} | collective-permute-start | bytes 2359304 | tf_op jit(solution)/shard_map/ppermute | solution.py:317
  310.0 29.1 %copy-start.32 = (f32[256,384]{1,0:T(8,128)}, f32[256,384]{1,0:T(8,128)S(1)}, u32[]{:S(2)}) copy-start(f32[256,384]{1,0:T(8,128)S(1)} %collective-permute-done.refs_12_) | copy-start | bytes 1179652
  310.0 27.2 %collective-permute-start.2 = (f32[512,256]{1,0:T(8,128)S(1)}, f32[512,256]{1,0:T(8,128)S(1)}, u32[]{:S(2)}, u32[]{:S(2)}) collective-permute-start(f32[512,256]{1,0:T(8,128)S(1)} %copy-done.6), channel_id=1, source_target_pairs={{0,4},{4,0},{1,5},{5,1},{2,6},{6,2},{3,7},{7,3}} | collective-permute-start | bytes 1572872 | tf_op jit(solution)/shard_map/ppermute | solution.py:317
  337.2 1.8 copy-start.30
  337.2 45.1 %collective-permute-start.7 = (f32[512,512]{1,0:T(8,128)S(1)}, f32[512,512]{1,0:T(8,128)S(1)}, u32[]{:S(2)}, u32[]{:S(2)}) collective-permute-start(f32[512,512]{1,0:T(8,128)S(1)} %fusion.6.refs_2_.refs_7_), channel_id=1, source_target_pairs={{0,4},{4,0},{1,5},{5,1},{2,6},{6,2},{3,7},{7,3}} | collective-permute-start | bytes 3145736 | tf_op jit(solution)/shard_map/ppermute | solution.py:317
  339.0 1.6 copy-start.27
  352.7 12.7 %copy-start = (f32[512,2048]{1,0:T(8,128)}, f32[512,2048]{1,0:T(8,128)S(1)}, u32[]{:S(2)}) copy-start(f32[512,2048]{1,0:T(8,128)S(1)} %multiply_subtract_fusion.2.refs_0_) | copy-start | bytes 12582916
  352.9 12.4 %copy-start.23 = (f32[512,2048]{1,0:T(8,128)S(1)}, f32[512,2048]{1,0:T(8,128)}, u32[]{:S(2)}) copy-start(f32[512,2048]{1,0:T(8,128)} %param.29) | copy-start | bytes 12582916
  365.4 1.2 copy-start.10
  365.9 15.3 %copy-start.1 = (f32[512,2048]{1,0:T(8,128)}, f32[512,2048]{1,0:T(8,128)S(1)}, u32[]{:S(2)}) copy-start(f32[512,2048]{1,0:T(8,128)S(1)} %multiply_subtract_fusion.1.refs_0_) | copy-start | bytes 12582916
  368.0 13.8 %copy-start.25 = (f32[2048,512]{1,0:T(8,128)S(1)}, f32[2048,512]{1,0:T(8,128)}, u32[]{:S(2)}) copy-start(f32[2048,512]{1,0:T(8,128)} %param.30) | copy-start | bytes 12582916
  382.3 8.2 %copy-start.2 = (f32[2048,512]{1,0:T(8,128)}, f32[2048,512]{1,0:T(8,128)S(1)}, u32[]{:S(2)}) copy-start(f32[2048,512]{1,0:T(8,128)S(1)} %multiply_subtract_fusion.refs_0_) | copy-start | bytes 12582916
  (12 other events, 9.2 us)

commit v7 on v6

--- a/solution.py
+++ b/solution.py
@@ -12,8 +12,11 @@
 MESH = pl.DeviceIdType.MESH
 LANES = 128
 NAMES = ('gate', 'up', 'down', 'attn')
-GATE_BOXES = ((0, 0, 256, 384), (256, 0, 256, 384), (0, 384, 512, 256), (0, 640, 512, 384), (0, 1024, 512, 1024))
-N_HEAD = 3
+GATE_BOXES = ((0, 0, 256, 256), (256, 0, 256, 256), (0, 256, 256, 256), (256, 256, 256, 256),
+              (0, 512, 512, 256), (0, 768, 512, 256), (0, 1024, 512, 384), (0, 1408, 512, 640))
+N_HEAD = 6
+N_NEAR = 4
+WAVE = 4
 HEAD_LIMIT = 58 * 1024 * 1024
 
 
@@ -82,14 +85,14 @@
 
     col_acc = lax.fori_loop(0, rows // step, first, jnp.zeros((8, cols), jnp.float32))
     send_col[...] = jnp.sum(col_acc, axis=0, keepdims=True)
+    pl.semaphore_wait(barrier, 2)
+    row_copy = swap(0, send_row, recv_row, col_peer)
+    col_copy = swap(1, send_col, recv_col, row_peer)
+    col_copy.start()
     for k in range(rows // LANES):
         tile = row_acc[k * LANES:(k + 1) * LANES, :].T
         send_row[:, k * LANES:(k + 1) * LANES] = jnp.sum(tile, axis=0, keepdims=True)
-    pl.semaphore_wait(barrier, 2)
-    row_copy = swap(0, send_row, recv_row, col_peer)
-    col_copy = swap(1, send_col, recv_col, row_peer)
     row_copy.start()
-    col_copy.start()
     beta_two = hyper[0:1, 0:1]
 
     col_copy.wait()
@@ -168,29 +171,37 @@
         return (pltpu.make_async_copy(x_ref.at[band, pl.ds(row_start, rows)], x_buf.at[band, :], x_sem.at[k]),
                 pltpu.make_async_copy(dy_ref.at[band, pl.ds(col_start, cols)], dy_buf.at[band, :], dy_sem.at[k]))
 
-    def begin(k, carry):
+    def begin(k):
         for copy in copies(k):
             copy.start()
-        return carry
-
-    def multiply(k):
+
+    def multiply(k, add):
         for copy in copies(k):
             copy.wait()
         band = pl.ds(at(k), depth)
-        return lax.dot_general(x_buf[band, :], dy_buf[band, :], (((0,), (0,)), ((), ())),
+        term = lax.dot_general(x_buf[band, :], dy_buf[band, :], (((0,), (0,)), ((), ())),
                                preferred_element_type=jnp.float32)
-
-    def follow(k, carry):
-        out[...] += multiply(k)
-        return carry
-
-    lax.fori_loop(0, n_step, begin, 0, unroll=True)
+        if add:
+            out[...] += term
+        else:
+            out[...] = term
+
     if rows < 512:
-        out[...] = multiply(0)
-        for k in range(1, n_step):
-            out[...] += multiply(k)
+        for k in range(WAVE):
+            begin(k)
+        for k in range(n_step):
+            multiply(k, k > 0)
+            if k + WAVE < n_step:
+                begin(k + WAVE)
     else:
+        for k in range(n_step):
+            begin(k)
         out[...] = jnp.zeros_like(out)
+
+        def follow(k, carry):
+            multiply(k, True)
+            return carry
+
         lax.fori_loop(0, n_step, follow, 0)
 
 
@@ -204,7 +215,7 @@
         out_specs=pl.BlockSpec(memory_space=pltpu.VMEM),
         scratch_shapes=[pltpu.VMEM((tokens, rows), x_block.dtype), pltpu.VMEM((tokens, cols), dy_block.dtype),
                         pltpu.SemaphoreType.DMA((8,)), pltpu.SemaphoreType.DMA((8,))],
-        compiler_params=pltpu.CompilerParams(vmem_limit_bytes=HEAD_LIMIT if col_start else 14 * 1024 * 1024),
+        compiler_params=pltpu.CompilerParams(vmem_limit_bytes=HEAD_LIMIT if rows == 512 else 14 * 1024 * 1024),
         cost_estimate=pl.CostEstimate(flops=2 * tokens * rows * cols, bytes_accessed=2 * tokens * (rows + cols),
                                       transcendentals=0),
         name="head_product",
@@ -229,21 +240,31 @@
     )(*values)
 
 
-def finish_kernel(weight, update, factor, row_in, col_in, new_weight, new_row, new_col):
-    new_row[...] = row_in[...]
-    new_col[...] = col_in[...]
+def finish_kernel(weight, update, factor, row_in, col_in, new_weight, new_row, new_col, buf, sem):
+    copies = [pltpu.make_async_copy(row_in, new_row, sem.at[0]), pltpu.make_async_copy(col_in, new_col, sem.at[1])]
+    for copy in copies:
+        copy.start()
     scale = factor[...]
-    for j in range(weight.shape[1] // LANES):
-        lanes = pl.ds(j * LANES, LANES)
-        new_weight[:, lanes] = weight[:, lanes] - update[:, lanes] * scale
+    depth = weight.shape[0] // 4
+    for k in range(4):
+        band = pl.ds(k * depth, depth)
+        for j in range(weight.shape[1] // LANES):
+            lanes = pl.ds(j * LANES, LANES)
+            buf[band, lanes] = weight[band, lanes] - update[band, lanes] * scale
+        copies.append(pltpu.make_async_copy(buf.at[band, :], new_weight.at[band, :], sem.at[2 + k]))
+        copies[-1].start()
+    for copy in copies:
+        copy.wait()
 
 
 def finish(weight, update, factor, new_row, new_col):
     vmem = pl.BlockSpec(memory_space=pltpu.VMEM)
+    anyw = pl.BlockSpec(memory_space=pl.ANY)
     return pl.pallas_call(
         finish_kernel,
         out_shape=[jax.ShapeDtypeStruct(v.shape, v.dtype) for v in (weight, new_row, new_col)],
-        in_specs=[vmem] * 5, out_specs=[vmem] * 3,
+        in_specs=[vmem] * 5, out_specs=[anyw] * 3,
+        scratch_shapes=[pltpu.VMEM(weight.shape, weight.dtype), pltpu.SemaphoreType.DMA((6,))],
         cost_estimate=pl.CostEstimate(flops=100000, bytes_accessed=12 * weight.size, transcendentals=0),
         compiler_params=pltpu.CompilerParams(vmem_limit_bytes=6 * 1024 * 1024),
         name="finish",
@@ -326,7 +347,7 @@
             rows, cols = weight.shape
             grad, row_scale, new_row, new_col = statistics(
                 tokens, tuple(b[:2] for b in GATE_BOXES) if name == 'gate' else ((0, 0),),
-                N_HEAD if name == 'gate' else 0, parts[name], recvs[name],
+                N_NEAR if name == 'gate' else 0, parts[name], recvs[name],
                 jnp.sum(weight * weight), *stats[name], hyper_rows, index)
             if index < 3:
                 new_weight = weight - grad * row_scale.reshape(rows, 1)

time: 391 us -> 387 us (0.990)
  waiting for transfers between devices: 223 us -> 208 us
  Pallas kernels: 63.3 us -> 75.4 us
    ppermute x8 -> x11, waiting for transfers between devices: 223 us -> 208 us  [per_device(): recvs[name].append(lax.ppermute(before, 'dp', SWAP))]
    pallas_call x3 -> x6, Pallas kernels: 16.8 us -> 29.7 us  [head_product(): pl.pallas_call(functools.partial(head_kernel, row_start, col_start), out_...]
    ppermute x8 -> x11, starting transfers between devices: 13.2 us -> 12 us  [per_device(): recvs[name].append(lax.ppermute(before, 'dp', SWAP))]
  transfers between devices with their start and end apart: 8 -> 11, of which waited for: 3 -> 2; matrix products, arithmetic and copies ran while one was open for 10% -> 22% of each run, Pallas kernels for 10% -> 15%
where the time goes in v7:
time: 387 us; the launch traced here: 386 us
  waiting for transfers between devices  208 us (54%)
  matrix products  78.5 us (20%)
  Pallas kernels  75.4 us (19%)
  starting transfers between devices  12 us (3%)
  other arithmetic  7.55 us (2%)
    ppermute x11, waiting for transfers between devices, per_device(): recvs[name].append(lax.ppermute(before, 'dp', SWAP))  208 us
    dot_general x5, matrix products, product(): jnp.einsum('tm,tn->mn', x_block, dy_block, preferred_element_type=jnp.flo...  78.5 us
    pallas_call x4, Pallas kernels, statistics(): pl.pallas_call(functools.partial(stats_kernel, len(tokens), boxes, near,...  42.8 us
    pallas_call x6, Pallas kernels, head_product(): pl.pallas_call(functools.partial(head_kernel, row_start, col_start), out_...  29.7 us
    ppermute x11, starting transfers between devices, per_device(): recvs[name].append(lax.ppermute(before, 'dp', SWAP))  12 us
  transfers between devices with their start and end apart: 11, of which 2 were waited for; matrix products, arithmetic and copies ran while one was open for 22% of the time, Pallas kernels for 15%

profile of v7, /device:TPU:0, one launch (start us, length us, event | category | flops | bytes accessed | tf_op | source)
XLA Modules:
  0.0 386.2 jit_solution(15000736997551780308)
XLA Ops:
  0.6 4.3 %head_product.6.refs_7_ = f32[256,256]{1,0:T(8,128)S(1)} custom-call(bf16[8192,512]{1,0:T(8,128)(2,1)} %x_ref.6, bf16[8192,2048]{1,0:T(8,128)(2,1)} %dy_ref.11), custom_call_target="tpu_custom_call" | custom-call | flops 1073741824 | bytes 8388608 | tf_op jit(solution)/shard_map/head_product/pallas_call | solution.py:211
  5.0 4.3 %head_product.7.refs_8_ = f32[256,256]{1,0:T(8,128)S(1)} custom-call(bf16[8192,512]{1,0:T(8,128)(2,1)} %x_ref.6, bf16[8192,2048]{1,0:T(8,128)(2,1)} %dy_ref.11), custom_call_target="tpu_custom_call" | custom-call | flops 1073741824 | bytes 8388608 | tf_op jit(solution)/shard_map/head_product/pallas_call | solution.py:211
  9.3 3.4 collective-permute-start.1
  12.6 4.3 %head_product.8.refs_9_ = f32[256,256]{1,0:T(8,128)S(1)} custom-call(bf16[8192,512]{1,0:T(8,128)(2,1)} %x_ref.6, bf16[8192,2048]{1,0:T(8,128)(2,1)} %dy_ref.11), custom_call_target="tpu_custom_call" | custom-call | flops 1073741824 | bytes 8388608 | tf_op jit(solution)/shard_map/head_product/pallas_call | solution.py:211
  17.0 4.3 %head_product.9.refs_10_ = f32[256,256]{1,0:T(8,128)S(1)} custom-call(bf16[8192,512]{1,0:T(8,128)(2,1)} %x_ref.6, bf16[8192,2048]{1,0:T(8,128)(2,1)} %dy_ref.11), custom_call_target="tpu_custom_call" | custom-call | flops 1073741824 | bytes 8388608 | tf_op jit(solution)/shard_map/head_product/pallas_call | solution.py:211
  21.3 2.0 collective-permute-start.3
  23.3 6.2 %head_product.10.refs_11_ = f32[512,256]{1,0:T(8,128)} custom-call(bf16[8192,512]{1,0:T(8,128)(2,1)} %x_ref.6, bf16[8192,2048]{1,0:T(8,128)(2,1)} %dy_ref.11), custom_call_target="tpu_custom_call" | custom-call | flops 2147483648 | bytes 12582912 | tf_op jit(solution)/shard_map/head_product/pallas_call | solution.py:211
  29.5 6.2 %head_product.11.refs_12_ = f32[512,256]{1,0:T(8,128)} custom-call(bf16[8192,512]{1,0:T(8,128)(2,1)} %x_ref.6, bf16[8192,2048]{1,0:T(8,128)(2,1)} %dy_ref.11), custom_call_target="tpu_custom_call" | custom-call | flops 2147483648 | bytes 12582912 | tf_op jit(solution)/shard_map/head_product/pallas_call | solution.py:211
  35.8 9.0 %fusion.2.refs_13_ = f32[512,384]{1,0:T(8,128)S(1)} fusion(bf16[8192,512]{1,0:T(8,128)(2,1)} %x_ref.6, bf16[8192,2048]{1,0:T(8,128)(2,1)} %dy_ref.11), kind=kOutput, calls=%fused_computation.2 | convolution fusion | flops 3221225472 | bytes 15466496 | tf_op jit(solution)/shard_map/tm,tn->mn/dot_general | solution.py:320
  44.8 13.3 %fusion.refs_14_ = f32[512,640]{1,0:T(8,128)} fusion(bf16[8192,512]{1,0:T(8,128)(2,1)} %x_ref.6, bf16[8192,2048]{1,0:T(8,128)(2,1)} %dy_ref.11), kind=kOutput, calls=%fused_computation | convolution fusion | flops 5368709120 | bytes 20185088 | tf_op jit(solution)/shard_map/tm,tn->mn/dot_general | solution.py:320
  58.1 21.5 %fusion.4.refs_0_.refs_7_ = f32[512,2048]{1,0:T(8,128)S(1)} fusion(bf16[8192,512]{1,0:T(8,128)(2,1)S(1)} %bitcast.49, bf16[8192,2048]{1,0:T(8,128)(2,1)} %param.24), kind=kOutput, calls=%fused_computation.11 | convolution fusion | flops 17179869184 | bytes 46137344 | tf_op jit(solution)/shard_map/tm,tn->mn/dot_general | solution.py:320
  79.7 25.3 %fusion.5.refs_1_.refs_7_ = f32[2048,512]{1,0:T(8,128)S(1)} fusion(bf16[8192,2048]{1,0:T(8,128)(2,1)} %param.25, bf16[8192,512]{1,0:T(8,128)(2,1)} %param.26), kind=kOutput, calls=%fused_computation.12 | convolution fusion | flops 17179869184 | bytes 46137344 | tf_op jit(solution)/shard_map/tm,tn->mn/dot_general | solution.py:320
  105.4 1.6 collective-permute-start.7
  107.4 1.6 collective-permute-start
  109.1 9.5 %fusion.6.refs_2_.refs_7_ = f32[512,512]{1,0:T(8,128)S(1)} fusion(bf16[8192,512]{1,0:T(8,128)(2,1)} %param.20, bf16[8192,512]{1,0:T(8,128)(2,1)} %param.21), kind=kOutput, calls=%fused_computation.13 | convolution fusion | flops 4294967296 | bytes 17825792 | tf_op jit(solution)/shard_map/tm,tn->mn/dot_general | solution.py:320
  118.7 0.9 multiply_reduce_fusion.3
  119.6 186.4 %collective-permute-done.refs_15_ = f32[256,256]{1,0:T(8,128)S(1)} collective-permute-done((f32[256,256]{1,0:T(8,128)S(1)}, f32[256,256]{1,0:T(8,128)S(1)}, u32[]{:S(2)}, u32[]{:S(2)}) %collective-permute-start) | collective-permute-done | bytes 262176 | tf_op jit(solution)/shard_map/ppermute | solution.py:338
  306.2 1.7 multiply_reduce_fusion.2
  307.9 1.7 collective-permute-start.4
  309.7 1.7 multiply_reduce_fusion.1
  311.3 1.7 multiply_reduce_fusion
  313.0 21.9 %collective-permute-done.4.refs_19_ = f32[512,256]{1,0:T(8,128)S(1)} collective-permute-done((f32[512,256]{1,0:T(8,128)S(1)}, f32[512,256]{1,0:T(8,128)S(1)}, u32[]{:S(2)}, u32[]{:S(2)}) %collective-permute-start.4) | collective-permute-done | bytes 524320 | tf_op jit(solution)/shard_map/ppermute | solution.py:338
  336.7 11.1 %shard_map.283 = (f32[512,2048]{1,0:T(8,128)S(1)}, f32[1,512]{1,0:T(1,128)S(1)}, f32[1,512]{1,0:T(1,128)S(1)}, f32[1,2048]{1,0:T(1,128)S(1)}) custom-call(f32[512,2048]{1,0:T(8,128)S(1)} %fusion.4.refs_0_.refs_7_, f32[2048,512]{1,0:T(8,128)S(1)} %fusion.5.refs_1_.refs_7_, f32[512,512]{1,0:T(8,128)S(1)} %fusion.6.refs_2_.refs_7_, f32[1,1]{1,0:T(1,128)} %bitcast.refs_3_, ...), custom_call_target="tpu_custom_call" | custom-call | flops 838860800 | bytes 12582912 | tf_op jit(solution)/shard_map/pallas_call | solution.py:289
  349.1 12.2 %shard_map.284 = (f32[512,2048]{1,0:T(8,128)S(1)}, f32[1,512]{1,0:T(1,128)S(1)}, f32[1,512]{1,0:T(1,128)S(1)}, f32[1,2048]{1,0:T(1,128)S(1)}) custom-call(f32[512,2048]{1,0:T(8,128)S(1)} %multiply_subtract_fusion.2.refs_0_, f32[1,512]{1,0:T(1,128)S(1)} %copy-done.18, f32[1,2048]{1,0:T(1,128)S(1)} %copy-done.10, f32[1,1]{1,0:T(1,128)} %bitcast.4.refs_3_, ...), custom_call_target="tpu_custom_call" | custom-call | flops 838860800 | bytes 12582912 | tf_op jit(solution)/shard_map/pallas_call | solution.py:289
  361.9 0.6 emit.4
  362.6 0.7 copy-done.11
  363.3 0.7 copy-done.19
  364.0 12.8 %shard_map.285 = (f32[2048,512]{1,0:T(8,128)S(1)}, f32[1,2048]{1,0:T(1,128)S(1)}, f32[1,2048]{1,0:T(1,128)S(1)}, f32[1,512]{1,0:T(1,128)S(1)}) custom-call(f32[512,2048]{1,0:T(8,128)S(1)} %multiply_subtract_fusion.1.refs_0_, f32[1,512]{1,0:T(1,128)S(1)} %copy-done.19, f32[1,2048]{1,0:T(1,128)S(1)} %copy-done.11, f32[1,1]{1,0:T(1,128)} %bitcast.8.refs_3_, ...), custom_call_target="tpu_custom_call" | custom-call | flops 838860800 | bytes 12582912 | tf_op jit(solution)/shard_map/pallas_call | solution.py:289
  376.9 0.6 emit.5
  377.5 0.7 multiply_subtract_fusion.refs_0_
  378.3 6.7 %shard_map.286 = (f32[512,512]{1,0:T(8,128)S(1)}, f32[1,128]{1,0:T(1,128)S(1)}, f32[1,512]{1,0:T(1,128)S(1)}, f32[1,512]{1,0:T(1,128)S(1)}) custom-call(f32[2048,512]{1,0:T(8,128)S(1)} %multiply_subtract_fusion.refs_0_, f32[1,2048]{1,0:T(1,128)S(1)} %copy-done.7, f32[1,512]{1,0:T(1,128)S(1)} %copy-done.15, f32[1,1]{1,0:T(1,128)} %bitcast.12.refs_3_, ...), custom_call_target="tpu_custom_call" | custom-call | flops 209715200 | bytes 3145728 | tf_op jit(solution)/shard_map/pallas_call | solution.py:289
  384.9 1.1 finish.1
  (91 shorter events, 4.8 us)
Async XLA Ops:
  9.3 98.2 %collective-permute-start.1 = (f32[256,256]{1,0:T(8,128)S(1)}, f32[256,256]{1,0:T(8,128)}, u32[]{:S(2)}, u32[]{:S(2)}) collective-permute-start(f32[256,256]{1,0:T(8,128)S(1)} %head_product.7.refs_8_), channel_id=1, source_target_pairs={{0,4},{4,0},{1,5},{5,1},{2,6},{6,2},{3,7},{7,3}} | collective-permute-start | bytes 786440 | tf_op jit(solution)/shard_map/ppermute | solution.py:338
  17.0 90.1 %collective-permute-start.2 = (f32[256,256]{1,0:T(8,128)S(1)}, f32[256,256]{1,0:T(8,128)}, u32[]{:S(2)}, u32[]{:S(2)}) collective-permute-start(f32[256,256]{1,0:T(8,128)S(1)} %head_product.8.refs_9_), channel_id=1, source_target_pairs={{0,4},{4,0},{1,5},{5,1},{2,6},{6,2},{3,7},{7,3}} | collective-permute-start | bytes 786440 | tf_op jit(solution)/shard_map/ppermute | solution.py:338
  21.3 84.1 %collective-permute-start.3 = (f32[256,256]{1,0:T(8,128)S(1)}, f32[256,256]{1,0:T(8,128)}, u32[]{:S(2)}, u32[]{:S(2)}) collective-permute-start(f32[256,256]{1,0:T(8,128)S(1)} %head_product.9.refs_10_), channel_id=1, source_target_pairs={{0,4},{4,0},{1,5},{5,1},{2,6},{6,2},{3,7},{7,3}} | collective-permute-start | bytes 786440 | tf_op jit(solution)/shard_map/ppermute | solution.py:338
  35.8 22.4 %slice-start = ((s8[8388608]{0:T(1024)(128)(4,1)}), s8[4194304]{0:T(1024)(128)(4,1)S(1)}, s32[]{:S(2)}) async-start(s8[8388608]{0:T(1024)(128)(4,1)} %bitcast.48), calls=%async_computation | async-start | bytes 8388608
  44.8 261.2 %copy-start.28 = (f32[512,384]{1,0:T(8,128)}, f32[512,384]{1,0:T(8,128)S(1)}, u32[]{:S(2)}) copy-start(f32[512,384]{1,0:T(8,128)S(1)} %fusion.2.refs_13_) | copy-start | bytes 2359300
  44.8 13.4 %slice-start.1 = ((s8[8388608]{0:T(1024)(128)(4,1)}), s8[4194304]{0:T(1024)(128)(4,1)S(1)}, s32[]{:S(2)}) async-start(s8[8388608]{0:T(1024)(128)(4,1)} %bitcast.48), calls=%async_computation.1 | async-start | bytes 8388608
  79.6 255.8 %copy-start.4 = (f32[512,2048]{1,0:T(8,128)}, f32[512,2048]{1,0:T(8,128)S(1)}, u32[]{:S(2)}) copy-start(f32[512,2048]{1,0:T(8,128)S(1)} %fusion.4.refs_0_.refs_7_) | copy-start | bytes 12582916
  79.6 27.4 %copy-start.26 = (f32[512,256]{1,0:T(8,128)S(1)}, f32[512,256]{1,0:T(8,128)}, u32[]{:S(2)}) copy-start(f32[512,256]{1,0:T(8,128)} %head_product.11.refs_12_) | copy-start | bytes 1572868
  79.6 269.3 %collective-permute-start.8 = (f32[512,2048]{1,0:T(8,128)S(1)}, f32[512,2048]{1,0:T(8,128)}, u32[]{:S(2)}, u32[]{:S(2)}) collective-permute-start(f32[512,2048]{1,0:T(8,128)S(1)} %fusion.4.refs_0_.refs_7_), channel_id=1, source_target_pairs={{0,4},{4,0},{1,5},{5,1},{2,6},{6,2},{3,7},{7,3}} | collective-permute-start | bytes 12582920 | tf_op jit(solution)/shard_map/ppermute | solution.py:338
  104.9 230.5 %copy-start.3 = (f32[2048,512]{1,0:T(8,128)}, f32[2048,512]{1,0:T(8,128)S(1)}, u32[]{:S(2)}) copy-start(f32[2048,512]{1,0:T(8,128)S(1)} %fusion.5.refs_1_.refs_7_) | copy-start | bytes 12582916
  105.0 13.6 %copy-start.33 = (f32[3]{0:T(128)S(1)}, f32[3]{0:T(128)}, u32[]{:S(2)}) copy-start(f32[3]{0:T(128)} %param.39) | copy-start | bytes 40
  105.0 13.7 %copy-start.5 = (f32[512,512]{1,0:T(8,128)S(1)}, f32[512,512]{1,0:T(8,128)}, u32[]{:S(2)}) copy-start(f32[512,512]{1,0:T(8,128)} %weight.1) | copy-start | bytes 3145732
  105.0 201.3 %copy-start.20 = (f32[512,2048]{1,0:T(8,128)S(1)}, f32[512,2048]{1,0:T(8,128)}, u32[]{:S(2)}) copy-start(f32[512,2048]{1,0:T(8,128)} %param.28) | copy-start | bytes 12582916
  105.0 202.9 %copy-start.25 = (f32[512,256]{1,0:T(8,128)S(1)}, f32[512,256]{1,0:T(8,128)}, u32[]{:S(2)}) copy-start(f32[512,256]{1,0:T(8,128)} %head_product.10.refs_11_) | copy-start | bytes 1572868
  105.0 257.5 %collective-permute-start.9 = (f32[2048,512]{1,0:T(8,128)S(1)}, f32[2048,512]{1,0:T(8,128)}, u32[]{:S(2)}, u32[]{:S(2)}) collective-permute-start(f32[2048,512]{1,0:T(8,128)S(1)} %fusion.5.refs_1_.refs_7_), channel_id=1, source_target_pairs={{0,4},{4,0},{1,5},{5,1},{2,6},{6,2},{3,7},{7,3}} | collective-permute-start | bytes 12582920 | tf_op jit(solution)/shard_map/ppermute | solution.py:338
  105.4 229.9 %collective-permute-start.7 = (f32[512,640]{1,0:T(8,128)}, f32[512,640]{1,0:T(8,128)S(1)}, u32[]{:S(2)}, u32[]{:S(2)}) collective-permute-start(f32[512,640]{1,0:T(8,128)} %fusion.refs_14_), channel_id=1, source_target_pairs={{0,4},{4,0},{1,5},{5,1},{2,6},{6,2},{3,7},{7,3}} | collective-permute-start | bytes 3932168 | tf_op jit(solution)/shard_map/ppermute | solution.py:338
  107.1 200.9 %collective-permute-start.5 = (f32[512,256]{1,0:T(8,128)S(1)}, f32[512,256]{1,0:T(8,128)S(1)}, u32[]{:S(2)}, u32[]{:S(2)}) collective-permute-start(f32[512,256]{1,0:T(8,128)S(1)} %copy-done.26), channel_id=1, source_target_pairs={{0,4},{4,0},{1,5},{5,1},{2,6},{6,2},{3,7},{7,3}} | collective-permute-start | bytes 1572872 | tf_op jit(solution)/shard_map/ppermute | solution.py:338
  107.4 198.5 %collective-permute-start = (f32[256,256]{1,0:T(8,128)S(1)}, f32[256,256]{1,0:T(8,128)S(1)}, u32[]{:S(2)}, u32[]{:S(2)}) collective-permute-start(f32[256,256]{1,0:T(8,128)S(1)} %head_product.6.refs_7_), channel_id=1, source_target_pairs={{0,4},{4,0},{1,5},{5,1},{2,6},{6,2},{3,7},{7,3}} | collective-permute-start | bytes 786440 | tf_op jit(solution)/shard_map/ppermute | solution.py:338
  118.6 191.1 %copy-start.21 = (f32[512,2048]{1,0:T(8,128)S(1)}, f32[512,2048]{1,0:T(8,128)}, u32[]{:S(2)}) copy-start(f32[512,2048]{1,0:T(8,128)} %param.29) | copy-start | bytes 12582916
  118.6 192.7 %copy-start.23 = (f32[2048,512]{1,0:T(8,128)S(1)}, f32[2048,512]{1,0:T(8,128)}, u32[]{:S(2)}) copy-start(f32[2048,512]{1,0:T(8,128)} %param.30) | copy-start | bytes 12582916
  119.6 217.1 %copy-start.6 = (f32[2048]{0:T(1024)S(1)}, f32[2048]{0:T(1024)}, u32[]{:S(2)}) copy-start(f32[2048]{0:T(1024)} %param.34) | copy-start | bytes 24580
  119.6 217.1 %copy-start.12 = (f32[512]{0:T(512)S(1)}, f32[512]{0:T(512)}, u32[]{:S(2)}) copy-start(f32[512]{0:T(512)} %param.33) | copy-start | bytes 6148
  305.9 7.1 %copy-start.32 = (f32[256,256]{1,0:T(8,128)}, f32[256,256]{1,0:T(8,128)S(1)}, u32[]{:S(2)}) copy-start(f32[256,256]{1,0:T(8,128)S(1)} %collective-permute-done.refs_15_) | copy-start | bytes 786436
  305.9 29.4 %collective-permute-start.6 = (f32[512,384]{1,0:T(8,128)S(1)}, f32[512,384]{1,0:T(8,128)S(1)}, u32[]{:S(2)}, u32[]{:S(2)}) collective-permute-start(f32[512,384]{1,0:T(8,128)S(1)} %fusion.2.refs_13_), channel_id=1, source_target_pairs={{0,4},{4,0},{1,5},{5,1},{2,6},{6,2},{3,7},{7,3}} | collective-permute-start | bytes 2359304 | tf_op jit(solution)/shard_map/ppermute | solution.py:338
  307.9 27.5 %copy-start.30 = (f32[512,256]{1,0:T(8,128)}, f32[512,256]{1,0:T(8,128)S(1)}, u32[]{:S(2)}) copy-start(f32[512,256]{1,0:T(8,128)S(1)} %collective-permute-done.5.refs_20_) | copy-start | bytes 1572868
  307.9 27.0 %collective-permute-start.4 = (f32[512,256]{1,0:T(8,128)S(1)}, f32[512,256]{1,0:T(8,128)S(1)}, u32[]{:S(2)}, u32[]{:S(2)}) collective-permute-start(f32[512,256]{1,0:T(8,128)S(1)} %copy-done.25), channel_id=1, source_target_pairs={{0,4},{4,0},{1,5},{5,1},{2,6},{6,2},{3,7},{7,3}} | collective-permute-start | bytes 1572872 | tf_op jit(solution)/shard_map/ppermute | solution.py:338
  334.9 43.3 %collective-permute-start.10 = (f32[512,512]{1,0:T(8,128)S(1)}, f32[512,512]{1,0:T(8,128)S(1)}, u32[]{:S(2)}, u32[]{:S(2)}) collective-permute-start(f32[512,512]{1,0:T(8,128)S(1)} %fusion.6.refs_2_.refs_7_), channel_id=1, source_target_pairs={{0,4},{4,0},{1,5},{5,1},{2,6},{6,2},{3,7},{7,3}} | collective-permute-start | bytes 3145736 | tf_op jit(solution)/shard_map/ppermute | solution.py:338
  348.9 12.5 %copy-start = (f32[512,2048]{1,0:T(8,128)}, f32[512,2048]{1,0:T(8,128)S(1)}, u32[]{:S(2)}) copy-start(f32[512,2048]{1,0:T(8,128)S(1)} %multiply_subtract_fusion.2.refs_0_) | copy-start | bytes 12582916
  349.1 12.2 %copy-start.22 = (f32[512,2048]{1,0:T(8,128)S(1)}, f32[512,2048]{1,0:T(8,128)}, u32[]{:S(2)}) copy-start(f32[512,2048]{1,0:T(8,128)} %param.29) | copy-start | bytes 12582916
  361.9 15.0 %copy-start.1 = (f32[512,2048]{1,0:T(8,128)}, f32[512,2048]{1,0:T(8,128)S(1)}, u32[]{:S(2)}) copy-start(f32[512,2048]{1,0:T(8,128)S(1)} %multiply_subtract_fusion.1.refs_0_) | copy-start | bytes 12582916
  364.0 13.5 %copy-start.24 = (f32[2048,512]{1,0:T(8,128)S(1)}, f32[2048,512]{1,0:T(8,128)}, u32[]{:S(2)}) copy-start(f32[2048,512]{1,0:T(8,128)} %param.30) | copy-start | bytes 12582916
  378.2 7.8 %copy-start.2 = (f32[2048,512]{1,0:T(8,128)}, f32[2048,512]{1,0:T(8,128)S(1)}, u32[]{:S(2)}) copy-start(f32[2048,512]{1,0:T(8,128)S(1)} %multiply_subtract_fusion.refs_0_) | copy-start | bytes 12582916
  (15 other events, 12.6 us)

commit v8 on v7

--- a/solution.py
+++ b/solution.py
@@ -16,8 +16,8 @@
               (0, 512, 512, 256), (0, 768, 512, 256), (0, 1024, 512, 384), (0, 1408, 512, 640))
 N_HEAD = 6
 N_NEAR = 4
-WAVE = 4
-HEAD_LIMIT = 58 * 1024 * 1024
+MIB = 1024 * 1024
+HEAD_LIMIT = 50 * MIB
 
 
 def peers():
@@ -158,44 +158,48 @@
         row_scale[...] = row_inv * factor
 
 
-def head_kernel(row_start, col_start, x_ref, dy_ref, out, x_buf, dy_buf, x_sem, dy_sem):
-    n_step = x_sem.shape[0]
-    depth = x_buf.shape[0] // n_step
-    rows, cols = out.shape
-
-    def at(k):
-        return k * depth if isinstance(k, int) else pl.multiple_of(k * depth, depth)
+def head_kernel(row_start, col_start, n_x, *refs):
+    refs = list(refs)
+    x_bufs = [refs.pop(0) for _ in range(n_x)]
+    dy_buf = refs.pop(0)
+    out = refs.pop(0)
+    loads = []
+    if row_start is not None:
+        source, x_bufs = x_bufs[0], [refs.pop(0)]
+        loads.append((source, row_start, x_bufs[0]))
+    if col_start is not None:
+        source, dy_buf = dy_buf, refs.pop(0)
+        loads.append((source, col_start, dy_buf))
+    sem = refs.pop(0) if loads else None
+    n_step = 8
+    depth = dy_buf.shape[0] // n_step
+    rows = x_bufs[0].shape[1]
 
     def copies(k):
-        band = pl.ds(at(k), depth)
-        return (pltpu.make_async_copy(x_ref.at[band, pl.ds(row_start, rows)], x_buf.at[band, :], x_sem.at[k]),
-                pltpu.make_async_copy(dy_ref.at[band, pl.ds(col_start, cols)], dy_buf.at[band, :], dy_sem.at[k]))
-
-    def begin(k):
-        for copy in copies(k):
-            copy.start()
+        band = pl.ds(k * depth if isinstance(k, int) else pl.multiple_of(k * depth, depth), depth)
+        return [pltpu.make_async_copy(source.at[band, pl.ds(start, buf.shape[1])], buf.at[band, :], sem.at[j, k])
+                for j, (source, start, buf) in enumerate(loads)]
 
     def multiply(k, add):
         for copy in copies(k):
             copy.wait()
-        band = pl.ds(at(k), depth)
-        term = lax.dot_general(x_buf[band, :], dy_buf[band, :], (((0,), (0,)), ((), ())),
-                               preferred_element_type=jnp.float32)
-        if add:
-            out[...] += term
-        else:
-            out[...] = term
-
-    if rows < 512:
-        for k in range(WAVE):
-            begin(k)
+        band = pl.ds(k * depth if isinstance(k, int) else pl.multiple_of(k * depth, depth), depth)
+        for j, x_buf in enumerate(x_bufs):
+            own = pl.ds(j * rows, rows)
+            term = lax.dot_general(x_buf[band, :], dy_buf[band, :], (((0,), (0,)), ((), ())),
+                                   preferred_element_type=jnp.float32)
+            if add:
+                out[own, :] += term
+            else:
+                out[own, :] = term
+
+    for k in range(n_step):
+        for copy in copies(k):
+            copy.start()
+    if n_x == 1:
         for k in range(n_step):
             multiply(k, k > 0)
-            if k + WAVE < n_step:
-                begin(k + WAVE)
     else:
-        for k in range(n_step):
-            begin(k)
         out[...] = jnp.zeros_like(out)
 
         def follow(k, carry):
@@ -205,21 +209,32 @@
         lax.fori_loop(0, n_step, follow, 0)
 
 
-def head_product(x_block, dy_block, row_start, rows, col_start, cols):
-    tokens = x_block.shape[0]
+def head_product(x_blocks, dy_block, row_start, col_start, keep, limit):
+    tokens = dy_block.shape[0]
+    n_x = len(x_blocks)
+    rows = 256 * n_x
+    vmem = pl.BlockSpec(memory_space=pltpu.VMEM)
     anyw = pl.BlockSpec(memory_space=pl.ANY)
+    x_far, dy_far = row_start is not None, col_start is not None
+    held = jax.ShapeDtypeStruct((tokens, 256), dy_block.dtype)
+    outs = [jax.ShapeDtypeStruct((rows, 256), jnp.float32)] + [held] * (x_far + (dy_far and keep))
+    scratch = [pltpu.VMEM((tokens, 256), dy_block.dtype)] * (dy_far and not keep)
+    if x_far or dy_far:
+        scratch.append(pltpu.SemaphoreType.DMA((x_far + dy_far, 8)))
+    far = [x_far] * n_x + [dy_far]
+    operands = [pltpu.with_memory_space_constraint(v, pltpu.HBM if f else pltpu.VMEM)
+                for v, f in zip(list(x_blocks) + [dy_block], far)]
     return pl.pallas_call(
-        functools.partial(head_kernel, row_start, col_start),
-        out_shape=jax.ShapeDtypeStruct((rows, cols), jnp.float32),
-        in_specs=[anyw, anyw],
-        out_specs=pl.BlockSpec(memory_space=pltpu.VMEM),
-        scratch_shapes=[pltpu.VMEM((tokens, rows), x_block.dtype), pltpu.VMEM((tokens, cols), dy_block.dtype),
-                        pltpu.SemaphoreType.DMA((8,)), pltpu.SemaphoreType.DMA((8,))],
-        compiler_params=pltpu.CompilerParams(vmem_limit_bytes=HEAD_LIMIT if rows == 512 else 14 * 1024 * 1024),
-        cost_estimate=pl.CostEstimate(flops=2 * tokens * rows * cols, bytes_accessed=2 * tokens * (rows + cols),
+        functools.partial(head_kernel, row_start, col_start, n_x),
+        out_shape=outs,
+        in_specs=[anyw if f else vmem for f in far],
+        out_specs=[vmem] * len(outs),
+        scratch_shapes=scratch,
+        compiler_params=pltpu.CompilerParams(vmem_limit_bytes=limit),
+        cost_estimate=pl.CostEstimate(flops=2 * tokens * rows * 256, bytes_accessed=2 * tokens * 256 * sum(far),
                                       transcendentals=0),
         name="head_product",
-    )(pltpu.with_memory_space_constraint(x_block, pltpu.HBM), pltpu.with_memory_space_constraint(dy_block, pltpu.HBM))
+    )(*operands)
 
 
 def emit_kernel(*refs):
@@ -287,7 +302,7 @@
     halves = [pltpu.with_memory_space_constraint(v, space) for v, space in zip(parts + recvs, spaces)]
     shapes = ((rows, cols), (1, rows if staged else LANES), (1, rows), (1, cols))
     return pl.pallas_call(
-        functools.partial(stats_kernel, len(tokens), boxes, near, not staged, 16, 2 * rows, 2 * cols),
+        functools.partial(stats_kernel, len(tokens), boxes, near, not staged, 16 if staged else 64, 2 * rows, 2 * cols),
         out_shape=[jax.ShapeDtypeStruct(s, f32) for s in shapes],
         in_specs=[anyw] * len(tokens) + [smem] + [vmem] * 3 + places,
         out_specs=[vmem] * 4,
@@ -325,12 +340,29 @@
         order += [('up', x_mlp, dy_up, None), ('down', h_mlp, dy_out, None), ('attn', x_attn, dy_attn, None)]
         parts = {name: [] for name in NAMES}
         recvs = {name: [] for name in NAMES}
+        held = {}
+
+        def head(held, number, x_block, dy_block):
+            if number == 0:
+                part, held['x0'], held['dy0'] = head_product([x_block], dy_block, 0, 0, True, 14 * MIB)
+            elif number == 1:
+                part, held['x1'] = head_product([x_block], held['dy0'], 256, None, True, 14 * MIB)
+            elif number == 2:
+                part, held['dy1'] = head_product([held['x0']], dy_block, None, 256, True, 14 * MIB)
+            elif number == 3:
+                part, = head_product([held['x1']], held['dy1'], None, None, True, 14 * MIB)
+            else:
+                part, = head_product([held['x0'], held['x1']], dy_block, None, GATE_BOXES[number][1], False, HEAD_LIMIT)
+            return part
+
         before = None
         for number, (name, x_block, dy_block, box) in enumerate(order):
-            if before is not None:
+            if before is not None and number < N_HEAD:
+                x_block, dy_block, held, before = lax.optimization_barrier((x_block, dy_block, held, before))
+            elif before is not None:
                 x_block, before = lax.optimization_barrier((x_block, before))
             if number < N_HEAD:
-                before = head_product(x_block, dy_block, box[0], box[2], box[1], box[3])
+                before = head(held, number, x_block, dy_block)
             elif box is not None:
                 before = product(x_block, dy_block[:, box[1]:box[1] + box[3]])
             else:

time: 387 us -> 385 us (level)
  Pallas kernels: 75.4 us -> 70.5 us
    pallas_call x6, Pallas kernels: 29.7 us -> 25 us  [head_product(): pl.pallas_call(functools.partial(head_kernel, row_start, col_start, n_x),...]
  transfers between devices with their start and end apart: 11 -> 11, of which waited for: 2 -> 2; matrix products, arithmetic and copies ran while one was open for 22% -> 23% of each run, Pallas kernels for 15% -> 14%
where the time goes in v8:
time: 385 us
  waiting for transfers between devices  208 us (54%)
  matrix products  81.9 us (21%)
  Pallas kernels  70.5 us (18%)
  starting transfers between devices  12.1 us (3%)
  other arithmetic  7.28 us (2%)
    ppermute x11, waiting for transfers between devices, per_device(): recvs[name].append(lax.ppermute(before, 'dp', SWAP))  208 us
    dot_general x5, matrix products, product(): jnp.einsum('tm,tn->mn', x_block, dy_block, preferred_element_type=jnp.flo...  81.9 us
    pallas_call x4, Pallas kernels, statistics(): pl.pallas_call(functools.partial(stats_kernel, len(tokens), boxes, near,...  42.7 us
    pallas_call x6, Pallas kernels, head_product(): pl.pallas_call(functools.partial(head_kernel, row_start, col_start, n_x),...  25 us
    ppermute x11, starting transfers between devices, per_device(): recvs[name].append(lax.ppermute(before, 'dp', SWAP))  12.1 us
  transfers between devices with their start and end apart: 11, of which 2 were waited for; matrix products, arithmetic and copies ran while one was open for 23% of the time, Pallas kernels for 14%

profile of v8, /device:TPU:0, one launch (start us, length us, event | category | flops | bytes accessed | tf_op | source)
XLA Modules:
  0.0 384.6 jit_solution(7834428917716212207)
XLA Ops:
  0.6 4.2 %head_product.6 = (f32[256,256]{1,0:T(8,128)S(1)}, bf16[8192,256]{1,0:T(8,128)(2,1)S(1)}, bf16[8192,256]{1,0:T(8,128)(2,1)S(1)}) custom-call(bf16[8192,512]{1,0:T(8,128)(2,1)} %refs_0_.2, bf16[8192,2048]{1,0:T(8,128)(2,1)} %refs_2_.1), custom_call_target="tpu_custom_call" | custom-call | flops 1073741824 | bytes 8388608 | tf_op jit(solution)/shard_map/head_product/pallas_call | solution.py:227
  4.8 4.0 %head_product.7 = (f32[256,256]{1,0:T(8,128)S(1)}, bf16[8192,256]{1,0:T(8,128)(2,1)S(1)}) custom-call(bf16[8192,512]{1,0:T(8,128)(2,1)} %refs_0_.2, bf16[8192,256]{1,0:T(8,128)(2,1)S(1)} %get-tuple-element.67.refs_1_), custom_call_target="tpu_custom_call" | custom-call | flops 1073741824 | bytes 4194304 | tf_op jit(solution)/shard_map/head_product/pallas_call | solution.py:227
  8.8 3.4 collective-permute-start.1
  12.2 3.9 %head_product.8 = (f32[256,256]{1,0:T(8,128)S(1)}, bf16[8192,256]{1,0:T(8,128)(2,1)S(1)}) custom-call(bf16[8192,256]{1,0:T(8,128)(2,1)S(1)} %get-tuple-element.83.refs_0_, bf16[8192,2048]{1,0:T(8,128)(2,1)} %refs_2_.1), custom_call_target="tpu_custom_call" | custom-call | flops 1073741824 | bytes 4194304 | tf_op jit(solution)/shard_map/head_product/pallas_call | solution.py:227
  16.2 1.3 head_product.9.refs_10_
  17.4 2.0 collective-permute-start.3
  19.5 5.8 %head_product.10.refs_11_ = f32[512,256]{1,0:T(8,128)} custom-call(bf16[8192,256]{1,0:T(8,128)(2,1)S(1)} %get-tuple-element.83.refs_0_, bf16[8192,256]{1,0:T(8,128)(2,1)S(1)} %get-tuple-element.84.refs_0_.refs_1_, bf16[8192,2048]{1,0:T(8,128)(2,1)} %refs_2_.1), custom_call_target="tpu_custom_call" | custom-call | flops 2147483648 | bytes 4194304 | tf_op jit(solution)/shard_map/head_product/pallas_call | solution.py:227
  25.3 5.8 %head_product.11.refs_12_ = f32[512,256]{1,0:T(8,128)} custom-call(bf16[8192,256]{1,0:T(8,128)(2,1)S(1)} %get-tuple-element.83.refs_0_, bf16[8192,256]{1,0:T(8,128)(2,1)S(1)} %get-tuple-element.84.refs_0_.refs_1_, bf16[8192,2048]{1,0:T(8,128)(2,1)} %refs_2_.1), custom_call_target="tpu_custom_call" | custom-call | flops 2147483648 | bytes 4194304 | tf_op jit(solution)/shard_map/head_product/pallas_call | solution.py:227
  31.1 9.0 %fusion.2.refs_13_ = f32[512,384]{1,0:T(8,128)S(1)} fusion(bf16[8192,512]{1,0:T(8,128)(2,1)} %refs_0_.2, bf16[8192,2048]{1,0:T(8,128)(2,1)} %refs_2_.1), kind=kOutput, calls=%fused_computation.2 | convolution fusion | flops 3221225472 | bytes 15466496 | tf_op jit(solution)/shard_map/tm,tn->mn/dot_general | solution.py:335
  40.1 16.2 %fusion.refs_14_ = f32[512,640]{1,0:T(8,128)S(1)} fusion(bf16[8192,512]{1,0:T(8,128)(2,1)} %refs_0_.2, bf16[8192,2048]{1,0:T(8,128)(2,1)} %refs_2_.1), kind=kOutput, calls=%fused_computation | convolution fusion | flops 5368709120 | bytes 20185088 | tf_op jit(solution)/shard_map/tm,tn->mn/dot_general | solution.py:335
  56.3 21.9 %fusion.4.refs_0_.refs_7_ = f32[512,2048]{1,0:T(8,128)S(1)} fusion(bf16[8192,512]{1,0:T(8,128)(2,1)S(1)} %bitcast.49, bf16[8192,2048]{1,0:T(8,128)(2,1)} %param.24), kind=kOutput, calls=%fused_computation.11 | convolution fusion | flops 17179869184 | bytes 46137344 | tf_op jit(solution)/shard_map/tm,tn->mn/dot_general | solution.py:335
  78.3 25.3 %fusion.5.refs_1_.refs_7_ = f32[2048,512]{1,0:T(8,128)S(1)} fusion(bf16[8192,2048]{1,0:T(8,128)(2,1)} %param.25, bf16[8192,512]{1,0:T(8,128)(2,1)} %param.26), kind=kOutput, calls=%fused_computation.12 | convolution fusion | flops 17179869184 | bytes 46137344 | tf_op jit(solution)/shard_map/tm,tn->mn/dot_general | solution.py:335
  104.1 1.7 collective-permute-start.7
  106.1 1.6 collective-permute-start
  107.8 9.5 %fusion.6.refs_2_.refs_7_ = f32[512,512]{1,0:T(8,128)S(1)} fusion(bf16[8192,512]{1,0:T(8,128)(2,1)} %param.20, bf16[8192,512]{1,0:T(8,128)(2,1)} %param.21), kind=kOutput, calls=%fused_computation.13 | convolution fusion | flops 4294967296 | bytes 17825792 | tf_op jit(solution)/shard_map/tm,tn->mn/dot_general | solution.py:335
  117.4 0.8 multiply_reduce_fusion.3
  118.2 186.4 %collective-permute-done.refs_15_ = f32[256,256]{1,0:T(8,128)S(1)} collective-permute-done((f32[256,256]{1,0:T(8,128)S(1)}, f32[256,256]{1,0:T(8,128)S(1)}, u32[]{:S(2)}, u32[]{:S(2)}) %collective-permute-start) | collective-permute-done | bytes 262176 | tf_op jit(solution)/shard_map/ppermute | solution.py:370
  304.9 1.7 multiply_reduce_fusion.2
  306.6 1.7 collective-permute-start.4
  308.4 1.7 multiply_reduce_fusion.1
  310.0 1.7 multiply_reduce_fusion
  311.7 21.8 %collective-permute-done.4.refs_19_ = f32[512,256]{1,0:T(8,128)S(1)} collective-permute-done((f32[512,256]{1,0:T(8,128)S(1)}, f32[512,256]{1,0:T(8,128)S(1)}, u32[]{:S(2)}, u32[]{:S(2)}) %collective-permute-start.4) | collective-permute-done | bytes 524320 | tf_op jit(solution)/shard_map/ppermute | solution.py:370
  335.4 11.1 %shard_map.283 = (f32[512,2048]{1,0:T(8,128)S(1)}, f32[1,512]{1,0:T(1,128)S(1)}, f32[1,512]{1,0:T(1,128)S(1)}, f32[1,2048]{1,0:T(1,128)S(1)}) custom-call(f32[512,2048]{1,0:T(8,128)S(1)} %fusion.4.refs_0_.refs_7_, f32[2048,512]{1,0:T(8,128)S(1)} %fusion.5.refs_1_.refs_7_, f32[512,512]{1,0:T(8,128)S(1)} %fusion.6.refs_2_.refs_7_, f32[1,1]{1,0:T(1,128)} %bitcast.refs_3_, ...), custom_call_target="tpu_custom_call" | custom-call | flops 838860800 | bytes 12582912 | tf_op jit(solution)/shard_map/pallas_call | solution.py:304
  346.5 0.6 emit.3
  347.8 12.2 %shard_map.284 = (f32[512,2048]{1,0:T(8,128)S(1)}, f32[1,512]{1,0:T(1,128)S(1)}, f32[1,512]{1,0:T(1,128)S(1)}, f32[1,2048]{1,0:T(1,128)S(1)}) custom-call(f32[512,2048]{1,0:T(8,128)S(1)} %multiply_subtract_fusion.2.refs_0_, f32[1,512]{1,0:T(1,128)S(1)} %copy-done.18, f32[1,2048]{1,0:T(1,128)S(1)} %copy-done.10, f32[1,1]{1,0:T(1,128)} %bitcast.4.refs_3_, ...), custom_call_target="tpu_custom_call" | custom-call | flops 838860800 | bytes 12582912 | tf_op jit(solution)/shard_map/pallas_call | solution.py:304
  360.6 0.6 emit.4
  361.2 0.7 copy-done.11
  362.0 0.7 copy-done.19
  362.7 12.8 %shard_map.285 = (f32[2048,512]{1,0:T(8,128)S(1)}, f32[1,2048]{1,0:T(1,128)S(1)}, f32[1,2048]{1,0:T(1,128)S(1)}, f32[1,512]{1,0:T(1,128)S(1)}) custom-call(f32[512,2048]{1,0:T(8,128)S(1)} %multiply_subtract_fusion.1.refs_0_, f32[1,512]{1,0:T(1,128)S(1)} %copy-done.19, f32[1,2048]{1,0:T(1,128)S(1)} %copy-done.11, f32[1,1]{1,0:T(1,128)} %bitcast.8.refs_3_, ...), custom_call_target="tpu_custom_call" | custom-call | flops 838860800 | bytes 12582912 | tf_op jit(solution)/shard_map/pallas_call | solution.py:304
  375.5 0.6 emit.5
  376.9 6.5 %shard_map.286 = (f32[512,512]{1,0:T(8,128)S(1)}, f32[1,128]{1,0:T(1,128)S(1)}, f32[1,512]{1,0:T(1,128)S(1)}, f32[1,512]{1,0:T(1,128)S(1)}) custom-call(f32[2048,512]{1,0:T(8,128)S(1)} %multiply_subtract_fusion.refs_0_, f32[1,2048]{1,0:T(1,128)S(1)} %copy-done.7, f32[1,512]{1,0:T(1,128)S(1)} %copy-done.15, f32[1,1]{1,0:T(1,128)} %bitcast.12.refs_3_, ...), custom_call_target="tpu_custom_call" | custom-call | flops 209715200 | bytes 3145728 | tf_op jit(solution)/shard_map/pallas_call | solution.py:304
  383.4 1.1 finish.1
  (99 shorter events, 5.0 us)
Async XLA Ops:
  8.8 97.3 %collective-permute-start.1 = (f32[256,256]{1,0:T(8,128)S(1)}, f32[256,256]{1,0:T(8,128)S(1)}, u32[]{:S(2)}, u32[]{:S(2)}) collective-permute-start(f32[256,256]{1,0:T(8,128)S(1)} %get-tuple-element.71.refs_8_), channel_id=1, source_target_pairs={{0,4},{4,0},{1,5},{5,1},{2,6},{6,2},{3,7},{7,3}} | collective-permute-start | bytes 786440 | tf_op jit(solution)/shard_map/ppermute | solution.py:370
  16.1 89.6 %collective-permute-start.2 = (f32[256,256]{1,0:T(8,128)S(1)}, f32[256,256]{1,0:T(8,128)S(1)}, u32[]{:S(2)}, u32[]{:S(2)}) collective-permute-start(f32[256,256]{1,0:T(8,128)S(1)} %get-tuple-element.76.refs_9_), channel_id=1, source_target_pairs={{0,4},{4,0},{1,5},{5,1},{2,6},{6,2},{3,7},{7,3}} | collective-permute-start | bytes 786440 | tf_op jit(solution)/shard_map/ppermute | solution.py:370
  17.4 86.6 %collective-permute-start.3 = (f32[256,256]{1,0:T(8,128)S(1)}, f32[256,256]{1,0:T(8,128)S(1)}, u32[]{:S(2)}, u32[]{:S(2)}) collective-permute-start(f32[256,256]{1,0:T(8,128)S(1)} %head_product.9.refs_10_), channel_id=1, source_target_pairs={{0,4},{4,0},{1,5},{5,1},{2,6},{6,2},{3,7},{7,3}} | collective-permute-start | bytes 786440 | tf_op jit(solution)/shard_map/ppermute | solution.py:370
  31.1 25.2 %slice-start = ((s8[8388608]{0:T(1024)(128)(4,1)}), s8[4194304]{0:T(1024)(128)(4,1)S(1)}, s32[]{:S(2)}) async-start(s8[8388608]{0:T(1024)(128)(4,1)} %bitcast.48), calls=%async_computation | async-start | bytes 8388608
  40.1 264.5 %copy-start.29 = (f32[512,384]{1,0:T(8,128)}, f32[512,384]{1,0:T(8,128)S(1)}, u32[]{:S(2)}) copy-start(f32[512,384]{1,0:T(8,128)S(1)} %fusion.2.refs_13_) | copy-start | bytes 2359300
  40.1 16.2 %slice-start.1 = ((s8[8388608]{0:T(1024)(128)(4,1)}), s8[4194304]{0:T(1024)(128)(4,1)S(1)}, s32[]{:S(2)}) async-start(s8[8388608]{0:T(1024)(128)(4,1)} %bitcast.48), calls=%async_computation.1 | async-start | bytes 8388608
  56.3 47.7 %copy-start.27 = (f32[512,640]{1,0:T(8,128)}, f32[512,640]{1,0:T(8,128)S(1)}, u32[]{:S(2)}) copy-start(f32[512,640]{1,0:T(8,128)S(1)} %fusion.refs_14_) | copy-start | bytes 3932164
  78.3 255.8 %copy-start.4 = (f32[512,2048]{1,0:T(8,128)}, f32[512,2048]{1,0:T(8,128)S(1)}, u32[]{:S(2)}) copy-start(f32[512,2048]{1,0:T(8,128)S(1)} %fusion.4.refs_0_.refs_7_) | copy-start | bytes 12582916
  78.3 27.5 %copy-start.26 = (f32[512,256]{1,0:T(8,128)S(1)}, f32[512,256]{1,0:T(8,128)}, u32[]{:S(2)}) copy-start(f32[512,256]{1,0:T(8,128)} %head_product.11.refs_12_) | copy-start | bytes 1572868
  78.3 269.3 %collective-permute-start.8 = (f32[512,2048]{1,0:T(8,128)S(1)}, f32[512,2048]{1,0:T(8,128)}, u32[]{:S(2)}, u32[]{:S(2)}) collective-permute-start(f32[512,2048]{1,0:T(8,128)S(1)} %fusion.4.refs_0_.refs_7_), channel_id=1, source_target_pairs={{0,4},{4,0},{1,5},{5,1},{2,6},{6,2},{3,7},{7,3}} | collective-permute-start | bytes 12582920 | tf_op jit(solution)/shard_map/ppermute | solution.py:370
  103.6 230.5 %copy-start.3 = (f32[2048,512]{1,0:T(8,128)}, f32[2048,512]{1,0:T(8,128)S(1)}, u32[]{:S(2)}) copy-start(f32[2048,512]{1,0:T(8,128)S(1)} %fusion.5.refs_1_.refs_7_) | copy-start | bytes 12582916
  103.6 13.7 %copy-start.37 = (f32[3]{0:T(128)S(1)}, f32[3]{0:T(128)}, u32[]{:S(2)}) copy-start(f32[3]{0:T(128)} %param.39) | copy-start | bytes 40
  103.6 13.7 %copy-start.5 = (f32[512,512]{1,0:T(8,128)S(1)}, f32[512,512]{1,0:T(8,128)}, u32[]{:S(2)}) copy-start(f32[512,512]{1,0:T(8,128)} %weight.1) | copy-start | bytes 3145732
  103.7 201.3 %copy-start.20 = (f32[512,2048]{1,0:T(8,128)S(1)}, f32[512,2048]{1,0:T(8,128)}, u32[]{:S(2)}) copy-start(f32[512,2048]{1,0:T(8,128)} %param.28) | copy-start | bytes 12582916
  103.7 257.6 %collective-permute-start.9 = (f32[2048,512]{1,0:T(8,128)S(1)}, f32[2048,512]{1,0:T(8,128)}, u32[]{:S(2)}, u32[]{:S(2)}) collective-permute-start(f32[2048,512]{1,0:T(8,128)S(1)} %fusion.5.refs_1_.refs_7_), channel_id=1, source_target_pairs={{0,4},{4,0},{1,5},{5,1},{2,6},{6,2},{3,7},{7,3}} | collective-permute-start | bytes 12582920 | tf_op jit(solution)/shard_map/ppermute | solution.py:370
  104.1 13.2 %copy-start.35 = (f32[256,256]{1,0:T(8,128)}, f32[256,256]{1,0:T(8,128)S(1)}, u32[]{:S(2)}) copy-start(f32[256,256]{1,0:T(8,128)S(1)} %collective-permute-done.3.refs_18_) | copy-start | bytes 786436
  104.1 230.0 %collective-permute-start.7 = (f32[512,640]{1,0:T(8,128)S(1)}, f32[512,640]{1,0:T(8,128)S(1)}, u32[]{:S(2)}, u32[]{:S(2)}) collective-permute-start(f32[512,640]{1,0:T(8,128)S(1)} %fusion.refs_14_), channel_id=1, source_target_pairs={{0,4},{4,0},{1,5},{5,1},{2,6},{6,2},{3,7},{7,3}} | collective-permute-start | bytes 3932168 | tf_op jit(solution)/shard_map/ppermute | solution.py:370
  105.7 11.6 %copy-start.34 = (f32[256,256]{1,0:T(8,128)}, f32[256,256]{1,0:T(8,128)S(1)}, u32[]{:S(2)}) copy-start(f32[256,256]{1,0:T(8,128)S(1)} %collective-permute-done.2.refs_17_) | copy-start | bytes 786436
  105.7 200.9 %collective-permute-start.5 = (f32[512,256]{1,0:T(8,128)S(1)}, f32[512,256]{1,0:T(8,128)S(1)}, u32[]{:S(2)}, u32[]{:S(2)}) collective-permute-start(f32[512,256]{1,0:T(8,128)S(1)} %copy-done.26), channel_id=1, source_target_pairs={{0,4},{4,0},{1,5},{5,1},{2,6},{6,2},{3,7},{7,3}} | collective-permute-start | bytes 1572872 | tf_op jit(solution)/shard_map/ppermute | solution.py:370
  106.1 198.5 %collective-permute-start = (f32[256,256]{1,0:T(8,128)S(1)}, f32[256,256]{1,0:T(8,128)S(1)}, u32[]{:S(2)}, u32[]{:S(2)}) collective-permute-start(f32[256,256]{1,0:T(8,128)S(1)} %get-tuple-element.66.refs_7_), channel_id=1, source_target_pairs={{0,4},{4,0},{1,5},{5,1},{2,6},{6,2},{3,7},{7,3}} | collective-permute-start | bytes 786440 | tf_op jit(solution)/shard_map/ppermute | solution.py:370
  117.3 189.3 %copy-start.25 = (f32[512,256]{1,0:T(8,128)S(1)}, f32[512,256]{1,0:T(8,128)}, u32[]{:S(2)}) copy-start(f32[512,256]{1,0:T(8,128)} %head_product.10.refs_11_) | copy-start | bytes 1572868
  117.4 191.0 %copy-start.21 = (f32[512,2048]{1,0:T(8,128)S(1)}, f32[512,2048]{1,0:T(8,128)}, u32[]{:S(2)}) copy-start(f32[512,2048]{1,0:T(8,128)} %param.29) | copy-start | bytes 12582916
  118.2 191.8 %copy-start.23 = (f32[2048,512]{1,0:T(8,128)S(1)}, f32[2048,512]{1,0:T(8,128)}, u32[]{:S(2)}) copy-start(f32[2048,512]{1,0:T(8,128)} %param.30) | copy-start | bytes 12582916
  304.6 29.4 %collective-permute-start.6 = (f32[512,384]{1,0:T(8,128)S(1)}, f32[512,384]{1,0:T(8,128)S(1)}, u32[]{:S(2)}, u32[]{:S(2)}) collective-permute-start(f32[512,384]{1,0:T(8,128)S(1)} %fusion.2.refs_13_), channel_id=1, source_target_pairs={{0,4},{4,0},{1,5},{5,1},{2,6},{6,2},{3,7},{7,3}} | collective-permute-start | bytes 2359304 | tf_op jit(solution)/shard_map/ppermute | solution.py:370
  306.6 28.8 %copy-start.6 = (f32[2048]{0:T(1024)S(1)}, f32[2048]{0:T(1024)}, u32[]{:S(2)}) copy-start(f32[2048]{0:T(1024)} %param.34) | copy-start | bytes 24580
  306.6 28.8 %copy-start.12 = (f32[512]{0:T(512)S(1)}, f32[512]{0:T(512)}, u32[]{:S(2)}) copy-start(f32[512]{0:T(512)} %param.33) | copy-start | bytes 6148
  306.6 26.9 %collective-permute-start.4 = (f32[512,256]{1,0:T(8,128)S(1)}, f32[512,256]{1,0:T(8,128)S(1)}, u32[]{:S(2)}, u32[]{:S(2)}) collective-permute-start(f32[512,256]{1,0:T(8,128)S(1)} %copy-done.25), channel_id=1, source_target_pairs={{0,4},{4,0},{1,5},{5,1},{2,6},{6,2},{3,7},{7,3}} | collective-permute-start | bytes 1572872 | tf_op jit(solution)/shard_map/ppermute | solution.py:370
  333.5 43.1 %collective-permute-start.10 = (f32[512,512]{1,0:T(8,128)S(1)}, f32[512,512]{1,0:T(8,128)S(1)}, u32[]{:S(2)}, u32[]{:S(2)}) collective-permute-start(f32[512,512]{1,0:T(8,128)S(1)} %fusion.6.refs_2_.refs_7_), channel_id=1, source_target_pairs={{0,4},{4,0},{1,5},{5,1},{2,6},{6,2},{3,7},{7,3}} | collective-permute-start | bytes 3145736 | tf_op jit(solution)/shard_map/ppermute | solution.py:370
  347.6 12.5 %copy-start = (f32[512,2048]{1,0:T(8,128)}, f32[512,2048]{1,0:T(8,128)S(1)}, u32[]{:S(2)}) copy-start(f32[512,2048]{1,0:T(8,128)S(1)} %multiply_subtract_fusion.2.refs_0_) | copy-start | bytes 12582916
  347.8 12.3 %copy-start.22 = (f32[512,2048]{1,0:T(8,128)S(1)}, f32[512,2048]{1,0:T(8,128)}, u32[]{:S(2)}) copy-start(f32[512,2048]{1,0:T(8,128)} %param.29) | copy-start | bytes 12582916
  360.6 15.0 %copy-start.1 = (f32[512,2048]{1,0:T(8,128)}, f32[512,2048]{1,0:T(8,128)S(1)}, u32[]{:S(2)}) copy-start(f32[512,2048]{1,0:T(8,128)S(1)} %multiply_subtract_fusion.1.refs_0_) | copy-start | bytes 12582916
  362.7 13.5 %copy-start.24 = (f32[2048,512]{1,0:T(8,128)S(1)}, f32[2048,512]{1,0:T(8,128)}, u32[]{:S(2)}) copy-start(f32[2048,512]{1,0:T(8,128)} %param.30) | copy-start | bytes 12582916
  (19 other events, 41.9 us)

commit v9 on v8

--- a/solution.py
+++ b/solution.py
@@ -16,6 +16,7 @@
               (0, 512, 512, 256), (0, 768, 512, 256), (0, 1024, 512, 384), (0, 1408, 512, 640))
 N_HEAD = 6
 N_NEAR = 4
+N_COPY = 4
 MIB = 1024 * 1024
 HEAD_LIMIT = 50 * MIB
 
@@ -193,9 +194,12 @@
             else:
                 out[own, :] = term
 
+    small = depth // N_COPY
     for k in range(n_step):
-        for copy in copies(k):
-            copy.start()
+        for c in range(N_COPY):
+            band = pl.ds(k * depth + c * small, small)
+            for j, (source, start, buf) in enumerate(loads):
+                pltpu.make_async_copy(source.at[band, pl.ds(start, buf.shape[1])], buf.at[band, :], sem.at[j, k]).start()
     if n_x == 1:
         for k in range(n_step):
             multiply(k, k > 0)

time: 385 us -> 385 us (level)
  no operation moved by 1% of the time
where the time goes in v9:
time: 385 us
  waiting for transfers between devices  208 us (54%)
  matrix products  81.8 us (21%)
  Pallas kernels  70.9 us (18%)
  starting transfers between devices  12.1 us (3%)
  other arithmetic  7.27 us (2%)
    ppermute x11, waiting for transfers between devices, per_device(): recvs[name].append(lax.ppermute(before, 'dp', SWAP))  208 us
    dot_general x5, matrix products, product(): jnp.einsum('tm,tn->mn', x_block, dy_block, preferred_element_type=jnp.flo...  81.8 us
    pallas_call x4, Pallas kernels, statistics(): pl.pallas_call(functools.partial(stats_kernel, len(tokens), boxes, near,...  42.7 us
    pallas_call x6, Pallas kernels, head_product(): pl.pallas_call(functools.partial(head_kernel, row_start, col_start, n_x),...  25.3 us
    ppermute x11, starting transfers between devices, per_device(): recvs[name].append(lax.ppermute(before, 'dp', SWAP))  12.1 us
  transfers between devices with their start and end apart: 11, of which 2 were waited for; matrix products, arithmetic and copies ran while one was open for 23% of the time, Pallas kernels for 14%

profile of v9, /device:TPU:0, one launch (start us, length us, event | category | flops | bytes accessed | tf_op | source)
XLA Modules:
  0.0 384.9 jit_solution(18444795560420796671)
XLA Ops:
  0.6 4.3 %head_product.6 = (f32[256,256]{1,0:T(8,128)S(1)}, bf16[8192,256]{1,0:T(8,128)(2,1)S(1)}, bf16[8192,256]{1,0:T(8,128)(2,1)S(1)}) custom-call(bf16[8192,512]{1,0:T(8,128)(2,1)} %refs_0_.2, bf16[8192,2048]{1,0:T(8,128)(2,1)} %refs_2_.1), custom_call_target="tpu_custom_call" | custom-call | flops 1073741824 | bytes 8388608 | tf_op jit(solution)/shard_map/head_product/pallas_call | solution.py:231
  4.9 4.0 %head_product.7 = (f32[256,256]{1,0:T(8,128)S(1)}, bf16[8192,256]{1,0:T(8,128)(2,1)S(1)}) custom-call(bf16[8192,512]{1,0:T(8,128)(2,1)} %refs_0_.2, bf16[8192,256]{1,0:T(8,128)(2,1)S(1)} %get-tuple-element.67.refs_1_), custom_call_target="tpu_custom_call" | custom-call | flops 1073741824 | bytes 4194304 | tf_op jit(solution)/shard_map/head_product/pallas_call | solution.py:231
  8.9 3.4 collective-permute-start.1
  12.3 4.0 %head_product.8 = (f32[256,256]{1,0:T(8,128)S(1)}, bf16[8192,256]{1,0:T(8,128)(2,1)S(1)}) custom-call(bf16[8192,256]{1,0:T(8,128)(2,1)S(1)} %get-tuple-element.83.refs_0_, bf16[8192,2048]{1,0:T(8,128)(2,1)} %refs_2_.1), custom_call_target="tpu_custom_call" | custom-call | flops 1073741824 | bytes 4194304 | tf_op jit(solution)/shard_map/head_product/pallas_call | solution.py:231
  16.3 1.3 head_product.9.refs_10_
  17.6 2.0 collective-permute-start.3
  19.7 5.8 %head_product.10.refs_11_ = f32[512,256]{1,0:T(8,128)} custom-call(bf16[8192,256]{1,0:T(8,128)(2,1)S(1)} %get-tuple-element.83.refs_0_, bf16[8192,256]{1,0:T(8,128)(2,1)S(1)} %get-tuple-element.84.refs_0_.refs_1_, bf16[8192,2048]{1,0:T(8,128)(2,1)} %refs_2_.1), custom_call_target="tpu_custom_call" | custom-call | flops 2147483648 | bytes 4194304 | tf_op jit(solution)/shard_map/head_product/pallas_call | solution.py:231
  25.5 5.9 %head_product.11.refs_12_ = f32[512,256]{1,0:T(8,128)} custom-call(bf16[8192,256]{1,0:T(8,128)(2,1)S(1)} %get-tuple-element.83.refs_0_, bf16[8192,256]{1,0:T(8,128)(2,1)S(1)} %get-tuple-element.84.refs_0_.refs_1_, bf16[8192,2048]{1,0:T(8,128)(2,1)} %refs_2_.1), custom_call_target="tpu_custom_call" | custom-call | flops 2147483648 | bytes 4194304 | tf_op jit(solution)/shard_map/head_product/pallas_call | solution.py:231
  31.4 9.0 %fusion.2.refs_13_ = f32[512,384]{1,0:T(8,128)S(1)} fusion(bf16[8192,512]{1,0:T(8,128)(2,1)} %refs_0_.2, bf16[8192,2048]{1,0:T(8,128)(2,1)} %refs_2_.1), kind=kOutput, calls=%fused_computation.2 | convolution fusion | flops 3221225472 | bytes 15466496 | tf_op jit(solution)/shard_map/tm,tn->mn/dot_general | solution.py:339
  40.4 16.2 %fusion.refs_14_ = f32[512,640]{1,0:T(8,128)S(1)} fusion(bf16[8192,512]{1,0:T(8,128)(2,1)} %refs_0_.2, bf16[8192,2048]{1,0:T(8,128)(2,1)} %refs_2_.1), kind=kOutput, calls=%fused_computation | convolution fusion | flops 5368709120 | bytes 20185088 | tf_op jit(solution)/shard_map/tm,tn->mn/dot_general | solution.py:339
  56.6 21.9 %fusion.4.refs_0_.refs_7_ = f32[512,2048]{1,0:T(8,128)S(1)} fusion(bf16[8192,512]{1,0:T(8,128)(2,1)S(1)} %bitcast.49, bf16[8192,2048]{1,0:T(8,128)(2,1)} %param.24), kind=kOutput, calls=%fused_computation.11 | convolution fusion | flops 17179869184 | bytes 46137344 | tf_op jit(solution)/shard_map/tm,tn->mn/dot_general | solution.py:339
  78.6 25.3 %fusion.5.refs_1_.refs_7_ = f32[2048,512]{1,0:T(8,128)S(1)} fusion(bf16[8192,2048]{1,0:T(8,128)(2,1)} %param.25, bf16[8192,512]{1,0:T(8,128)(2,1)} %param.26), kind=kOutput, calls=%fused_computation.12 | convolution fusion | flops 17179869184 | bytes 46137344 | tf_op jit(solution)/shard_map/tm,tn->mn/dot_general | solution.py:339
  104.4 1.6 collective-permute-start.7
  106.5 1.6 collective-permute-start
  108.1 9.5 %fusion.6.refs_2_.refs_7_ = f32[512,512]{1,0:T(8,128)S(1)} fusion(bf16[8192,512]{1,0:T(8,128)(2,1)} %param.20, bf16[8192,512]{1,0:T(8,128)(2,1)} %param.21), kind=kOutput, calls=%fused_computation.13 | convolution fusion | flops 4294967296 | bytes 17825792 | tf_op jit(solution)/shard_map/tm,tn->mn/dot_general | solution.py:339
  117.7 0.8 multiply_reduce_fusion.3
  118.5 186.4 %collective-permute-done.refs_15_ = f32[256,256]{1,0:T(8,128)S(1)} collective-permute-done((f32[256,256]{1,0:T(8,128)S(1)}, f32[256,256]{1,0:T(8,128)S(1)}, u32[]{:S(2)}, u32[]{:S(2)}) %collective-permute-start) | collective-permute-done | bytes 262176 | tf_op jit(solution)/shard_map/ppermute | solution.py:374
  305.2 1.7 multiply_reduce_fusion.2
  306.9 1.8 collective-permute-start.4
  308.7 1.7 multiply_reduce_fusion.1
  310.4 1.7 multiply_reduce_fusion
  312.0 21.8 %collective-permute-done.4.refs_19_ = f32[512,256]{1,0:T(8,128)S(1)} collective-permute-done((f32[512,256]{1,0:T(8,128)S(1)}, f32[512,256]{1,0:T(8,128)S(1)}, u32[]{:S(2)}, u32[]{:S(2)}) %collective-permute-start.4) | collective-permute-done | bytes 524320 | tf_op jit(solution)/shard_map/ppermute | solution.py:374
  335.6 11.1 %shard_map.283 = (f32[512,2048]{1,0:T(8,128)S(1)}, f32[1,512]{1,0:T(1,128)S(1)}, f32[1,512]{1,0:T(1,128)S(1)}, f32[1,2048]{1,0:T(1,128)S(1)}) custom-call(f32[512,2048]{1,0:T(8,128)S(1)} %fusion.4.refs_0_.refs_7_, f32[2048,512]{1,0:T(8,128)S(1)} %fusion.5.refs_1_.refs_7_, f32[512,512]{1,0:T(8,128)S(1)} %fusion.6.refs_2_.refs_7_, f32[1,1]{1,0:T(1,128)} %bitcast.refs_3_, ...), custom_call_target="tpu_custom_call" | custom-call | flops 838860800 | bytes 12582912 | tf_op jit(solution)/shard_map/pallas_call | solution.py:308
  346.8 0.6 emit.3
  348.1 12.2 %shard_map.284 = (f32[512,2048]{1,0:T(8,128)S(1)}, f32[1,512]{1,0:T(1,128)S(1)}, f32[1,512]{1,0:T(1,128)S(1)}, f32[1,2048]{1,0:T(1,128)S(1)}) custom-call(f32[512,2048]{1,0:T(8,128)S(1)} %multiply_subtract_fusion.2.refs_0_, f32[1,512]{1,0:T(1,128)S(1)} %copy-done.18, f32[1,2048]{1,0:T(1,128)S(1)} %copy-done.10, f32[1,1]{1,0:T(1,128)} %bitcast.4.refs_3_, ...), custom_call_target="tpu_custom_call" | custom-call | flops 838860800 | bytes 12582912 | tf_op jit(solution)/shard_map/pallas_call | solution.py:308
  360.9 0.6 emit.4
  361.5 0.7 copy-done.11
  362.3 0.7 copy-done.19
  363.0 12.9 %shard_map.285 = (f32[2048,512]{1,0:T(8,128)S(1)}, f32[1,2048]{1,0:T(1,128)S(1)}, f32[1,2048]{1,0:T(1,128)S(1)}, f32[1,512]{1,0:T(1,128)S(1)}) custom-call(f32[512,2048]{1,0:T(8,128)S(1)} %multiply_subtract_fusion.1.refs_0_, f32[1,512]{1,0:T(1,128)S(1)} %copy-done.19, f32[1,2048]{1,0:T(1,128)S(1)} %copy-done.11, f32[1,1]{1,0:T(1,128)} %bitcast.8.refs_3_, ...), custom_call_target="tpu_custom_call" | custom-call | flops 838860800 | bytes 12582912 | tf_op jit(solution)/shard_map/pallas_call | solution.py:308
  375.8 0.6 emit.5
  377.2 6.5 %shard_map.286 = (f32[512,512]{1,0:T(8,128)S(1)}, f32[1,128]{1,0:T(1,128)S(1)}, f32[1,512]{1,0:T(1,128)S(1)}, f32[1,512]{1,0:T(1,128)S(1)}) custom-call(f32[2048,512]{1,0:T(8,128)S(1)} %multiply_subtract_fusion.refs_0_, f32[1,2048]{1,0:T(1,128)S(1)} %copy-done.7, f32[1,512]{1,0:T(1,128)S(1)} %copy-done.15, f32[1,1]{1,0:T(1,128)} %bitcast.12.refs_3_, ...), custom_call_target="tpu_custom_call" | custom-call | flops 209715200 | bytes 3145728 | tf_op jit(solution)/shard_map/pallas_call | solution.py:308
  383.7 1.1 finish.1
  (99 shorter events, 5.0 us)
Async XLA Ops:
  8.9 97.5 %collective-permute-start.1 = (f32[256,256]{1,0:T(8,128)S(1)}, f32[256,256]{1,0:T(8,128)S(1)}, u32[]{:S(2)}, u32[]{:S(2)}) collective-permute-start(f32[256,256]{1,0:T(8,128)S(1)} %get-tuple-element.71.refs_8_), channel_id=1, source_target_pairs={{0,4},{4,0},{1,5},{5,1},{2,6},{6,2},{3,7},{7,3}} | collective-permute-start | bytes 786440 | tf_op jit(solution)/shard_map/ppermute | solution.py:374
  16.3 89.7 %collective-permute-start.2 = (f32[256,256]{1,0:T(8,128)S(1)}, f32[256,256]{1,0:T(8,128)S(1)}, u32[]{:S(2)}, u32[]{:S(2)}) collective-permute-start(f32[256,256]{1,0:T(8,128)S(1)} %get-tuple-element.76.refs_9_), channel_id=1, source_target_pairs={{0,4},{4,0},{1,5},{5,1},{2,6},{6,2},{3,7},{7,3}} | collective-permute-start | bytes 786440 | tf_op jit(solution)/shard_map/ppermute | solution.py:374
  17.6 86.7 %collective-permute-start.3 = (f32[256,256]{1,0:T(8,128)S(1)}, f32[256,256]{1,0:T(8,128)S(1)}, u32[]{:S(2)}, u32[]{:S(2)}) collective-permute-start(f32[256,256]{1,0:T(8,128)S(1)} %head_product.9.refs_10_), channel_id=1, source_target_pairs={{0,4},{4,0},{1,5},{5,1},{2,6},{6,2},{3,7},{7,3}} | collective-permute-start | bytes 786440 | tf_op jit(solution)/shard_map/ppermute | solution.py:374
  31.4 25.2 %slice-start = ((s8[8388608]{0:T(1024)(128)(4,1)}), s8[4194304]{0:T(1024)(128)(4,1)S(1)}, s32[]{:S(2)}) async-start(s8[8388608]{0:T(1024)(128)(4,1)} %bitcast.48), calls=%async_computation | async-start | bytes 8388608
  40.4 264.5 %copy-start.29 = (f32[512,384]{1,0:T(8,128)}, f32[512,384]{1,0:T(8,128)S(1)}, u32[]{:S(2)}) copy-start(f32[512,384]{1,0:T(8,128)S(1)} %fusion.2.refs_13_) | copy-start | bytes 2359300
  40.4 16.2 %slice-start.1 = ((s8[8388608]{0:T(1024)(128)(4,1)}), s8[4194304]{0:T(1024)(128)(4,1)S(1)}, s32[]{:S(2)}) async-start(s8[8388608]{0:T(1024)(128)(4,1)} %bitcast.48), calls=%async_computation.1 | async-start | bytes 8388608
  56.6 47.7 %copy-start.27 = (f32[512,640]{1,0:T(8,128)}, f32[512,640]{1,0:T(8,128)S(1)}, u32[]{:S(2)}) copy-start(f32[512,640]{1,0:T(8,128)S(1)} %fusion.refs_14_) | copy-start | bytes 3932164
  78.6 255.8 %copy-start.4 = (f32[512,2048]{1,0:T(8,128)}, f32[512,2048]{1,0:T(8,128)S(1)}, u32[]{:S(2)}) copy-start(f32[512,2048]{1,0:T(8,128)S(1)} %fusion.4.refs_0_.refs_7_) | copy-start | bytes 12582916
  78.6 27.4 %copy-start.26 = (f32[512,256]{1,0:T(8,128)S(1)}, f32[512,256]{1,0:T(8,128)}, u32[]{:S(2)}) copy-start(f32[512,256]{1,0:T(8,128)} %head_product.11.refs_12_) | copy-start | bytes 1572868
  78.6 269.3 %collective-permute-start.8 = (f32[512,2048]{1,0:T(8,128)S(1)}, f32[512,2048]{1,0:T(8,128)}, u32[]{:S(2)}, u32[]{:S(2)}) collective-permute-start(f32[512,2048]{1,0:T(8,128)S(1)} %fusion.4.refs_0_.refs_7_), channel_id=1, source_target_pairs={{0,4},{4,0},{1,5},{5,1},{2,6},{6,2},{3,7},{7,3}} | collective-permute-start | bytes 12582920 | tf_op jit(solution)/shard_map/ppermute | solution.py:374
  103.9 230.5 %copy-start.3 = (f32[2048,512]{1,0:T(8,128)}, f32[2048,512]{1,0:T(8,128)S(1)}, u32[]{:S(2)}) copy-start(f32[2048,512]{1,0:T(8,128)S(1)} %fusion.5.refs_1_.refs_7_) | copy-start | bytes 12582916
  103.9 13.7 %copy-start.37 = (f32[3]{0:T(128)S(1)}, f32[3]{0:T(128)}, u32[]{:S(2)}) copy-start(f32[3]{0:T(128)} %param.39) | copy-start | bytes 40
  103.9 13.7 %copy-start.5 = (f32[512,512]{1,0:T(8,128)S(1)}, f32[512,512]{1,0:T(8,128)}, u32[]{:S(2)}) copy-start(f32[512,512]{1,0:T(8,128)} %weight.1) | copy-start | bytes 3145732
  103.9 201.3 %copy-start.20 = (f32[512,2048]{1,0:T(8,128)S(1)}, f32[512,2048]{1,0:T(8,128)}, u32[]{:S(2)}) copy-start(f32[512,2048]{1,0:T(8,128)} %param.28) | copy-start | bytes 12582916
  104.0 257.6 %collective-permute-start.9 = (f32[2048,512]{1,0:T(8,128)S(1)}, f32[2048,512]{1,0:T(8,128)}, u32[]{:S(2)}, u32[]{:S(2)}) collective-permute-start(f32[2048,512]{1,0:T(8,128)S(1)} %fusion.5.refs_1_.refs_7_), channel_id=1, source_target_pairs={{0,4},{4,0},{1,5},{5,1},{2,6},{6,2},{3,7},{7,3}} | collective-permute-start | bytes 12582920 | tf_op jit(solution)/shard_map/ppermute | solution.py:374
  104.4 13.2 %copy-start.35 = (f32[256,256]{1,0:T(8,128)}, f32[256,256]{1,0:T(8,128)S(1)}, u32[]{:S(2)}) copy-start(f32[256,256]{1,0:T(8,128)S(1)} %collective-permute-done.3.refs_18_) | copy-start | bytes 786436
  104.4 229.9 %collective-permute-start.7 = (f32[512,640]{1,0:T(8,128)S(1)}, f32[512,640]{1,0:T(8,128)S(1)}, u32[]{:S(2)}, u32[]{:S(2)}) collective-permute-start(f32[512,640]{1,0:T(8,128)S(1)} %fusion.refs_14_), channel_id=1, source_target_pairs={{0,4},{4,0},{1,5},{5,1},{2,6},{6,2},{3,7},{7,3}} | collective-permute-start | bytes 3932168 | tf_op jit(solution)/shard_map/ppermute | solution.py:374
  106.0 11.6 %copy-start.34 = (f32[256,256]{1,0:T(8,128)}, f32[256,256]{1,0:T(8,128)S(1)}, u32[]{:S(2)}) copy-start(f32[256,256]{1,0:T(8,128)S(1)} %collective-permute-done.2.refs_17_) | copy-start | bytes 786436
  106.0 200.9 %collective-permute-start.5 = (f32[512,256]{1,0:T(8,128)S(1)}, f32[512,256]{1,0:T(8,128)S(1)}, u32[]{:S(2)}, u32[]{:S(2)}) collective-permute-start(f32[512,256]{1,0:T(8,128)S(1)} %copy-done.26), channel_id=1, source_target_pairs={{0,4},{4,0},{1,5},{5,1},{2,6},{6,2},{3,7},{7,3}} | collective-permute-start | bytes 1572872 | tf_op jit(solution)/shard_map/ppermute | solution.py:374
  106.5 198.5 %collective-permute-start = (f32[256,256]{1,0:T(8,128)S(1)}, f32[256,256]{1,0:T(8,128)S(1)}, u32[]{:S(2)}, u32[]{:S(2)}) collective-permute-start(f32[256,256]{1,0:T(8,128)S(1)} %get-tuple-element.66.refs_7_), channel_id=1, source_target_pairs={{0,4},{4,0},{1,5},{5,1},{2,6},{6,2},{3,7},{7,3}} | collective-permute-start | bytes 786440 | tf_op jit(solution)/shard_map/ppermute | solution.py:374
  117.6 189.3 %copy-start.25 = (f32[512,256]{1,0:T(8,128)S(1)}, f32[512,256]{1,0:T(8,128)}, u32[]{:S(2)}) copy-start(f32[512,256]{1,0:T(8,128)} %head_product.10.refs_11_) | copy-start | bytes 1572868
  117.6 191.0 %copy-start.21 = (f32[512,2048]{1,0:T(8,128)S(1)}, f32[512,2048]{1,0:T(8,128)}, u32[]{:S(2)}) copy-start(f32[512,2048]{1,0:T(8,128)} %param.29) | copy-start | bytes 12582916
  118.5 191.8 %copy-start.23 = (f32[2048,512]{1,0:T(8,128)S(1)}, f32[2048,512]{1,0:T(8,128)}, u32[]{:S(2)}) copy-start(f32[2048,512]{1,0:T(8,128)} %param.30) | copy-start | bytes 12582916
  304.9 29.4 %collective-permute-start.6 = (f32[512,384]{1,0:T(8,128)S(1)}, f32[512,384]{1,0:T(8,128)S(1)}, u32[]{:S(2)}, u32[]{:S(2)}) collective-permute-start(f32[512,384]{1,0:T(8,128)S(1)} %fusion.2.refs_13_), channel_id=1, source_target_pairs={{0,4},{4,0},{1,5},{5,1},{2,6},{6,2},{3,7},{7,3}} | collective-permute-start | bytes 2359304 | tf_op jit(solution)/shard_map/ppermute | solution.py:374
  306.9 28.7 %copy-start.6 = (f32[2048]{0:T(1024)S(1)}, f32[2048]{0:T(1024)}, u32[]{:S(2)}) copy-start(f32[2048]{0:T(1024)} %param.34) | copy-start | bytes 24580
  306.9 28.7 %copy-start.12 = (f32[512]{0:T(512)S(1)}, f32[512]{0:T(512)}, u32[]{:S(2)}) copy-start(f32[512]{0:T(512)} %param.33) | copy-start | bytes 6148
  306.9 26.9 %collective-permute-start.4 = (f32[512,256]{1,0:T(8,128)S(1)}, f32[512,256]{1,0:T(8,128)S(1)}, u32[]{:S(2)}, u32[]{:S(2)}) collective-permute-start(f32[512,256]{1,0:T(8,128)S(1)} %copy-done.25), channel_id=1, source_target_pairs={{0,4},{4,0},{1,5},{5,1},{2,6},{6,2},{3,7},{7,3}} | collective-permute-start | bytes 1572872 | tf_op jit(solution)/shard_map/ppermute | solution.py:374
  333.9 43.1 %collective-permute-start.10 = (f32[512,512]{1,0:T(8,128)S(1)}, f32[512,512]{1,0:T(8,128)S(1)}, u32[]{:S(2)}, u32[]{:S(2)}) collective-permute-start(f32[512,512]{1,0:T(8,128)S(1)} %fusion.6.refs_2_.refs_7_), channel_id=1, source_target_pairs={{0,4},{4,0},{1,5},{5,1},{2,6},{6,2},{3,7},{7,3}} | collective-permute-start | bytes 3145736 | tf_op jit(solution)/shard_map/ppermute | solution.py:374
  347.9 12.5 %copy-start = (f32[512,2048]{1,0:T(8,128)}, f32[512,2048]{1,0:T(8,128)S(1)}, u32[]{:S(2)}) copy-start(f32[512,2048]{1,0:T(8,128)S(1)} %multiply_subtract_fusion.2.refs_0_) | copy-start | bytes 12582916
  348.1 12.2 %copy-start.22 = (f32[512,2048]{1,0:T(8,128)S(1)}, f32[512,2048]{1,0:T(8,128)}, u32[]{:S(2)}) copy-start(f32[512,2048]{1,0:T(8,128)} %param.29) | copy-start | bytes 12582916
  360.9 15.0 %copy-start.1 = (f32[512,2048]{1,0:T(8,128)}, f32[512,2048]{1,0:T(8,128)S(1)}, u32[]{:S(2)}) copy-start(f32[512,2048]{1,0:T(8,128)S(1)} %multiply_subtract_fusion.1.refs_0_) | copy-start | bytes 12582916
  363.0 13.5 %copy-start.24 = (f32[2048,512]{1,0:T(8,128)S(1)}, f32[2048,512]{1,0:T(8,128)}, u32[]{:S(2)}) copy-start(f32[2048,512]{1,0:T(8,128)} %param.30) | copy-start | bytes 12582916
  (19 other events, 41.9 us)

commit v10 on v8

--- a/solution.py
+++ b/solution.py
@@ -16,6 +16,7 @@
               (0, 512, 512, 256), (0, 768, 512, 256), (0, 1024, 512, 384), (0, 1408, 512, 640))
 N_HEAD = 6
 N_NEAR = 4
+STEPS = 16
 MIB = 1024 * 1024
 HEAD_LIMIT = 50 * MIB
 
@@ -171,7 +172,8 @@
         source, dy_buf = dy_buf, refs.pop(0)
         loads.append((source, col_start, dy_buf))
     sem = refs.pop(0) if loads else None
-    n_step = 8
+    n_step = STEPS if n_x == 1 and loads else 8
+    window = n_step if n_x == 2 else (12 // max(1, len(loads)))
     depth = dy_buf.shape[0] // n_step
     rows = x_bufs[0].shape[1]
 
@@ -180,9 +182,15 @@
         return [pltpu.make_async_copy(source.at[band, pl.ds(start, buf.shape[1])], buf.at[band, :], sem.at[j, k])
                 for j, (source, start, buf) in enumerate(loads)]
 
+    def begin(k):
+        for copy in copies(k):
+            copy.start()
+
     def multiply(k, add):
         for copy in copies(k):
             copy.wait()
+        if isinstance(k, int) and k + window < n_step:
+            begin(k + window)
         band = pl.ds(k * depth if isinstance(k, int) else pl.multiple_of(k * depth, depth), depth)
         for j, x_buf in enumerate(x_bufs):
             own = pl.ds(j * rows, rows)
@@ -193,9 +201,8 @@
             else:
                 out[own, :] = term
 
-    for k in range(n_step):
-        for copy in copies(k):
-            copy.start()
+    for k in range(min(window, n_step)):
+        begin(k)
     if n_x == 1:
         for k in range(n_step):
             multiply(k, k > 0)
@@ -220,7 +227,7 @@
     outs = [jax.ShapeDtypeStruct((rows, 256), jnp.float32)] + [held] * (x_far + (dy_far and keep))
     scratch = [pltpu.VMEM((tokens, 256), dy_block.dtype)] * (dy_far and not keep)
     if x_far or dy_far:
-        scratch.append(pltpu.SemaphoreType.DMA((x_far + dy_far, 8)))
+        scratch.append(pltpu.SemaphoreType.DMA((x_far + dy_far, STEPS)))
     far = [x_far] * n_x + [dy_far]
     operands = [pltpu.with_memory_space_constraint(v, pltpu.HBM if f else pltpu.VMEM)
                 for v, f in zip(list(x_blocks) + [dy_block], far)]

time: 385 us -> 387 us (level)
  no operation moved by 1% of the time
where the time goes in v10:
time: 387 us; the launch traced here: 386 us
  waiting for transfers between devices  208 us (54%)
  matrix products  81.9 us (21%)
  Pallas kernels  72.1 us (19%)
  starting transfers between devices  12.1 us (3%)
  other arithmetic  7.28 us (2%)
    ppermute x11, waiting for transfers between devices, per_device(): recvs[name].append(lax.ppermute(before, 'dp', SWAP))  208 us
    dot_general x5, matrix products, product(): jnp.einsum('tm,tn->mn', x_block, dy_block, preferred_element_type=jnp.flo...  81.9 us
    pallas_call x4, Pallas kernels, statistics(): pl.pallas_call(functools.partial(stats_kernel, len(tokens), boxes, near,...  42.7 us
    pallas_call x6, Pallas kernels, head_product(): pl.pallas_call(functools.partial(head_kernel, row_start, col_start, n_x),...  26.5 us
    ppermute x11, starting transfers between devices, per_device(): recvs[name].append(lax.ppermute(before, 'dp', SWAP))  12.1 us
  transfers between devices with their start and end apart: 11, of which 2 were waited for; matrix products, arithmetic and copies ran while one was open for 23% of the time, Pallas kernels for 14%

profile of v10, /device:TPU:0, one launch (start us, length us, event | category | flops | bytes accessed | tf_op | source)
XLA Modules:
  0.0 386.2 jit_solution(6888190776474955687)
XLA Ops:
  0.6 4.7 %head_product.6 = (f32[256,256]{1,0:T(8,128)S(1)}, bf16[8192,256]{1,0:T(8,128)(2,1)S(1)}, bf16[8192,256]{1,0:T(8,128)(2,1)S(1)}) custom-call(bf16[8192,512]{1,0:T(8,128)(2,1)} %refs_0_.2, bf16[8192,2048]{1,0:T(8,128)(2,1)} %refs_2_.1), custom_call_target="tpu_custom_call" | custom-call | flops 1073741824 | bytes 8388608 | tf_op jit(solution)/shard_map/head_product/pallas_call | solution.py:234
  5.4 4.4 %head_product.7 = (f32[256,256]{1,0:T(8,128)S(1)}, bf16[8192,256]{1,0:T(8,128)(2,1)S(1)}) custom-call(bf16[8192,512]{1,0:T(8,128)(2,1)} %refs_0_.2, bf16[8192,256]{1,0:T(8,128)(2,1)S(1)} %get-tuple-element.67.refs_1_), custom_call_target="tpu_custom_call" | custom-call | flops 1073741824 | bytes 4194304 | tf_op jit(solution)/shard_map/head_product/pallas_call | solution.py:234
  9.8 3.4 collective-permute-start.1
  13.1 4.4 %head_product.8 = (f32[256,256]{1,0:T(8,128)S(1)}, bf16[8192,256]{1,0:T(8,128)(2,1)S(1)}) custom-call(bf16[8192,256]{1,0:T(8,128)(2,1)S(1)} %get-tuple-element.83.refs_0_, bf16[8192,2048]{1,0:T(8,128)(2,1)} %refs_2_.1), custom_call_target="tpu_custom_call" | custom-call | flops 1073741824 | bytes 4194304 | tf_op jit(solution)/shard_map/head_product/pallas_call | solution.py:234
  17.6 1.3 head_product.9.refs_10_
  18.8 2.0 collective-permute-start.3
  20.9 5.9 %head_product.10.refs_11_ = f32[512,256]{1,0:T(8,128)} custom-call(bf16[8192,256]{1,0:T(8,128)(2,1)S(1)} %get-tuple-element.83.refs_0_, bf16[8192,256]{1,0:T(8,128)(2,1)S(1)} %get-tuple-element.84.refs_0_.refs_1_, bf16[8192,2048]{1,0:T(8,128)(2,1)} %refs_2_.1), custom_call_target="tpu_custom_call" | custom-call | flops 2147483648 | bytes 4194304 | tf_op jit(solution)/shard_map/head_product/pallas_call | solution.py:234
  26.7 5.9 %head_product.11.refs_12_ = f32[512,256]{1,0:T(8,128)} custom-call(bf16[8192,256]{1,0:T(8,128)(2,1)S(1)} %get-tuple-element.83.refs_0_, bf16[8192,256]{1,0:T(8,128)(2,1)S(1)} %get-tuple-element.84.refs_0_.refs_1_, bf16[8192,2048]{1,0:T(8,128)(2,1)} %refs_2_.1), custom_call_target="tpu_custom_call" | custom-call | flops 2147483648 | bytes 4194304 | tf_op jit(solution)/shard_map/head_product/pallas_call | solution.py:234
  32.6 9.0 %fusion.2.refs_13_ = f32[512,384]{1,0:T(8,128)S(1)} fusion(bf16[8192,512]{1,0:T(8,128)(2,1)} %refs_0_.2, bf16[8192,2048]{1,0:T(8,128)(2,1)} %refs_2_.1), kind=kOutput, calls=%fused_computation.2 | convolution fusion | flops 3221225472 | bytes 15466496 | tf_op jit(solution)/shard_map/tm,tn->mn/dot_general | solution.py:342
  41.7 16.2 %fusion.refs_14_ = f32[512,640]{1,0:T(8,128)S(1)} fusion(bf16[8192,512]{1,0:T(8,128)(2,1)} %refs_0_.2, bf16[8192,2048]{1,0:T(8,128)(2,1)} %refs_2_.1), kind=kOutput, calls=%fused_computation | convolution fusion | flops 5368709120 | bytes 20185088 | tf_op jit(solution)/shard_map/tm,tn->mn/dot_general | solution.py:342
  57.9 21.9 %fusion.4.refs_0_.refs_7_ = f32[512,2048]{1,0:T(8,128)S(1)} fusion(bf16[8192,512]{1,0:T(8,128)(2,1)S(1)} %bitcast.49, bf16[8192,2048]{1,0:T(8,128)(2,1)} %param.24), kind=kOutput, calls=%fused_computation.11 | convolution fusion | flops 17179869184 | bytes 46137344 | tf_op jit(solution)/shard_map/tm,tn->mn/dot_general | solution.py:342
  79.9 25.3 %fusion.5.refs_1_.refs_7_ = f32[2048,512]{1,0:T(8,128)S(1)} fusion(bf16[8192,2048]{1,0:T(8,128)(2,1)} %param.25, bf16[8192,512]{1,0:T(8,128)(2,1)} %param.26), kind=kOutput, calls=%fused_computation.12 | convolution fusion | flops 17179869184 | bytes 46137344 | tf_op jit(solution)/shard_map/tm,tn->mn/dot_general | solution.py:342
  105.6 1.7 collective-permute-start.7
  107.7 1.6 collective-permute-start
  109.3 9.5 %fusion.6.refs_2_.refs_7_ = f32[512,512]{1,0:T(8,128)S(1)} fusion(bf16[8192,512]{1,0:T(8,128)(2,1)} %param.20, bf16[8192,512]{1,0:T(8,128)(2,1)} %param.21), kind=kOutput, calls=%fused_computation.13 | convolution fusion | flops 4294967296 | bytes 17825792 | tf_op jit(solution)/shard_map/tm,tn->mn/dot_general | solution.py:342
  118.9 0.8 multiply_reduce_fusion.3
  119.8 186.4 %collective-permute-done.refs_15_ = f32[256,256]{1,0:T(8,128)S(1)} collective-permute-done((f32[256,256]{1,0:T(8,128)S(1)}, f32[256,256]{1,0:T(8,128)S(1)}, u32[]{:S(2)}, u32[]{:S(2)}) %collective-permute-start) | collective-permute-done | bytes 262176 | tf_op jit(solution)/shard_map/ppermute | solution.py:377
  306.5 1.7 multiply_reduce_fusion.2
  308.2 1.7 collective-permute-start.4
  309.9 1.7 multiply_reduce_fusion.1
  311.6 1.7 multiply_reduce_fusion
  313.3 21.8 %collective-permute-done.4.refs_19_ = f32[512,256]{1,0:T(8,128)S(1)} collective-permute-done((f32[512,256]{1,0:T(8,128)S(1)}, f32[512,256]{1,0:T(8,128)S(1)}, u32[]{:S(2)}, u32[]{:S(2)}) %collective-permute-start.4) | collective-permute-done | bytes 524320 | tf_op jit(solution)/shard_map/ppermute | solution.py:377
  336.9 11.1 %shard_map.283 = (f32[512,2048]{1,0:T(8,128)S(1)}, f32[1,512]{1,0:T(1,128)S(1)}, f32[1,512]{1,0:T(1,128)S(1)}, f32[1,2048]{1,0:T(1,128)S(1)}) custom-call(f32[512,2048]{1,0:T(8,128)S(1)} %fusion.4.refs_0_.refs_7_, f32[2048,512]{1,0:T(8,128)S(1)} %fusion.5.refs_1_.refs_7_, f32[512,512]{1,0:T(8,128)S(1)} %fusion.6.refs_2_.refs_7_, f32[1,1]{1,0:T(1,128)} %bitcast.refs_3_, ...), custom_call_target="tpu_custom_call" | custom-call | flops 838860800 | bytes 12582912 | tf_op jit(solution)/shard_map/pallas_call | solution.py:311
  348.0 0.6 emit.3
  349.4 12.2 %shard_map.284 = (f32[512,2048]{1,0:T(8,128)S(1)}, f32[1,512]{1,0:T(1,128)S(1)}, f32[1,512]{1,0:T(1,128)S(1)}, f32[1,2048]{1,0:T(1,128)S(1)}) custom-call(f32[512,2048]{1,0:T(8,128)S(1)} %multiply_subtract_fusion.2.refs_0_, f32[1,512]{1,0:T(1,128)S(1)} %copy-done.18, f32[1,2048]{1,0:T(1,128)S(1)} %copy-done.10, f32[1,1]{1,0:T(1,128)} %bitcast.4.refs_3_, ...), custom_call_target="tpu_custom_call" | custom-call | flops 838860800 | bytes 12582912 | tf_op jit(solution)/shard_map/pallas_call | solution.py:311
  362.1 0.6 emit.4
  362.8 0.7 copy-done.11
  363.5 0.7 copy-done.19
  364.2 12.8 %shard_map.285 = (f32[2048,512]{1,0:T(8,128)S(1)}, f32[1,2048]{1,0:T(1,128)S(1)}, f32[1,2048]{1,0:T(1,128)S(1)}, f32[1,512]{1,0:T(1,128)S(1)}) custom-call(f32[512,2048]{1,0:T(8,128)S(1)} %multiply_subtract_fusion.1.refs_0_, f32[1,512]{1,0:T(1,128)S(1)} %copy-done.19, f32[1,2048]{1,0:T(1,128)S(1)} %copy-done.11, f32[1,1]{1,0:T(1,128)} %bitcast.8.refs_3_, ...), custom_call_target="tpu_custom_call" | custom-call | flops 838860800 | bytes 12582912 | tf_op jit(solution)/shard_map/pallas_call | solution.py:311
  377.1 0.6 emit.5
  378.4 6.5 %shard_map.286 = (f32[512,512]{1,0:T(8,128)S(1)}, f32[1,128]{1,0:T(1,128)S(1)}, f32[1,512]{1,0:T(1,128)S(1)}, f32[1,512]{1,0:T(1,128)S(1)}) custom-call(f32[2048,512]{1,0:T(8,128)S(1)} %multiply_subtract_fusion.refs_0_, f32[1,2048]{1,0:T(1,128)S(1)} %copy-done.7, f32[1,512]{1,0:T(1,128)S(1)} %copy-done.15, f32[1,1]{1,0:T(1,128)} %bitcast.12.refs_3_, ...), custom_call_target="tpu_custom_call" | custom-call | flops 209715200 | bytes 3145728 | tf_op jit(solution)/shard_map/pallas_call | solution.py:311
  384.9 1.1 finish.1
  (99 shorter events, 5.0 us)
Async XLA Ops:
  9.8 97.9 %collective-permute-start.1 = (f32[256,256]{1,0:T(8,128)S(1)}, f32[256,256]{1,0:T(8,128)S(1)}, u32[]{:S(2)}, u32[]{:S(2)}) collective-permute-start(f32[256,256]{1,0:T(8,128)S(1)} %get-tuple-element.71.refs_8_), channel_id=1, source_target_pairs={{0,4},{4,0},{1,5},{5,1},{2,6},{6,2},{3,7},{7,3}} | collective-permute-start | bytes 786440 | tf_op jit(solution)/shard_map/ppermute | solution.py:377
  17.5 89.8 %collective-permute-start.2 = (f32[256,256]{1,0:T(8,128)S(1)}, f32[256,256]{1,0:T(8,128)S(1)}, u32[]{:S(2)}, u32[]{:S(2)}) collective-permute-start(f32[256,256]{1,0:T(8,128)S(1)} %get-tuple-element.76.refs_9_), channel_id=1, source_target_pairs={{0,4},{4,0},{1,5},{5,1},{2,6},{6,2},{3,7},{7,3}} | collective-permute-start | bytes 786440 | tf_op jit(solution)/shard_map/ppermute | solution.py:377
  18.8 86.8 %collective-permute-start.3 = (f32[256,256]{1,0:T(8,128)S(1)}, f32[256,256]{1,0:T(8,128)S(1)}, u32[]{:S(2)}, u32[]{:S(2)}) collective-permute-start(f32[256,256]{1,0:T(8,128)S(1)} %head_product.9.refs_10_), channel_id=1, source_target_pairs={{0,4},{4,0},{1,5},{5,1},{2,6},{6,2},{3,7},{7,3}} | collective-permute-start | bytes 786440 | tf_op jit(solution)/shard_map/ppermute | solution.py:377
  32.6 25.2 %slice-start = ((s8[8388608]{0:T(1024)(128)(4,1)}), s8[4194304]{0:T(1024)(128)(4,1)S(1)}, s32[]{:S(2)}) async-start(s8[8388608]{0:T(1024)(128)(4,1)} %bitcast.48), calls=%async_computation | async-start | bytes 8388608
  41.6 264.5 %copy-start.29 = (f32[512,384]{1,0:T(8,128)}, f32[512,384]{1,0:T(8,128)S(1)}, u32[]{:S(2)}) copy-start(f32[512,384]{1,0:T(8,128)S(1)} %fusion.2.refs_13_) | copy-start | bytes 2359300
  41.6 16.2 %slice-start.1 = ((s8[8388608]{0:T(1024)(128)(4,1)}), s8[4194304]{0:T(1024)(128)(4,1)S(1)}, s32[]{:S(2)}) async-start(s8[8388608]{0:T(1024)(128)(4,1)} %bitcast.48), calls=%async_computation.1 | async-start | bytes 8388608
  57.9 47.7 %copy-start.27 = (f32[512,640]{1,0:T(8,128)}, f32[512,640]{1,0:T(8,128)S(1)}, u32[]{:S(2)}) copy-start(f32[512,640]{1,0:T(8,128)S(1)} %fusion.refs_14_) | copy-start | bytes 3932164
  79.8 255.8 %copy-start.4 = (f32[512,2048]{1,0:T(8,128)}, f32[512,2048]{1,0:T(8,128)S(1)}, u32[]{:S(2)}) copy-start(f32[512,2048]{1,0:T(8,128)S(1)} %fusion.4.refs_0_.refs_7_) | copy-start | bytes 12582916
  79.8 27.5 %copy-start.26 = (f32[512,256]{1,0:T(8,128)S(1)}, f32[512,256]{1,0:T(8,128)}, u32[]{:S(2)}) copy-start(f32[512,256]{1,0:T(8,128)} %head_product.11.refs_12_) | copy-start | bytes 1572868
  79.8 269.3 %collective-permute-start.8 = (f32[512,2048]{1,0:T(8,128)S(1)}, f32[512,2048]{1,0:T(8,128)}, u32[]{:S(2)}, u32[]{:S(2)}) collective-permute-start(f32[512,2048]{1,0:T(8,128)S(1)} %fusion.4.refs_0_.refs_7_), channel_id=1, source_target_pairs={{0,4},{4,0},{1,5},{5,1},{2,6},{6,2},{3,7},{7,3}} | collective-permute-start | bytes 12582920 | tf_op jit(solution)/shard_map/ppermute | solution.py:377
  105.2 230.5 %copy-start.3 = (f32[2048,512]{1,0:T(8,128)}, f32[2048,512]{1,0:T(8,128)S(1)}, u32[]{:S(2)}) copy-start(f32[2048,512]{1,0:T(8,128)S(1)} %fusion.5.refs_1_.refs_7_) | copy-start | bytes 12582916
  105.2 13.7 %copy-start.37 = (f32[3]{0:T(128)S(1)}, f32[3]{0:T(128)}, u32[]{:S(2)}) copy-start(f32[3]{0:T(128)} %param.39) | copy-start | bytes 40
  105.2 13.7 %copy-start.5 = (f32[512,512]{1,0:T(8,128)S(1)}, f32[512,512]{1,0:T(8,128)}, u32[]{:S(2)}) copy-start(f32[512,512]{1,0:T(8,128)} %weight.1) | copy-start | bytes 3145732
  105.2 201.3 %copy-start.20 = (f32[512,2048]{1,0:T(8,128)S(1)}, f32[512,2048]{1,0:T(8,128)}, u32[]{:S(2)}) copy-start(f32[512,2048]{1,0:T(8,128)} %param.28) | copy-start | bytes 12582916
  105.2 257.5 %collective-permute-start.9 = (f32[2048,512]{1,0:T(8,128)S(1)}, f32[2048,512]{1,0:T(8,128)}, u32[]{:S(2)}, u32[]{:S(2)}) collective-permute-start(f32[2048,512]{1,0:T(8,128)S(1)} %fusion.5.refs_1_.refs_7_), channel_id=1, source_target_pairs={{0,4},{4,0},{1,5},{5,1},{2,6},{6,2},{3,7},{7,3}} | collective-permute-start | bytes 12582920 | tf_op jit(solution)/shard_map/ppermute | solution.py:377
  105.6 13.2 %copy-start.35 = (f32[256,256]{1,0:T(8,128)}, f32[256,256]{1,0:T(8,128)S(1)}, u32[]{:S(2)}) copy-start(f32[256,256]{1,0:T(8,128)S(1)} %collective-permute-done.3.refs_18_) | copy-start | bytes 786436
  105.6 230.0 %collective-permute-start.7 = (f32[512,640]{1,0:T(8,128)S(1)}, f32[512,640]{1,0:T(8,128)S(1)}, u32[]{:S(2)}, u32[]{:S(2)}) collective-permute-start(f32[512,640]{1,0:T(8,128)S(1)} %fusion.refs_14_), channel_id=1, source_target_pairs={{0,4},{4,0},{1,5},{5,1},{2,6},{6,2},{3,7},{7,3}} | collective-permute-start | bytes 3932168 | tf_op jit(solution)/shard_map/ppermute | solution.py:377
  107.3 11.6 %copy-start.34 = (f32[256,256]{1,0:T(8,128)}, f32[256,256]{1,0:T(8,128)S(1)}, u32[]{:S(2)}) copy-start(f32[256,256]{1,0:T(8,128)S(1)} %collective-permute-done.2.refs_17_) | copy-start | bytes 786436
  107.3 200.9 %collective-permute-start.5 = (f32[512,256]{1,0:T(8,128)S(1)}, f32[512,256]{1,0:T(8,128)S(1)}, u32[]{:S(2)}, u32[]{:S(2)}) collective-permute-start(f32[512,256]{1,0:T(8,128)S(1)} %copy-done.26), channel_id=1, source_target_pairs={{0,4},{4,0},{1,5},{5,1},{2,6},{6,2},{3,7},{7,3}} | collective-permute-start | bytes 1572872 | tf_op jit(solution)/shard_map/ppermute | solution.py:377
  107.7 198.5 %collective-permute-start = (f32[256,256]{1,0:T(8,128)S(1)}, f32[256,256]{1,0:T(8,128)S(1)}, u32[]{:S(2)}, u32[]{:S(2)}) collective-permute-start(f32[256,256]{1,0:T(8,128)S(1)} %get-tuple-element.66.refs_7_), channel_id=1, source_target_pairs={{0,4},{4,0},{1,5},{5,1},{2,6},{6,2},{3,7},{7,3}} | collective-permute-start | bytes 786440 | tf_op jit(solution)/shard_map/ppermute | solution.py:377
  118.9 189.3 %copy-start.25 = (f32[512,256]{1,0:T(8,128)S(1)}, f32[512,256]{1,0:T(8,128)}, u32[]{:S(2)}) copy-start(f32[512,256]{1,0:T(8,128)} %head_product.10.refs_11_) | copy-start | bytes 1572868
  118.9 191.0 %copy-start.21 = (f32[512,2048]{1,0:T(8,128)S(1)}, f32[512,2048]{1,0:T(8,128)}, u32[]{:S(2)}) copy-start(f32[512,2048]{1,0:T(8,128)} %param.29) | copy-start | bytes 12582916
  119.8 191.8 %copy-start.23 = (f32[2048,512]{1,0:T(8,128)S(1)}, f32[2048,512]{1,0:T(8,128)}, u32[]{:S(2)}) copy-start(f32[2048,512]{1,0:T(8,128)} %param.30) | copy-start | bytes 12582916
  306.2 29.4 %collective-permute-start.6 = (f32[512,384]{1,0:T(8,128)S(1)}, f32[512,384]{1,0:T(8,128)S(1)}, u32[]{:S(2)}, u32[]{:S(2)}) collective-permute-start(f32[512,384]{1,0:T(8,128)S(1)} %fusion.2.refs_13_), channel_id=1, source_target_pairs={{0,4},{4,0},{1,5},{5,1},{2,6},{6,2},{3,7},{7,3}} | collective-permute-start | bytes 2359304 | tf_op jit(solution)/shard_map/ppermute | solution.py:377
  308.1 28.7 %copy-start.6 = (f32[2048]{0:T(1024)S(1)}, f32[2048]{0:T(1024)}, u32[]{:S(2)}) copy-start(f32[2048]{0:T(1024)} %param.34) | copy-start | bytes 24580
  308.1 28.7 %copy-start.12 = (f32[512]{0:T(512)S(1)}, f32[512]{0:T(512)}, u32[]{:S(2)}) copy-start(f32[512]{0:T(512)} %param.33) | copy-start | bytes 6148
  308.2 26.9 %collective-permute-start.4 = (f32[512,256]{1,0:T(8,128)S(1)}, f32[512,256]{1,0:T(8,128)S(1)}, u32[]{:S(2)}, u32[]{:S(2)}) collective-permute-start(f32[512,256]{1,0:T(8,128)S(1)} %copy-done.25), channel_id=1, source_target_pairs={{0,4},{4,0},{1,5},{5,1},{2,6},{6,2},{3,7},{7,3}} | collective-permute-start | bytes 1572872 | tf_op jit(solution)/shard_map/ppermute | solution.py:377
  335.1 43.1 %collective-permute-start.10 = (f32[512,512]{1,0:T(8,128)S(1)}, f32[512,512]{1,0:T(8,128)S(1)}, u32[]{:S(2)}, u32[]{:S(2)}) collective-permute-start(f32[512,512]{1,0:T(8,128)S(1)} %fusion.6.refs_2_.refs_7_), channel_id=1, source_target_pairs={{0,4},{4,0},{1,5},{5,1},{2,6},{6,2},{3,7},{7,3}} | collective-permute-start | bytes 3145736 | tf_op jit(solution)/shard_map/ppermute | solution.py:377
  349.1 12.5 %copy-start = (f32[512,2048]{1,0:T(8,128)}, f32[512,2048]{1,0:T(8,128)S(1)}, u32[]{:S(2)}) copy-start(f32[512,2048]{1,0:T(8,128)S(1)} %multiply_subtract_fusion.2.refs_0_) | copy-start | bytes 12582916
  349.4 12.2 %copy-start.22 = (f32[512,2048]{1,0:T(8,128)S(1)}, f32[512,2048]{1,0:T(8,128)}, u32[]{:S(2)}) copy-start(f32[512,2048]{1,0:T(8,128)} %param.29) | copy-start | bytes 12582916
  362.1 15.0 %copy-start.1 = (f32[512,2048]{1,0:T(8,128)}, f32[512,2048]{1,0:T(8,128)S(1)}, u32[]{:S(2)}) copy-start(f32[512,2048]{1,0:T(8,128)S(1)} %multiply_subtract_fusion.1.refs_0_) | copy-start | bytes 12582916
  364.2 13.5 %copy-start.24 = (f32[2048,512]{1,0:T(8,128)S(1)}, f32[2048,512]{1,0:T(8,128)}, u32[]{:S(2)}) copy-start(f32[2048,512]{1,0:T(8,128)} %param.30) | copy-start | bytes 12582916
  (19 other events, 41.9 us)

commit v11 on v8

--- a/solution.py
+++ b/solution.py
@@ -16,6 +16,7 @@
               (0, 512, 512, 256), (0, 768, 512, 256), (0, 1024, 512, 384), (0, 1408, 512, 640))
 N_HEAD = 6
 N_NEAR = 4
+STEPS = 4
 MIB = 1024 * 1024
 HEAD_LIMIT = 50 * MIB
 
@@ -171,7 +172,7 @@
         source, dy_buf = dy_buf, refs.pop(0)
         loads.append((source, col_start, dy_buf))
     sem = refs.pop(0) if loads else None
-    n_step = 8
+    n_step = STEPS if loads and n_x == 1 else 8
     depth = dy_buf.shape[0] // n_step
     rows = x_bufs[0].shape[1]
 
@@ -194,8 +195,8 @@
                 out[own, :] = term
 
     for k in range(n_step):
-        for copy in copies(k):
-            copy.start()
+        for j, copy in enumerate(copies(k)):
+            copy.start(priority=(k + j) % 2)
     if n_x == 1:
         for k in range(n_step):
             multiply(k, k > 0)

time: 385 us -> 386 us (level)
  no operation moved by 1% of the time
where the time goes in v11:
time: 386 us
  waiting for transfers between devices  208 us (54%)
  matrix products  81.8 us (21%)
  Pallas kernels  72 us (19%)
  starting transfers between devices  12.1 us (3%)
  other arithmetic  7.28 us (2%)
    ppermute x11, waiting for transfers between devices, per_device(): recvs[name].append(lax.ppermute(before, 'dp', SWAP))  208 us
    dot_general x5, matrix products, product(): jnp.einsum('tm,tn->mn', x_block, dy_block, preferred_element_type=jnp.flo...  81.8 us
    pallas_call x4, Pallas kernels, statistics(): pl.pallas_call(functools.partial(stats_kernel, len(tokens), boxes, near,...  42.7 us
    pallas_call x6, Pallas kernels, head_product(): pl.pallas_call(functools.partial(head_kernel, row_start, col_start, n_x),...  26.4 us
    ppermute x11, starting transfers between devices, per_device(): recvs[name].append(lax.ppermute(before, 'dp', SWAP))  12.1 us
  transfers between devices with their start and end apart: 11, of which 2 were waited for; matrix products, arithmetic and copies ran while one was open for 23% of the time, Pallas kernels for 14%

profile of v11, /device:TPU:0, one launch (start us, length us, event | category | flops | bytes accessed | tf_op | source)
XLA Modules:
  0.0 386.1 jit_solution(18242546613337867730)
XLA Ops:
  0.6 5.3 %head_product.6 = (f32[256,256]{1,0:T(8,128)S(1)}, bf16[8192,256]{1,0:T(8,128)(2,1)S(1)}, bf16[8192,256]{1,0:T(8,128)(2,1)S(1)}) custom-call(bf16[8192,512]{1,0:T(8,128)(2,1)} %refs_0_.2, bf16[8192,2048]{1,0:T(8,128)(2,1)} %refs_2_.1), custom_call_target="tpu_custom_call" | custom-call | flops 1073741824 | bytes 8388608 | tf_op jit(solution)/shard_map/head_product/pallas_call | solution.py:228
  5.9 3.9 %head_product.7 = (f32[256,256]{1,0:T(8,128)S(1)}, bf16[8192,256]{1,0:T(8,128)(2,1)S(1)}) custom-call(bf16[8192,512]{1,0:T(8,128)(2,1)} %refs_0_.2, bf16[8192,256]{1,0:T(8,128)(2,1)S(1)} %get-tuple-element.67.refs_1_), custom_call_target="tpu_custom_call" | custom-call | flops 1073741824 | bytes 4194304 | tf_op jit(solution)/shard_map/head_product/pallas_call | solution.py:228
  9.9 3.4 collective-permute-start.1
  13.2 4.0 %head_product.8 = (f32[256,256]{1,0:T(8,128)S(1)}, bf16[8192,256]{1,0:T(8,128)(2,1)S(1)}) custom-call(bf16[8192,256]{1,0:T(8,128)(2,1)S(1)} %get-tuple-element.83.refs_0_, bf16[8192,2048]{1,0:T(8,128)(2,1)} %refs_2_.1), custom_call_target="tpu_custom_call" | custom-call | flops 1073741824 | bytes 4194304 | tf_op jit(solution)/shard_map/head_product/pallas_call | solution.py:228
  17.3 1.3 head_product.9.refs_10_
  18.6 2.0 collective-permute-start.3
  20.6 6.0 %head_product.10.refs_11_ = f32[512,256]{1,0:T(8,128)} custom-call(bf16[8192,256]{1,0:T(8,128)(2,1)S(1)} %get-tuple-element.83.refs_0_, bf16[8192,256]{1,0:T(8,128)(2,1)S(1)} %get-tuple-element.84.refs_0_.refs_1_, bf16[8192,2048]{1,0:T(8,128)(2,1)} %refs_2_.1), custom_call_target="tpu_custom_call" | custom-call | flops 2147483648 | bytes 4194304 | tf_op jit(solution)/shard_map/head_product/pallas_call | solution.py:228
  26.5 6.0 %head_product.11.refs_12_ = f32[512,256]{1,0:T(8,128)} custom-call(bf16[8192,256]{1,0:T(8,128)(2,1)S(1)} %get-tuple-element.83.refs_0_, bf16[8192,256]{1,0:T(8,128)(2,1)S(1)} %get-tuple-element.84.refs_0_.refs_1_, bf16[8192,2048]{1,0:T(8,128)(2,1)} %refs_2_.1), custom_call_target="tpu_custom_call" | custom-call | flops 2147483648 | bytes 4194304 | tf_op jit(solution)/shard_map/head_product/pallas_call | solution.py:228
  32.6 9.0 %fusion.2.refs_13_ = f32[512,384]{1,0:T(8,128)S(1)} fusion(bf16[8192,512]{1,0:T(8,128)(2,1)} %refs_0_.2, bf16[8192,2048]{1,0:T(8,128)(2,1)} %refs_2_.1), kind=kOutput, calls=%fused_computation.2 | convolution fusion | flops 3221225472 | bytes 15466496 | tf_op jit(solution)/shard_map/tm,tn->mn/dot_general | solution.py:336
  41.6 16.2 %fusion.refs_14_ = f32[512,640]{1,0:T(8,128)S(1)} fusion(bf16[8192,512]{1,0:T(8,128)(2,1)} %refs_0_.2, bf16[8192,2048]{1,0:T(8,128)(2,1)} %refs_2_.1), kind=kOutput, calls=%fused_computation | convolution fusion | flops 5368709120 | bytes 20185088 | tf_op jit(solution)/shard_map/tm,tn->mn/dot_general | solution.py:336
  57.8 21.9 %fusion.4.refs_0_.refs_7_ = f32[512,2048]{1,0:T(8,128)S(1)} fusion(bf16[8192,512]{1,0:T(8,128)(2,1)S(1)} %bitcast.49, bf16[8192,2048]{1,0:T(8,128)(2,1)} %param.24), kind=kOutput, calls=%fused_computation.11 | convolution fusion | flops 17179869184 | bytes 46137344 | tf_op jit(solution)/shard_map/tm,tn->mn/dot_general | solution.py:336
  79.8 25.2 %fusion.5.refs_1_.refs_7_ = f32[2048,512]{1,0:T(8,128)S(1)} fusion(bf16[8192,2048]{1,0:T(8,128)(2,1)} %param.25, bf16[8192,512]{1,0:T(8,128)(2,1)} %param.26), kind=kOutput, calls=%fused_computation.12 | convolution fusion | flops 17179869184 | bytes 46137344 | tf_op jit(solution)/shard_map/tm,tn->mn/dot_general | solution.py:336
  105.5 1.6 collective-permute-start.7
  107.6 1.6 collective-permute-start
  109.2 9.5 %fusion.6.refs_2_.refs_7_ = f32[512,512]{1,0:T(8,128)S(1)} fusion(bf16[8192,512]{1,0:T(8,128)(2,1)} %param.20, bf16[8192,512]{1,0:T(8,128)(2,1)} %param.21), kind=kOutput, calls=%fused_computation.13 | convolution fusion | flops 4294967296 | bytes 17825792 | tf_op jit(solution)/shard_map/tm,tn->mn/dot_general | solution.py:336
  118.8 0.8 multiply_reduce_fusion.3
  119.7 186.4 %collective-permute-done.refs_15_ = f32[256,256]{1,0:T(8,128)S(1)} collective-permute-done((f32[256,256]{1,0:T(8,128)S(1)}, f32[256,256]{1,0:T(8,128)S(1)}, u32[]{:S(2)}, u32[]{:S(2)}) %collective-permute-start) | collective-permute-done | bytes 262176 | tf_op jit(solution)/shard_map/ppermute | solution.py:371
  306.4 1.7 multiply_reduce_fusion.2
  308.1 1.7 collective-permute-start.4
  309.8 1.7 multiply_reduce_fusion.1
  311.5 1.7 multiply_reduce_fusion
  313.2 21.8 %collective-permute-done.4.refs_19_ = f32[512,256]{1,0:T(8,128)S(1)} collective-permute-done((f32[512,256]{1,0:T(8,128)S(1)}, f32[512,256]{1,0:T(8,128)S(1)}, u32[]{:S(2)}, u32[]{:S(2)}) %collective-permute-start.4) | collective-permute-done | bytes 524320 | tf_op jit(solution)/shard_map/ppermute | solution.py:371
  336.8 11.1 %shard_map.283 = (f32[512,2048]{1,0:T(8,128)S(1)}, f32[1,512]{1,0:T(1,128)S(1)}, f32[1,512]{1,0:T(1,128)S(1)}, f32[1,2048]{1,0:T(1,128)S(1)}) custom-call(f32[512,2048]{1,0:T(8,128)S(1)} %fusion.4.refs_0_.refs_7_, f32[2048,512]{1,0:T(8,128)S(1)} %fusion.5.refs_1_.refs_7_, f32[512,512]{1,0:T(8,128)S(1)} %fusion.6.refs_2_.refs_7_, f32[1,1]{1,0:T(1,128)} %bitcast.refs_3_, ...), custom_call_target="tpu_custom_call" | custom-call | flops 838860800 | bytes 12582912 | tf_op jit(solution)/shard_map/pallas_call | solution.py:305
  347.9 0.6 emit.3
  349.3 12.2 %shard_map.284 = (f32[512,2048]{1,0:T(8,128)S(1)}, f32[1,512]{1,0:T(1,128)S(1)}, f32[1,512]{1,0:T(1,128)S(1)}, f32[1,2048]{1,0:T(1,128)S(1)}) custom-call(f32[512,2048]{1,0:T(8,128)S(1)} %multiply_subtract_fusion.2.refs_0_, f32[1,512]{1,0:T(1,128)S(1)} %copy-done.18, f32[1,2048]{1,0:T(1,128)S(1)} %copy-done.10, f32[1,1]{1,0:T(1,128)} %bitcast.4.refs_3_, ...), custom_call_target="tpu_custom_call" | custom-call | flops 838860800 | bytes 12582912 | tf_op jit(solution)/shard_map/pallas_call | solution.py:305
  362.0 0.6 emit.4
  362.7 0.7 copy-done.11
  363.4 0.7 copy-done.19
  364.1 12.8 %shard_map.285 = (f32[2048,512]{1,0:T(8,128)S(1)}, f32[1,2048]{1,0:T(1,128)S(1)}, f32[1,2048]{1,0:T(1,128)S(1)}, f32[1,512]{1,0:T(1,128)S(1)}) custom-call(f32[512,2048]{1,0:T(8,128)S(1)} %multiply_subtract_fusion.1.refs_0_, f32[1,512]{1,0:T(1,128)S(1)} %copy-done.19, f32[1,2048]{1,0:T(1,128)S(1)} %copy-done.11, f32[1,1]{1,0:T(1,128)} %bitcast.8.refs_3_, ...), custom_call_target="tpu_custom_call" | custom-call | flops 838860800 | bytes 12582912 | tf_op jit(solution)/shard_map/pallas_call | solution.py:305
  377.0 0.6 emit.5
  378.3 6.5 %shard_map.286 = (f32[512,512]{1,0:T(8,128)S(1)}, f32[1,128]{1,0:T(1,128)S(1)}, f32[1,512]{1,0:T(1,128)S(1)}, f32[1,512]{1,0:T(1,128)S(1)}) custom-call(f32[2048,512]{1,0:T(8,128)S(1)} %multiply_subtract_fusion.refs_0_, f32[1,2048]{1,0:T(1,128)S(1)} %copy-done.7, f32[1,512]{1,0:T(1,128)S(1)} %copy-done.15, f32[1,1]{1,0:T(1,128)} %bitcast.12.refs_3_, ...), custom_call_target="tpu_custom_call" | custom-call | flops 209715200 | bytes 3145728 | tf_op jit(solution)/shard_map/pallas_call | solution.py:305
  384.8 1.1 finish.1
  (99 shorter events, 5.0 us)
Async XLA Ops:
  9.9 97.7 %collective-permute-start.1 = (f32[256,256]{1,0:T(8,128)S(1)}, f32[256,256]{1,0:T(8,128)S(1)}, u32[]{:S(2)}, u32[]{:S(2)}) collective-permute-start(f32[256,256]{1,0:T(8,128)S(1)} %get-tuple-element.71.refs_8_), channel_id=1, source_target_pairs={{0,4},{4,0},{1,5},{5,1},{2,6},{6,2},{3,7},{7,3}} | collective-permute-start | bytes 786440 | tf_op jit(solution)/shard_map/ppermute | solution.py:371
  17.2 90.0 %collective-permute-start.2 = (f32[256,256]{1,0:T(8,128)S(1)}, f32[256,256]{1,0:T(8,128)S(1)}, u32[]{:S(2)}, u32[]{:S(2)}) collective-permute-start(f32[256,256]{1,0:T(8,128)S(1)} %get-tuple-element.76.refs_9_), channel_id=1, source_target_pairs={{0,4},{4,0},{1,5},{5,1},{2,6},{6,2},{3,7},{7,3}} | collective-permute-start | bytes 786440 | tf_op jit(solution)/shard_map/ppermute | solution.py:371
  18.6 87.0 %collective-permute-start.3 = (f32[256,256]{1,0:T(8,128)S(1)}, f32[256,256]{1,0:T(8,128)S(1)}, u32[]{:S(2)}, u32[]{:S(2)}) collective-permute-start(f32[256,256]{1,0:T(8,128)S(1)} %head_product.9.refs_10_), channel_id=1, source_target_pairs={{0,4},{4,0},{1,5},{5,1},{2,6},{6,2},{3,7},{7,3}} | collective-permute-start | bytes 786440 | tf_op jit(solution)/shard_map/ppermute | solution.py:371
  32.5 25.2 %slice-start = ((s8[8388608]{0:T(1024)(128)(4,1)}), s8[4194304]{0:T(1024)(128)(4,1)S(1)}, s32[]{:S(2)}) async-start(s8[8388608]{0:T(1024)(128)(4,1)} %bitcast.48), calls=%async_computation | async-start | bytes 8388608
  41.6 264.5 %copy-start.29 = (f32[512,384]{1,0:T(8,128)}, f32[512,384]{1,0:T(8,128)S(1)}, u32[]{:S(2)}) copy-start(f32[512,384]{1,0:T(8,128)S(1)} %fusion.2.refs_13_) | copy-start | bytes 2359300
  41.6 16.2 %slice-start.1 = ((s8[8388608]{0:T(1024)(128)(4,1)}), s8[4194304]{0:T(1024)(128)(4,1)S(1)}, s32[]{:S(2)}) async-start(s8[8388608]{0:T(1024)(128)(4,1)} %bitcast.48), calls=%async_computation.1 | async-start | bytes 8388608
  57.8 47.7 %copy-start.27 = (f32[512,640]{1,0:T(8,128)}, f32[512,640]{1,0:T(8,128)S(1)}, u32[]{:S(2)}) copy-start(f32[512,640]{1,0:T(8,128)S(1)} %fusion.refs_14_) | copy-start | bytes 3932164
  79.7 255.9 %copy-start.4 = (f32[512,2048]{1,0:T(8,128)}, f32[512,2048]{1,0:T(8,128)S(1)}, u32[]{:S(2)}) copy-start(f32[512,2048]{1,0:T(8,128)S(1)} %fusion.4.refs_0_.refs_7_) | copy-start | bytes 12582916
  79.7 27.4 %copy-start.26 = (f32[512,256]{1,0:T(8,128)S(1)}, f32[512,256]{1,0:T(8,128)}, u32[]{:S(2)}) copy-start(f32[512,256]{1,0:T(8,128)} %head_product.11.refs_12_) | copy-start | bytes 1572868
  79.8 269.3 %collective-permute-start.8 = (f32[512,2048]{1,0:T(8,128)S(1)}, f32[512,2048]{1,0:T(8,128)}, u32[]{:S(2)}, u32[]{:S(2)}) collective-permute-start(f32[512,2048]{1,0:T(8,128)S(1)} %fusion.4.refs_0_.refs_7_), channel_id=1, source_target_pairs={{0,4},{4,0},{1,5},{5,1},{2,6},{6,2},{3,7},{7,3}} | collective-permute-start | bytes 12582920 | tf_op jit(solution)/shard_map/ppermute | solution.py:371
  105.1 230.5 %copy-start.3 = (f32[2048,512]{1,0:T(8,128)}, f32[2048,512]{1,0:T(8,128)S(1)}, u32[]{:S(2)}) copy-start(f32[2048,512]{1,0:T(8,128)S(1)} %fusion.5.refs_1_.refs_7_) | copy-start | bytes 12582916
  105.1 13.7 %copy-start.37 = (f32[3]{0:T(128)S(1)}, f32[3]{0:T(128)}, u32[]{:S(2)}) copy-start(f32[3]{0:T(128)} %param.39) | copy-start | bytes 40
  105.1 13.7 %copy-start.5 = (f32[512,512]{1,0:T(8,128)S(1)}, f32[512,512]{1,0:T(8,128)}, u32[]{:S(2)}) copy-start(f32[512,512]{1,0:T(8,128)} %weight.1) | copy-start | bytes 3145732
  105.1 201.3 %copy-start.20 = (f32[512,2048]{1,0:T(8,128)S(1)}, f32[512,2048]{1,0:T(8,128)}, u32[]{:S(2)}) copy-start(f32[512,2048]{1,0:T(8,128)} %param.28) | copy-start | bytes 12582916
  105.1 257.6 %collective-permute-start.9 = (f32[2048,512]{1,0:T(8,128)S(1)}, f32[2048,512]{1,0:T(8,128)}, u32[]{:S(2)}, u32[]{:S(2)}) collective-permute-start(f32[2048,512]{1,0:T(8,128)S(1)} %fusion.5.refs_1_.refs_7_), channel_id=1, source_target_pairs={{0,4},{4,0},{1,5},{5,1},{2,6},{6,2},{3,7},{7,3}} | collective-permute-start | bytes 12582920 | tf_op jit(solution)/shard_map/ppermute | solution.py:371
  105.5 13.2 %copy-start.35 = (f32[256,256]{1,0:T(8,128)}, f32[256,256]{1,0:T(8,128)S(1)}, u32[]{:S(2)}) copy-start(f32[256,256]{1,0:T(8,128)S(1)} %collective-permute-done.3.refs_18_) | copy-start | bytes 786436
  105.5 230.0 %collective-permute-start.7 = (f32[512,640]{1,0:T(8,128)S(1)}, f32[512,640]{1,0:T(8,128)S(1)}, u32[]{:S(2)}, u32[]{:S(2)}) collective-permute-start(f32[512,640]{1,0:T(8,128)S(1)} %fusion.refs_14_), channel_id=1, source_target_pairs={{0,4},{4,0},{1,5},{5,1},{2,6},{6,2},{3,7},{7,3}} | collective-permute-start | bytes 3932168 | tf_op jit(solution)/shard_map/ppermute | solution.py:371
  107.2 11.6 %copy-start.34 = (f32[256,256]{1,0:T(8,128)}, f32[256,256]{1,0:T(8,128)S(1)}, u32[]{:S(2)}) copy-start(f32[256,256]{1,0:T(8,128)S(1)} %collective-permute-done.2.refs_17_) | copy-start | bytes 786436
  107.2 200.9 %collective-permute-start.5 = (f32[512,256]{1,0:T(8,128)S(1)}, f32[512,256]{1,0:T(8,128)S(1)}, u32[]{:S(2)}, u32[]{:S(2)}) collective-permute-start(f32[512,256]{1,0:T(8,128)S(1)} %copy-done.26), channel_id=1, source_target_pairs={{0,4},{4,0},{1,5},{5,1},{2,6},{6,2},{3,7},{7,3}} | collective-permute-start | bytes 1572872 | tf_op jit(solution)/shard_map/ppermute | solution.py:371
  107.6 198.5 %collective-permute-start = (f32[256,256]{1,0:T(8,128)S(1)}, f32[256,256]{1,0:T(8,128)S(1)}, u32[]{:S(2)}, u32[]{:S(2)}) collective-permute-start(f32[256,256]{1,0:T(8,128)S(1)} %get-tuple-element.66.refs_7_), channel_id=1, source_target_pairs={{0,4},{4,0},{1,5},{5,1},{2,6},{6,2},{3,7},{7,3}} | collective-permute-start | bytes 786440 | tf_op jit(solution)/shard_map/ppermute | solution.py:371
  118.8 189.3 %copy-start.25 = (f32[512,256]{1,0:T(8,128)S(1)}, f32[512,256]{1,0:T(8,128)}, u32[]{:S(2)}) copy-start(f32[512,256]{1,0:T(8,128)} %head_product.10.refs_11_) | copy-start | bytes 1572868
  118.8 191.0 %copy-start.21 = (f32[512,2048]{1,0:T(8,128)S(1)}, f32[512,2048]{1,0:T(8,128)}, u32[]{:S(2)}) copy-start(f32[512,2048]{1,0:T(8,128)} %param.29) | copy-start | bytes 12582916
  119.7 191.9 %copy-start.23 = (f32[2048,512]{1,0:T(8,128)S(1)}, f32[2048,512]{1,0:T(8,128)}, u32[]{:S(2)}) copy-start(f32[2048,512]{1,0:T(8,128)} %param.30) | copy-start | bytes 12582916
  306.1 29.4 %collective-permute-start.6 = (f32[512,384]{1,0:T(8,128)S(1)}, f32[512,384]{1,0:T(8,128)S(1)}, u32[]{:S(2)}, u32[]{:S(2)}) collective-permute-start(f32[512,384]{1,0:T(8,128)S(1)} %fusion.2.refs_13_), channel_id=1, source_target_pairs={{0,4},{4,0},{1,5},{5,1},{2,6},{6,2},{3,7},{7,3}} | collective-permute-start | bytes 2359304 | tf_op jit(solution)/shard_map/ppermute | solution.py:371
  308.1 28.7 %copy-start.6 = (f32[2048]{0:T(1024)S(1)}, f32[2048]{0:T(1024)}, u32[]{:S(2)}) copy-start(f32[2048]{0:T(1024)} %param.34) | copy-start | bytes 24580
  308.1 28.7 %copy-start.12 = (f32[512]{0:T(512)S(1)}, f32[512]{0:T(512)}, u32[]{:S(2)}) copy-start(f32[512]{0:T(512)} %param.33) | copy-start | bytes 6148
  308.1 26.9 %collective-permute-start.4 = (f32[512,256]{1,0:T(8,128)S(1)}, f32[512,256]{1,0:T(8,128)S(1)}, u32[]{:S(2)}, u32[]{:S(2)}) collective-permute-start(f32[512,256]{1,0:T(8,128)S(1)} %copy-done.25), channel_id=1, source_target_pairs={{0,4},{4,0},{1,5},{5,1},{2,6},{6,2},{3,7},{7,3}} | collective-permute-start | bytes 1572872 | tf_op jit(solution)/shard_map/ppermute | solution.py:371
  335.0 43.1 %collective-permute-start.10 = (f32[512,512]{1,0:T(8,128)S(1)}, f32[512,512]{1,0:T(8,128)S(1)}, u32[]{:S(2)}, u32[]{:S(2)}) collective-permute-start(f32[512,512]{1,0:T(8,128)S(1)} %fusion.6.refs_2_.refs_7_), channel_id=1, source_target_pairs={{0,4},{4,0},{1,5},{5,1},{2,6},{6,2},{3,7},{7,3}} | collective-permute-start | bytes 3145736 | tf_op jit(solution)/shard_map/ppermute | solution.py:371
  349.0 12.5 %copy-start = (f32[512,2048]{1,0:T(8,128)}, f32[512,2048]{1,0:T(8,128)S(1)}, u32[]{:S(2)}) copy-start(f32[512,2048]{1,0:T(8,128)S(1)} %multiply_subtract_fusion.2.refs_0_) | copy-start | bytes 12582916
  349.3 12.2 %copy-start.22 = (f32[512,2048]{1,0:T(8,128)S(1)}, f32[512,2048]{1,0:T(8,128)}, u32[]{:S(2)}) copy-start(f32[512,2048]{1,0:T(8,128)} %param.29) | copy-start | bytes 12582916
  362.0 15.0 %copy-start.1 = (f32[512,2048]{1,0:T(8,128)}, f32[512,2048]{1,0:T(8,128)S(1)}, u32[]{:S(2)}) copy-start(f32[512,2048]{1,0:T(8,128)S(1)} %multiply_subtract_fusion.1.refs_0_) | copy-start | bytes 12582916
  364.1 13.5 %copy-start.24 = (f32[2048,512]{1,0:T(8,128)S(1)}, f32[2048,512]{1,0:T(8,128)}, u32[]{:S(2)}) copy-start(f32[2048,512]{1,0:T(8,128)} %param.30) | copy-start | bytes 12582916
  (19 other events, 41.9 us)

commit v12 on v8

--- a/solution.py
+++ b/solution.py
@@ -111,10 +111,21 @@
         row_acc[band, :] = lane_sum
         return carry
 
-    lax.fori_loop(0, rows // step, second, 0)
-    for k in range(rows // LANES):
-        tile = row_acc[k * LANES:(k + 1) * LANES, :].T
-        send_upd[:, k * LANES:(k + 1) * LANES] = jnp.sum(tile, axis=0, keepdims=True)
+    if direct:
+        for k in range(rows // LANES):
+            band = pl.ds(k * LANES, LANES)
+            lane_sum = None
+            for j in range(cols // LANES):
+                lanes = pl.ds(j * LANES, LANES)
+                upd = grad[band, lanes] * col_inv[:, j * LANES:(j + 1) * LANES]
+                grad[band, lanes] = upd
+                lane_sum = upd * upd if j == 0 else lane_sum + upd * upd
+            send_upd[:, k * LANES:(k + 1) * LANES] = jnp.sum(lane_sum.T, axis=0, keepdims=True)
+    else:
+        lax.fori_loop(0, rows // step, second, 0)
+        for k in range(rows // LANES):
+            tile = row_acc[k * LANES:(k + 1) * LANES, :].T
+            send_upd[:, k * LANES:(k + 1) * LANES] = jnp.sum(tile, axis=0, keepdims=True)
     lane = lax.broadcasted_iota(jnp.int32, (1, LANES), 1)
     send_upd[:, rows:] = jnp.where(lane == 0, w_sq[0, 0], 0.0)
     upd_copy = swap(2, send_upd, recv_upd, col_peer)

time: 385 us -> 385 us (level)
  no operation moved by 1% of the time
where the time goes in v12:
time: 385 us
  waiting for transfers between devices  208 us (54%)
  matrix products  81.9 us (21%)
  Pallas kernels  70.4 us (18%)
  starting transfers between devices  12.1 us (3%)
  other arithmetic  7.28 us (2%)
    ppermute x11, waiting for transfers between devices, per_device(): recvs[name].append(lax.ppermute(before, 'dp', SWAP))  208 us
    dot_general x5, matrix products, product(): jnp.einsum('tm,tn->mn', x_block, dy_block, preferred_element_type=jnp.flo...  81.9 us
    pallas_call x4, Pallas kernels, statistics(): pl.pallas_call(functools.partial(stats_kernel, len(tokens), boxes, near,...  42.5 us
    pallas_call x6, Pallas kernels, head_product(): pl.pallas_call(functools.partial(head_kernel, row_start, col_start, n_x),...  25 us
    ppermute x11, starting transfers between devices, per_device(): recvs[name].append(lax.ppermute(before, 'dp', SWAP))  12.1 us
  transfers between devices with their start and end apart: 11, of which 2 were waited for; matrix products, arithmetic and copies ran while one was open for 23% of the time, Pallas kernels for 14%

profile of v12, /device:TPU:0, one launch (start us, length us, event | category | flops | bytes accessed | tf_op | source)
XLA Modules:
  0.0 384.5 jit_solution(8768943451122415103)
XLA Ops:
  0.6 4.2 %head_product.6 = (f32[256,256]{1,0:T(8,128)S(1)}, bf16[8192,256]{1,0:T(8,128)(2,1)S(1)}, bf16[8192,256]{1,0:T(8,128)(2,1)S(1)}) custom-call(bf16[8192,512]{1,0:T(8,128)(2,1)} %refs_0_.2, bf16[8192,2048]{1,0:T(8,128)(2,1)} %refs_2_.1), custom_call_target="tpu_custom_call" | custom-call | flops 1073741824 | bytes 8388608 | tf_op jit(solution)/shard_map/head_product/pallas_call | solution.py:238
  4.8 4.0 %head_product.7 = (f32[256,256]{1,0:T(8,128)S(1)}, bf16[8192,256]{1,0:T(8,128)(2,1)S(1)}) custom-call(bf16[8192,512]{1,0:T(8,128)(2,1)} %refs_0_.2, bf16[8192,256]{1,0:T(8,128)(2,1)S(1)} %get-tuple-element.67.refs_1_), custom_call_target="tpu_custom_call" | custom-call | flops 1073741824 | bytes 4194304 | tf_op jit(solution)/shard_map/head_product/pallas_call | solution.py:238
  8.8 3.4 collective-permute-start.1
  12.2 3.9 %head_product.8 = (f32[256,256]{1,0:T(8,128)S(1)}, bf16[8192,256]{1,0:T(8,128)(2,1)S(1)}) custom-call(bf16[8192,256]{1,0:T(8,128)(2,1)S(1)} %get-tuple-element.83.refs_0_, bf16[8192,2048]{1,0:T(8,128)(2,1)} %refs_2_.1), custom_call_target="tpu_custom_call" | custom-call | flops 1073741824 | bytes 4194304 | tf_op jit(solution)/shard_map/head_product/pallas_call | solution.py:238
  16.2 1.3 head_product.9.refs_10_
  17.4 2.0 collective-permute-start.3
  19.5 5.8 %head_product.10.refs_11_ = f32[512,256]{1,0:T(8,128)} custom-call(bf16[8192,256]{1,0:T(8,128)(2,1)S(1)} %get-tuple-element.83.refs_0_, bf16[8192,256]{1,0:T(8,128)(2,1)S(1)} %get-tuple-element.84.refs_0_.refs_1_, bf16[8192,2048]{1,0:T(8,128)(2,1)} %refs_2_.1), custom_call_target="tpu_custom_call" | custom-call | flops 2147483648 | bytes 4194304 | tf_op jit(solution)/shard_map/head_product/pallas_call | solution.py:238
  25.3 5.8 %head_product.11.refs_12_ = f32[512,256]{1,0:T(8,128)} custom-call(bf16[8192,256]{1,0:T(8,128)(2,1)S(1)} %get-tuple-element.83.refs_0_, bf16[8192,256]{1,0:T(8,128)(2,1)S(1)} %get-tuple-element.84.refs_0_.refs_1_, bf16[8192,2048]{1,0:T(8,128)(2,1)} %refs_2_.1), custom_call_target="tpu_custom_call" | custom-call | flops 2147483648 | bytes 4194304 | tf_op jit(solution)/shard_map/head_product/pallas_call | solution.py:238
  31.1 9.0 %fusion.2.refs_13_ = f32[512,384]{1,0:T(8,128)S(1)} fusion(bf16[8192,512]{1,0:T(8,128)(2,1)} %refs_0_.2, bf16[8192,2048]{1,0:T(8,128)(2,1)} %refs_2_.1), kind=kOutput, calls=%fused_computation.2 | convolution fusion | flops 3221225472 | bytes 15466496 | tf_op jit(solution)/shard_map/tm,tn->mn/dot_general | solution.py:346
  40.1 16.2 %fusion.refs_14_ = f32[512,640]{1,0:T(8,128)S(1)} fusion(bf16[8192,512]{1,0:T(8,128)(2,1)} %refs_0_.2, bf16[8192,2048]{1,0:T(8,128)(2,1)} %refs_2_.1), kind=kOutput, calls=%fused_computation | convolution fusion | flops 5368709120 | bytes 20185088 | tf_op jit(solution)/shard_map/tm,tn->mn/dot_general | solution.py:346
  56.3 21.9 %fusion.4.refs_0_.refs_7_ = f32[512,2048]{1,0:T(8,128)S(1)} fusion(bf16[8192,512]{1,0:T(8,128)(2,1)S(1)} %bitcast.49, bf16[8192,2048]{1,0:T(8,128)(2,1)} %param.24), kind=kOutput, calls=%fused_computation.11 | convolution fusion | flops 17179869184 | bytes 46137344 | tf_op jit(solution)/shard_map/tm,tn->mn/dot_general | solution.py:346
  78.3 25.3 %fusion.5.refs_1_.refs_7_ = f32[2048,512]{1,0:T(8,128)S(1)} fusion(bf16[8192,2048]{1,0:T(8,128)(2,1)} %param.25, bf16[8192,512]{1,0:T(8,128)(2,1)} %param.26), kind=kOutput, calls=%fused_computation.12 | convolution fusion | flops 17179869184 | bytes 46137344 | tf_op jit(solution)/shard_map/tm,tn->mn/dot_general | solution.py:346
  104.1 1.7 collective-permute-start.7
  106.1 1.6 collective-permute-start
  107.8 9.5 %fusion.6.refs_2_.refs_7_ = f32[512,512]{1,0:T(8,128)S(1)} fusion(bf16[8192,512]{1,0:T(8,128)(2,1)} %param.20, bf16[8192,512]{1,0:T(8,128)(2,1)} %param.21), kind=kOutput, calls=%fused_computation.13 | convolution fusion | flops 4294967296 | bytes 17825792 | tf_op jit(solution)/shard_map/tm,tn->mn/dot_general | solution.py:346
  117.4 0.8 multiply_reduce_fusion.3
  118.2 186.4 %collective-permute-done.refs_15_ = f32[256,256]{1,0:T(8,128)S(1)} collective-permute-done((f32[256,256]{1,0:T(8,128)S(1)}, f32[256,256]{1,0:T(8,128)S(1)}, u32[]{:S(2)}, u32[]{:S(2)}) %collective-permute-start) | collective-permute-done | bytes 262176 | tf_op jit(solution)/shard_map/ppermute | solution.py:381
  304.9 1.7 multiply_reduce_fusion.2
  306.6 1.7 collective-permute-start.4
  308.4 1.7 multiply_reduce_fusion.1
  310.0 1.7 multiply_reduce_fusion
  311.7 21.8 %collective-permute-done.4.refs_19_ = f32[512,256]{1,0:T(8,128)S(1)} collective-permute-done((f32[512,256]{1,0:T(8,128)S(1)}, f32[512,256]{1,0:T(8,128)S(1)}, u32[]{:S(2)}, u32[]{:S(2)}) %collective-permute-start.4) | collective-permute-done | bytes 524320 | tf_op jit(solution)/shard_map/ppermute | solution.py:381
  335.4 11.1 %shard_map.283 = (f32[512,2048]{1,0:T(8,128)S(1)}, f32[1,512]{1,0:T(1,128)S(1)}, f32[1,512]{1,0:T(1,128)S(1)}, f32[1,2048]{1,0:T(1,128)S(1)}) custom-call(f32[512,2048]{1,0:T(8,128)S(1)} %fusion.4.refs_0_.refs_7_, f32[2048,512]{1,0:T(8,128)S(1)} %fusion.5.refs_1_.refs_7_, f32[512,512]{1,0:T(8,128)S(1)} %fusion.6.refs_2_.refs_7_, f32[1,1]{1,0:T(1,128)} %bitcast.refs_3_, ...), custom_call_target="tpu_custom_call" | custom-call | flops 838860800 | bytes 12582912 | tf_op jit(solution)/shard_map/pallas_call | solution.py:315
  346.5 0.6 emit.3
  347.8 12.2 %shard_map.284 = (f32[512,2048]{1,0:T(8,128)S(1)}, f32[1,512]{1,0:T(1,128)S(1)}, f32[1,512]{1,0:T(1,128)S(1)}, f32[1,2048]{1,0:T(1,128)S(1)}) custom-call(f32[512,2048]{1,0:T(8,128)S(1)} %multiply_subtract_fusion.2.refs_0_, f32[1,512]{1,0:T(1,128)S(1)} %copy-done.18, f32[1,2048]{1,0:T(1,128)S(1)} %copy-done.10, f32[1,1]{1,0:T(1,128)} %bitcast.4.refs_3_, ...), custom_call_target="tpu_custom_call" | custom-call | flops 838860800 | bytes 12582912 | tf_op jit(solution)/shard_map/pallas_call | solution.py:315
  360.6 0.6 emit.4
  361.2 0.7 copy-done.11
  362.0 0.7 copy-done.19
  362.7 12.8 %shard_map.285 = (f32[2048,512]{1,0:T(8,128)S(1)}, f32[1,2048]{1,0:T(1,128)S(1)}, f32[1,2048]{1,0:T(1,128)S(1)}, f32[1,512]{1,0:T(1,128)S(1)}) custom-call(f32[512,2048]{1,0:T(8,128)S(1)} %multiply_subtract_fusion.1.refs_0_, f32[1,512]{1,0:T(1,128)S(1)} %copy-done.19, f32[1,2048]{1,0:T(1,128)S(1)} %copy-done.11, f32[1,1]{1,0:T(1,128)} %bitcast.8.refs_3_, ...), custom_call_target="tpu_custom_call" | custom-call | flops 838860800 | bytes 12582912 | tf_op jit(solution)/shard_map/pallas_call | solution.py:315
  375.5 0.6 emit.5
  376.9 6.4 %shard_map.286 = (f32[512,512]{1,0:T(8,128)S(1)}, f32[1,128]{1,0:T(1,128)S(1)}, f32[1,512]{1,0:T(1,128)S(1)}, f32[1,512]{1,0:T(1,128)S(1)}) custom-call(f32[2048,512]{1,0:T(8,128)S(1)} %multiply_subtract_fusion.refs_0_, f32[1,2048]{1,0:T(1,128)S(1)} %copy-done.7, f32[1,512]{1,0:T(1,128)S(1)} %copy-done.15, f32[1,1]{1,0:T(1,128)} %bitcast.12.refs_3_, ...), custom_call_target="tpu_custom_call" | custom-call | flops 209715200 | bytes 3145728 | tf_op jit(solution)/shard_map/pallas_call | solution.py:315
  383.3 1.1 finish.1
  (99 shorter events, 5.0 us)
Async XLA Ops:
  8.8 97.3 %collective-permute-start.1 = (f32[256,256]{1,0:T(8,128)S(1)}, f32[256,256]{1,0:T(8,128)S(1)}, u32[]{:S(2)}, u32[]{:S(2)}) collective-permute-start(f32[256,256]{1,0:T(8,128)S(1)} %get-tuple-element.71.refs_8_), channel_id=1, source_target_pairs={{0,4},{4,0},{1,5},{5,1},{2,6},{6,2},{3,7},{7,3}} | collective-permute-start | bytes 786440 | tf_op jit(solution)/shard_map/ppermute | solution.py:381
  16.1 89.6 %collective-permute-start.2 = (f32[256,256]{1,0:T(8,128)S(1)}, f32[256,256]{1,0:T(8,128)S(1)}, u32[]{:S(2)}, u32[]{:S(2)}) collective-permute-start(f32[256,256]{1,0:T(8,128)S(1)} %get-tuple-element.76.refs_9_), channel_id=1, source_target_pairs={{0,4},{4,0},{1,5},{5,1},{2,6},{6,2},{3,7},{7,3}} | collective-permute-start | bytes 786440 | tf_op jit(solution)/shard_map/ppermute | solution.py:381
  17.4 86.6 %collective-permute-start.3 = (f32[256,256]{1,0:T(8,128)S(1)}, f32[256,256]{1,0:T(8,128)S(1)}, u32[]{:S(2)}, u32[]{:S(2)}) collective-permute-start(f32[256,256]{1,0:T(8,128)S(1)} %head_product.9.refs_10_), channel_id=1, source_target_pairs={{0,4},{4,0},{1,5},{5,1},{2,6},{6,2},{3,7},{7,3}} | collective-permute-start | bytes 786440 | tf_op jit(solution)/shard_map/ppermute | solution.py:381
  31.1 25.2 %slice-start = ((s8[8388608]{0:T(1024)(128)(4,1)}), s8[4194304]{0:T(1024)(128)(4,1)S(1)}, s32[]{:S(2)}) async-start(s8[8388608]{0:T(1024)(128)(4,1)} %bitcast.48), calls=%async_computation | async-start | bytes 8388608
  40.1 264.5 %copy-start.29 = (f32[512,384]{1,0:T(8,128)}, f32[512,384]{1,0:T(8,128)S(1)}, u32[]{:S(2)}) copy-start(f32[512,384]{1,0:T(8,128)S(1)} %fusion.2.refs_13_) | copy-start | bytes 2359300
  40.1 16.2 %slice-start.1 = ((s8[8388608]{0:T(1024)(128)(4,1)}), s8[4194304]{0:T(1024)(128)(4,1)S(1)}, s32[]{:S(2)}) async-start(s8[8388608]{0:T(1024)(128)(4,1)} %bitcast.48), calls=%async_computation.1 | async-start | bytes 8388608
  56.3 47.7 %copy-start.27 = (f32[512,640]{1,0:T(8,128)}, f32[512,640]{1,0:T(8,128)S(1)}, u32[]{:S(2)}) copy-start(f32[512,640]{1,0:T(8,128)S(1)} %fusion.refs_14_) | copy-start | bytes 3932164
  78.3 255.8 %copy-start.4 = (f32[512,2048]{1,0:T(8,128)}, f32[512,2048]{1,0:T(8,128)S(1)}, u32[]{:S(2)}) copy-start(f32[512,2048]{1,0:T(8,128)S(1)} %fusion.4.refs_0_.refs_7_) | copy-start | bytes 12582916
  78.3 27.5 %copy-start.26 = (f32[512,256]{1,0:T(8,128)S(1)}, f32[512,256]{1,0:T(8,128)}, u32[]{:S(2)}) copy-start(f32[512,256]{1,0:T(8,128)} %head_product.11.refs_12_) | copy-start | bytes 1572868
  78.3 269.3 %collective-permute-start.8 = (f32[512,2048]{1,0:T(8,128)S(1)}, f32[512,2048]{1,0:T(8,128)}, u32[]{:S(2)}, u32[]{:S(2)}) collective-permute-start(f32[512,2048]{1,0:T(8,128)S(1)} %fusion.4.refs_0_.refs_7_), channel_id=1, source_target_pairs={{0,4},{4,0},{1,5},{5,1},{2,6},{6,2},{3,7},{7,3}} | collective-permute-start | bytes 12582920 | tf_op jit(solution)/shard_map/ppermute | solution.py:381
  103.6 230.5 %copy-start.3 = (f32[2048,512]{1,0:T(8,128)}, f32[2048,512]{1,0:T(8,128)S(1)}, u32[]{:S(2)}) copy-start(f32[2048,512]{1,0:T(8,128)S(1)} %fusion.5.refs_1_.refs_7_) | copy-start | bytes 12582916
  103.6 13.7 %copy-start.37 = (f32[3]{0:T(128)S(1)}, f32[3]{0:T(128)}, u32[]{:S(2)}) copy-start(f32[3]{0:T(128)} %param.39) | copy-start | bytes 40
  103.6 13.7 %copy-start.5 = (f32[512,512]{1,0:T(8,128)S(1)}, f32[512,512]{1,0:T(8,128)}, u32[]{:S(2)}) copy-start(f32[512,512]{1,0:T(8,128)} %weight.1) | copy-start | bytes 3145732
  103.7 201.3 %copy-start.20 = (f32[512,2048]{1,0:T(8,128)S(1)}, f32[512,2048]{1,0:T(8,128)}, u32[]{:S(2)}) copy-start(f32[512,2048]{1,0:T(8,128)} %param.28) | copy-start | bytes 12582916
  103.7 257.6 %collective-permute-start.9 = (f32[2048,512]{1,0:T(8,128)S(1)}, f32[2048,512]{1,0:T(8,128)}, u32[]{:S(2)}, u32[]{:S(2)}) collective-permute-start(f32[2048,512]{1,0:T(8,128)S(1)} %fusion.5.refs_1_.refs_7_), channel_id=1, source_target_pairs={{0,4},{4,0},{1,5},{5,1},{2,6},{6,2},{3,7},{7,3}} | collective-permute-start | bytes 12582920 | tf_op jit(solution)/shard_map/ppermute | solution.py:381
  104.1 13.2 %copy-start.35 = (f32[256,256]{1,0:T(8,128)}, f32[256,256]{1,0:T(8,128)S(1)}, u32[]{:S(2)}) copy-start(f32[256,256]{1,0:T(8,128)S(1)} %collective-permute-done.3.refs_18_) | copy-start | bytes 786436
  104.1 230.0 %collective-permute-start.7 = (f32[512,640]{1,0:T(8,128)S(1)}, f32[512,640]{1,0:T(8,128)S(1)}, u32[]{:S(2)}, u32[]{:S(2)}) collective-permute-start(f32[512,640]{1,0:T(8,128)S(1)} %fusion.refs_14_), channel_id=1, source_target_pairs={{0,4},{4,0},{1,5},{5,1},{2,6},{6,2},{3,7},{7,3}} | collective-permute-start | bytes 3932168 | tf_op jit(solution)/shard_map/ppermute | solution.py:381
  105.7 11.6 %copy-start.34 = (f32[256,256]{1,0:T(8,128)}, f32[256,256]{1,0:T(8,128)S(1)}, u32[]{:S(2)}) copy-start(f32[256,256]{1,0:T(8,128)S(1)} %collective-permute-done.2.refs_17_) | copy-start | bytes 786436
  105.7 200.9 %collective-permute-start.5 = (f32[512,256]{1,0:T(8,128)S(1)}, f32[512,256]{1,0:T(8,128)S(1)}, u32[]{:S(2)}, u32[]{:S(2)}) collective-permute-start(f32[512,256]{1,0:T(8,128)S(1)} %copy-done.26), channel_id=1, source_target_pairs={{0,4},{4,0},{1,5},{5,1},{2,6},{6,2},{3,7},{7,3}} | collective-permute-start | bytes 1572872 | tf_op jit(solution)/shard_map/ppermute | solution.py:381
  106.1 198.5 %collective-permute-start = (f32[256,256]{1,0:T(8,128)S(1)}, f32[256,256]{1,0:T(8,128)S(1)}, u32[]{:S(2)}, u32[]{:S(2)}) collective-permute-start(f32[256,256]{1,0:T(8,128)S(1)} %get-tuple-element.66.refs_7_), channel_id=1, source_target_pairs={{0,4},{4,0},{1,5},{5,1},{2,6},{6,2},{3,7},{7,3}} | collective-permute-start | bytes 786440 | tf_op jit(solution)/shard_map/ppermute | solution.py:381
  117.3 189.3 %copy-start.25 = (f32[512,256]{1,0:T(8,128)S(1)}, f32[512,256]{1,0:T(8,128)}, u32[]{:S(2)}) copy-start(f32[512,256]{1,0:T(8,128)} %head_product.10.refs_11_) | copy-start | bytes 1572868
  117.4 191.0 %copy-start.21 = (f32[512,2048]{1,0:T(8,128)S(1)}, f32[512,2048]{1,0:T(8,128)}, u32[]{:S(2)}) copy-start(f32[512,2048]{1,0:T(8,128)} %param.29) | copy-start | bytes 12582916
  118.2 191.8 %copy-start.23 = (f32[2048,512]{1,0:T(8,128)S(1)}, f32[2048,512]{1,0:T(8,128)}, u32[]{:S(2)}) copy-start(f32[2048,512]{1,0:T(8,128)} %param.30) | copy-start | bytes 12582916
  304.6 29.4 %collective-permute-start.6 = (f32[512,384]{1,0:T(8,128)S(1)}, f32[512,384]{1,0:T(8,128)S(1)}, u32[]{:S(2)}, u32[]{:S(2)}) collective-permute-start(f32[512,384]{1,0:T(8,128)S(1)} %fusion.2.refs_13_), channel_id=1, source_target_pairs={{0,4},{4,0},{1,5},{5,1},{2,6},{6,2},{3,7},{7,3}} | collective-permute-start | bytes 2359304 | tf_op jit(solution)/shard_map/ppermute | solution.py:381
  306.6 28.8 %copy-start.6 = (f32[2048]{0:T(1024)S(1)}, f32[2048]{0:T(1024)}, u32[]{:S(2)}) copy-start(f32[2048]{0:T(1024)} %param.34) | copy-start | bytes 24580
  306.6 28.8 %copy-start.12 = (f32[512]{0:T(512)S(1)}, f32[512]{0:T(512)}, u32[]{:S(2)}) copy-start(f32[512]{0:T(512)} %param.33) | copy-start | bytes 6148
  306.6 26.9 %collective-permute-start.4 = (f32[512,256]{1,0:T(8,128)S(1)}, f32[512,256]{1,0:T(8,128)S(1)}, u32[]{:S(2)}, u32[]{:S(2)}) collective-permute-start(f32[512,256]{1,0:T(8,128)S(1)} %copy-done.25), channel_id=1, source_target_pairs={{0,4},{4,0},{1,5},{5,1},{2,6},{6,2},{3,7},{7,3}} | collective-permute-start | bytes 1572872 | tf_op jit(solution)/shard_map/ppermute | solution.py:381
  333.5 43.1 %collective-permute-start.10 = (f32[512,512]{1,0:T(8,128)S(1)}, f32[512,512]{1,0:T(8,128)S(1)}, u32[]{:S(2)}, u32[]{:S(2)}) collective-permute-start(f32[512,512]{1,0:T(8,128)S(1)} %fusion.6.refs_2_.refs_7_), channel_id=1, source_target_pairs={{0,4},{4,0},{1,5},{5,1},{2,6},{6,2},{3,7},{7,3}} | collective-permute-start | bytes 3145736 | tf_op jit(solution)/shard_map/ppermute | solution.py:381
  347.6 12.5 %copy-start = (f32[512,2048]{1,0:T(8,128)}, f32[512,2048]{1,0:T(8,128)S(1)}, u32[]{:S(2)}) copy-start(f32[512,2048]{1,0:T(8,128)S(1)} %multiply_subtract_fusion.2.refs_0_) | copy-start | bytes 12582916
  347.8 12.3 %copy-start.22 = (f32[512,2048]{1,0:T(8,128)S(1)}, f32[512,2048]{1,0:T(8,128)}, u32[]{:S(2)}) copy-start(f32[512,2048]{1,0:T(8,128)} %param.29) | copy-start | bytes 12582916
  360.6 15.0 %copy-start.1 = (f32[512,2048]{1,0:T(8,128)}, f32[512,2048]{1,0:T(8,128)S(1)}, u32[]{:S(2)}) copy-start(f32[512,2048]{1,0:T(8,128)S(1)} %multiply_subtract_fusion.1.refs_0_) | copy-start | bytes 12582916
  362.7 13.5 %copy-start.24 = (f32[2048,512]{1,0:T(8,128)S(1)}, f32[2048,512]{1,0:T(8,128)}, u32[]{:S(2)}) copy-start(f32[2048,512]{1,0:T(8,128)} %param.30) | copy-start | bytes 12582916
  (19 other events, 41.8 us)
